TPU v7x, 32 devices: a whole 2x2x4 slice. The times are simulated.
32 devices in a mesh: dp: 2 (over x), seq: 8 (over z, y), tensor: 2 (over core).
Axes of the slice: x: 2, y: 2, z: 4, core: 2. Of those that a mesh axis runs over, the one named last changes fastest.
Arguments:
- tokens: bfloat16 [2, 8192, 1024], P('dp', 'seq'), may hold values from -6 to 6
- norm1_gain: float32 [1024], replicated, may hold values from 0.1 to 1.9
- in_weight: bfloat16 [3, 1024, 1024], P(None, None, 'tensor'), may hold values from -0.1875 to 0.1875
- conv_weight: float32 [3, 1024], P(None, 'tensor'), may hold values from -3.5 to 3.5
- out_weight: bfloat16 [1024, 1024], P('tensor'), may hold values from -0.1875 to 0.1875
- norm2_gain: float32 [1024], replicated, may hold values from 0.1 to 1.9
- gate_weight: bfloat16 [1024, 4608], P(None, 'tensor'), may hold values from -0.1875 to 0.1875
- up_weight: bfloat16 [1024, 4608], P(None, 'tensor'), may hold values from -0.1875 to 0.1875
- down_weight: bfloat16 [4608, 1024], P('tensor'), may hold values from -0.09375 to 0.09375
- out_cotangent: bfloat16 [2, 8192, 1024], P('dp', 'seq', 'tensor'), may hold values from -6 to 6
Outputs:
- block_out: bfloat16 [2, 8192, 1024], P('dp', 'seq', 'tensor')
- tokens_grad: float32 [2, 8192, 1024], P('dp', 'seq', 'tensor')
- norm1_grad: float32 [1024], P('tensor')
- in_grad: float32 [3, 1024, 1024], P(None, ('dp', 'seq'), 'tensor')
- conv_grad: float32 [3, 1024], P(None, 'tensor')
- out_grad: float32 [1024, 1024], P('tensor', ('dp', 'seq'))
- norm2_grad: float32 [1024], P('tensor')
- gate_grad: float32 [1024, 4608], P(('dp', 'seq'), 'tensor')
- up_grad: float32 [1024, 4608], P(('dp', 'seq'), 'tensor')
- down_grad: float32 [4608, 1024], P('tensor', ('dp', 'seq'))
All inputs are finite; a program needn't handle non-finite values.
Results may differ from a plain program's by a relative error of at most 0.014.
Values may be sent and summed in bfloat16 or wider, within the bound.
A program may use at most 256 MiB of HBM per device.

v0:
```python
import jax
import jax.numpy as jnp
from jax import lax
from jax.sharding import PartitionSpec as P

EPSILON = 1e-05


def shifted(value, axis, steps):
    count = lax.axis_size(axis)
    first, last = (max(0, -steps), min(count, count - steps))
    return lax.ppermute(value, axis, [(source, source + steps) for source in range(first, last)])


def inverse_rms(values):
    return lax.rsqrt(jnp.mean(values * values, axis=-1, keepdims=True) + EPSILON)


def product(left, right):
    return jnp.dot(left, right, preferred_element_type=jnp.float32)


def own_columns(values, start, count):
    return lax.dynamic_slice_in_dim(values, start, count, 1)


def local(
    tokens,
    norm1_gain,
    in_weight,
    conv_weight,
    out_weight,
    norm2_gain,
    gate_weight,
    up_weight,
    down_weight,
    out_cotangent,
):
    seqs, length, width = tokens.shape
    half = in_weight.shape[2]
    total_rows = seqs * length
    start = lax.axis_index("tensor") * half
    token_float = tokens.reshape(total_rows, width).astype(jnp.float32)
    scale_one = inverse_rms(token_float)
    unit_one = token_float * scale_one
    normed = (unit_one * norm1_gain).astype(jnp.bfloat16)
    b_signal = product(normed, in_weight[0])
    c_signal = product(normed, in_weight[1])
    x_signal = product(normed, in_weight[2])
    gated = (b_signal * x_signal).reshape(seqs, length, half)
    prior = shifted(gated[:, length - 2 :], "seq", 1)
    extended = jnp.concatenate([prior, gated], axis=1)
    conv_out = (
        conv_weight[0] * extended[:, 0:length]
        + conv_weight[1] * extended[:, 1 : length + 1]
        + conv_weight[2] * extended[:, 2 : length + 2]
    ).reshape(total_rows, half)
    mixed_in = (c_signal * conv_out).astype(jnp.bfloat16)
    resid = token_float + lax.psum(product(mixed_in, out_weight), "tensor")
    scale_two = inverse_rms(resid)
    unit_two = resid * scale_two
    normed_two = (unit_two * norm2_gain).astype(jnp.bfloat16)
    gate_pre = product(normed_two, gate_weight)
    up_pre = product(normed_two, up_weight)
    sigma = jax.nn.sigmoid(gate_pre)
    active = gate_pre * sigma
    hidden = (active * up_pre).astype(jnp.bfloat16)
    ffn_share = lax.psum_scatter(
        product(hidden, down_weight).astype(jnp.bfloat16), "tensor", scatter_dimension=1, tiled=True
    ).astype(jnp.float32)
    block_out = (
        (own_columns(resid, start, half) + ffn_share)
        .astype(jnp.bfloat16)
        .reshape(seqs, length, half)
    )
    cotangent = lax.all_gather(
        out_cotangent.reshape(total_rows, half), "tensor", axis=1, tiled=True
    )
    down_term = product(hidden.T, cotangent)
    grad_hidden = product(cotangent, down_weight.T)
    grad_gate = (grad_hidden * up_pre * (sigma * (1.0 + gate_pre * (1.0 - sigma)))).astype(
        jnp.bfloat16
    )
    grad_up = (grad_hidden * active).astype(jnp.bfloat16)
    gate_term = product(normed_two.T, grad_gate)
    up_term = product(normed_two.T, grad_up)
    partial_norm = product(grad_gate, gate_weight.T) + product(grad_up, up_weight.T)
    grad_norm_two = lax.psum(partial_norm.astype(jnp.bfloat16), "tensor").astype(jnp.float32)
    gain_two_term = lax.dynamic_slice_in_dim(
        jnp.sum(grad_norm_two * unit_two, axis=0), start, half, 0
    )
    grad_unit = grad_norm_two * norm2_gain
    grad_resid = cotangent.astype(jnp.float32) + scale_two * (
        grad_unit - unit_two * jnp.mean(grad_unit * unit_two, axis=-1, keepdims=True)
    )
    resid_bf = grad_resid.astype(jnp.bfloat16)
    out_term = product(mixed_in.T, resid_bf)
    grad_mixed = product(resid_bf, out_weight.T)
    grad_c = (grad_mixed * conv_out).astype(jnp.bfloat16)
    grad_conv = (grad_mixed * c_signal).reshape(seqs, length, half)
    following = shifted(grad_conv[:, 0:2], "seq", -1)
    grad_ext = jnp.concatenate([grad_conv, following], axis=1)
    grad_gated = (
        conv_weight[0] * grad_ext[:, 2 : length + 2]
        + conv_weight[1] * grad_ext[:, 1 : length + 1]
        + conv_weight[2] * grad_ext[:, 0:length]
    ).reshape(total_rows, half)
    kernel_term = jnp.stack(
        [
            jnp.sum(grad_conv * extended[:, index : index + length], axis=(0, 1))
            for index in range(3)
        ]
    )
    grad_b = (grad_gated * x_signal).astype(jnp.bfloat16)
    grad_x = (grad_gated * b_signal).astype(jnp.bfloat16)
    in_term = jnp.stack(
        [product(normed.T, grad_b), product(normed.T, grad_c), product(normed.T, grad_x)]
    )
    partial_input = (
        product(grad_b, in_weight[0].T)
        + product(grad_c, in_weight[1].T)
        + product(grad_x, in_weight[2].T)
    )
    grad_normed = lax.psum(partial_input.astype(jnp.bfloat16), "tensor").astype(jnp.float32)
    grad_unit_one = grad_normed * norm1_gain
    row_mean = jnp.mean(grad_unit_one * unit_one, axis=-1, keepdims=True)
    tokens_full = grad_resid + scale_one * (grad_unit_one - unit_one * row_mean)
    tokens_grad = own_columns(tokens_full, start, half)
    gain_one_term = lax.dynamic_slice_in_dim(
        jnp.sum(grad_normed * unit_one, axis=0), start, half, 0
    )
    in_grad, out_grad, gate_grad, up_grad, down_grad = (
        lax.psum_scatter(in_term, ("dp", "seq"), scatter_dimension=1, tiled=True),
        lax.psum_scatter(out_term, ("dp", "seq"), scatter_dimension=1, tiled=True),
        lax.psum_scatter(gate_term, ("dp", "seq"), scatter_dimension=0, tiled=True),
        lax.psum_scatter(up_term, ("dp", "seq"), scatter_dimension=0, tiled=True),
        lax.psum_scatter(down_term, ("dp", "seq"), scatter_dimension=1, tiled=True),
    )
    conv_grad, norm1_grad, norm2_grad = lax.psum(
        (kernel_term, gain_one_term, gain_two_term), ("dp", "seq")
    )
    tokens_grad = tokens_grad.reshape(seqs, length, half)
    return (
        block_out,
        tokens_grad,
        norm1_grad,
        in_grad,
        conv_grad,
        out_grad,
        norm2_grad,
        gate_grad,
        up_grad,
        down_grad,
    )


def solution(mesh):
    return jax.shard_map(
        local,
        mesh=mesh,
        in_specs=(
            P("dp", "seq", None),
            P(),
            P(None, None, "tensor"),
            P(None, "tensor"),
            P("tensor", None),
            P(),
            P(None, "tensor"),
            P(None, "tensor"),
            P("tensor", None),
            P("dp", "seq", "tensor"),
        ),
        out_specs=(
            P("dp", "seq", "tensor"),
            P("dp", "seq", "tensor"),
            P("tensor"),
            P(None, ("dp", "seq"), "tensor"),
            P(None, "tensor"),
            P("tensor", ("dp", "seq")),
            P("tensor"),
            P(("dp", "seq"), "tensor"),
            P(("dp", "seq"), "tensor"),
            P("tensor", ("dp", "seq")),
        ),
        check_vma=False,
    )
```

profile of v0, /device:TPU:0, one launch (start us, length us, event | category | flops | bytes accessed | tf_op | source)
XLA Modules:
  0.0 945.4 jit_solution(15730880226286648059)
XLA Ops:
  7.2 2.1 fusion.11
  9.4 3.3 fusion.32
  12.9 2.6 fusion.58
  15.5 4.9 collective-permute-start
  20.5 1.3 collective-permute-done
  21.7 3.3 fusion.28
  25.1 1.0 copy-done.17
  26.1 3.2 fusion.59
  29.4 0.7 all-gather.3.cloned.1.call-update
  30.3 29.3 %all-reduce.5.cloned.1.call-done = f32[1024,1024]{1,0:T(8,128)} async-done(((f32[1024,1024]{1,0:T(8,128)}), f32[1024,1024]{1,0:T(8,128)}) %all-reduce.5.cloned.1.call-update) | async-done | bytes 4194320 | tf_op jit(solution)/shard_map/psum | solution.py:59
  59.6 2.8 multiply_reduce_fusion.1
  62.9 12.2 %fusion.60 = f32[1024,2304]{1,0:T(8,128)} fusion(bf16[1024,1024]{1,0:T(8,128)(2,1)S(1)} %multiply_convert_fusion.4, bf16[1024,2304]{1,0:T(8,128)(2,1)} %param.16), kind=kOutput, calls=%fused_computation.99 | convolution fusion | flops 4831838208 | bytes 16252928 | tf_op jit(solution)/shard_map/dot_general | solution.py:20
  75.1 7.4 fusion.61
  82.5 18.0 %multiply_convert_fusion = (bf16[1024,2304]{1,0:T(8,128)(2,1)}, bf16[1024,2304]{1,0:T(8,128)(2,1)}, bf16[1024,2304]{1,0:T(8,128)(2,1)}) fusion(f32[1024,2304]{1,0:T(8,128)} %fusion.60, f32[1024,2304]{1,0:T(8,128)} %fusion.61, bf16[2304,1024]{1,0:T(8,128)(2,1)} %param.18, bf16[1,1024,1024]{2,1,0:T(8,128)(2,1)} %all-gather.3.cloned.1.call-done), kind=kOutput, calls=%fused_computation | convolution fusion | flops 4867227648 | bytes 39845888 | tf_op jit(solution)/shard_map/dot_general | solution.py:20
  100.5 8.5 fusion.62
  109.0 8.7 add_convert_fusion.1
  117.9 9.3 convolution_convert_fusion
  127.3 13.0 %all-reduce.7.cloned.1.call-done = bf16[1024,1024]{1,0:T(8,128)(2,1)} async-done(((bf16[1024,1024]{1,0:T(8,128)(2,1)}), bf16[1024,1024]{1,0:T(8,128)(2,1)}) %all-reduce.7.cloned.1.call-update) | async-done | bytes 2097168 | tf_op jit(solution)/shard_map/psum | solution.py:88
  140.3 4.3 fusion.9
  145.0 2.8 fusion.8
  147.9 1.7 multiply_reduce_fusion.4
  149.6 0.5 copy-done.4
  150.0 1.5 collective-permute-start.1
  151.6 0.5 fusion.29
  152.2 1.3 fusion.38
  153.5 2.3 collective-permute-done.1
  155.8 1.2 multiply_convert_fusion.5
  157.0 0.4 copy-done.10
  157.4 0.6 multiply_convert_fusion.6
  158.0 1.3 fusion.34
  159.3 2.9 add_convert_fusion
  162.2 5.1 fusion.42
  167.4 0.4 reduce-scatter.9.cloned.1.call-start
  167.9 2.7 convolution_bitcast_fusion.1
  170.6 1.5 convolution_bitcast_fusion.2
  172.1 1.4 convolution_bitcast_fusion
  173.5 3.3 pad_maximum_fusion
  176.9 10.2 %fusion.63 = f32[1024,2304]{1,0:T(8,128)} fusion(bf16[1024,1024]{1,0:T(8,128)(2,1)} %copy-done.12, bf16[1024,2304]{1,0:T(8,128)(2,1)} %get-tuple-element.27), kind=kOutput, calls=%fused_computation.102 | convolution fusion | flops 4831838208 | bytes 16252928 | tf_op jit(solution)/shard_map/dot_general | solution.py:20
  187.2 10.1 %fusion.64 = f32[1024,2304]{1,0:T(8,128)} fusion(bf16[1024,1024]{1,0:T(8,128)(2,1)} %copy-done.12, bf16[1024,2304]{1,0:T(8,128)(2,1)} %get-tuple-element.26), kind=kOutput, calls=%fused_computation.103 | convolution fusion | flops 4831838208 | bytes 16252928 | tf_op jit(solution)/shard_map/dot_general | solution.py:20
  197.6 10.2 %fusion.24 = f32[2304,1024]{0,1:T(8,128)} fusion(bf16[1024,2304]{1,0:T(8,128)(2,1)} %get-tuple-element.28, bf16[1,1024,1024]{2,1,0:T(8,128)(2,1)} %all-gather.3.cloned.1.call-done), kind=kOutput, calls=%fused_computation.50 | convolution fusion | flops 4831838208 | bytes 16252928 | tf_op jit(solution)/shard_map/dot_general | solution.py:20
  207.9 3.2 fusion.30
  211.2 6.3 fusion.10
  217.6 77.6 %all-reduce = (f32[512]{0:T(512)}, f32[3,512]{1,0:T(4,128)}, f32[512]{0:T(512)}) all-reduce(f32[512]{0:T(512)S(1)} %dynamic_slice.14, f32[3,512]{1,0:T(4,128)S(1)} %pad_maximum_fusion.3, f32[512]{0:T(512)S(1)} %dynamic_slice.15), channel_id=1, replica_groups=mesh['dp'=2,'seq'=8,'tensor'=2] {'dp','seq'}, use_global_device_ids=true, to_apply=%region_9.0 | all-reduce | flops 2560 | bytes 20480 | tf_op jit(solution)/shard_map/psum | solution.py:139
  295.2 4.7 fusion.21
  299.8 106.3 %reduce-scatter.9.cloned.1.call-done = f32[3,64,512]{2,1,0:T(8,128)} async-done(((f32[3,1024,512]{2,1,0:T(8,128)}), f32[3,64,512]{2,1,0:T(8,128)}) %reduce-scatter.9.cloned.1.call-update) | async-done | bytes 393232 | tf_op jit(solution)/shard_map/reduce_scatter | solution.py:133
  406.2 178.0 %reduce-scatter.13.cloned.1.call-done = f32[64,2304]{1,0:T(8,128)} async-done(((f32[1024,2304]{1,0:T(8,128)}), f32[64,2304]{1,0:T(8,128)}) %reduce-scatter.13.cloned.1.call-update) | async-done | bytes 589840 | tf_op jit(solution)/shard_map/reduce_scatter | solution.py:135
  584.2 177.1 %reduce-scatter.15.cloned.1.call-done = f32[64,2304]{1,0:T(8,128)} async-done(((f32[1024,2304]{1,0:T(8,128)}), f32[64,2304]{1,0:T(8,128)}) %reduce-scatter.15.cloned.1.call-update) | async-done | bytes 589840 | tf_op jit(solution)/shard_map/reduce_scatter | solution.py:136
  761.3 177.0 %reduce-scatter.17.cloned.1.call-done = f32[2304,64]{0,1:T(8,128)} async-done(((f32[2304,1024]{0,1:T(8,128)}), f32[2304,64]{0,1:T(8,128)}) %reduce-scatter.17.cloned.1.call-update) | async-done | bytes 589840 | tf_op jit(solution)/shard_map/reduce_scatter | solution.py:137
  (85 shorter events, 2.4 us)
Async XLA Ops:
  7.2 18.9 %copy-start = (bf16[512,1024]{1,0:T(8,128)(2,1)S(1)}, bf16[512,1024]{1,0:T(8,128)(2,1)}, u32[]{:S(2)}) copy-start(bf16[512,1024]{1,0:T(8,128)(2,1)} %param.14) | copy-start | bytes 3145732
  7.2 52.4 %all-reduce.5.cloned.1.call-start = ((), (), s32[]{:S(2)}) async-start(), calls=%async_computation.6 | async-start | bytes 8388608 | tf_op jit(solution)/shard_map/psum | solution.py:59
  9.4 3.4 copy-start.5
  9.4 3.5 copy-start.15
  9.4 3.5 copy-start.22
  12.9 2.6 copy-start.9
  12.9 7.5 copy-start.23
  15.5 9.5 %copy-start.6 = (f32[1024,512]{1,0:T(8,128)}, f32[1024,512]{1,0:T(8,128)S(1)}, u32[]{:S(2)}) copy-start(f32[1024,512]{1,0:T(8,128)S(1)} %get-tuple-element.35) | copy-start | bytes 6291460
  15.5 6.2 collective-permute-start
  25.1 1.0 copy-start.17
  29.3 53.2 %all-gather.3.cloned.1.call-start = ((), (), s32[]{:S(2)}) async-start(), calls=%async_computation.15 | async-start | bytes 3145728 | tf_op jit(solution)/shard_map/all_gather | solution.py:76
  30.1 32.3 %copy-start.21 = (f32[1024]{0:T(1024)S(1)}, f32[1024]{0:T(1024)}, u32[]{:S(2)}) copy-start(f32[1024]{0:T(1024)} %param.15) | copy-start | bytes 12292
  30.1 110.2 %all-reduce.7.cloned.1.call-start = ((), (), s32[]{:S(2)}) async-start(), calls=%async_computation.8 | async-start | bytes 4194304 | tf_op jit(solution)/shard_map/psum | solution.py:88
  62.4 12.7 %copy-start.2 = (f32[1024,1024]{1,0:T(8,128)}, f32[1024,1024]{1,0:T(8,128)S(1)}, u32[]{:S(2)}) copy-start(f32[1024,1024]{1,0:T(8,128)S(1)} %get-tuple-element.23) | copy-start | bytes 12582916
  62.4 12.7 %slice-start = ((s8[4718592]{0:T(1024)(128)(4,1)}), s8[4194304]{0:T(1024)(128)(4,1)S(1)}, s32[]{:S(2)}) async-start(s8[4718592]{0:T(1024)(128)(4,1)} %bitcast.132), calls=%async_computation.16 | async-start | bytes 8388608
  62.8 12.2 %copy-start.12 = (bf16[1024,1024]{1,0:T(8,128)(2,1)}, bf16[1024,1024]{1,0:T(8,128)(2,1)S(1)}, u32[]{:S(2)}) copy-start(bf16[1024,1024]{1,0:T(8,128)(2,1)S(1)} %multiply_convert_fusion.4) | copy-start | bytes 6291460
  62.8 12.2 %slice-start.1 = ((s8[4718592]{0:T(1024)(128)(4,1)}), s8[524288]{0:T(1024)(128)(4,1)S(1)}, s32[]{:S(2)}) async-start(s8[4718592]{0:T(1024)(128)(4,1)} %bitcast.132), calls=%async_computation.17 | async-start | bytes 1048576
  100.5 8.5 copy-start.24
  117.7 90.2 %reduce-scatter.7.cloned.1.call-start = ((), (), s32[]{:S(2)}) async-start(), calls=%async_computation.7 | async-start | bytes 3145728 | tf_op jit(solution)/shard_map/reduce_scatter | solution.py:68
  127.3 83.9 %all-reduce.9.cloned.1.call-start = ((), (), s32[]{:S(2)}) async-start(), calls=%async_computation.9 | async-start | bytes 4194304 | tf_op jit(solution)/shard_map/psum | solution.py:124
  140.3 4.3 copy-start.3
  140.3 4.7 copy-start.8
  145.0 2.8 copy-start.7
  145.0 2.9 copy-start.14
  147.8 2.2 copy-start.4
  147.9 3.7 copy-start.13
  150.0 2.1 copy-start.16
  150.0 5.8 collective-permute-start.1
  152.2 1.3 copy-start.18
  152.2 3.6 copy-start.11
  155.8 1.6 copy-start.10
  157.9 1.3 copy-start.19
  162.2 137.6 %reduce-scatter.11.cloned.1.call-start = ((), (), s32[]{:S(2)}) async-start(), calls=%async_computation.11 | async-start | bytes 2228224 | tf_op jit(solution)/shard_map/reduce_scatter | solution.py:134
  167.4 238.7 %reduce-scatter.9.cloned.1.call-start = ((), (), s32[]{:S(2)}) async-start(), calls=%async_computation.10 | async-start | bytes 6684672 | tf_op jit(solution)/shard_map/reduce_scatter | solution.py:133
  167.9 2.7 copy-start.20
  176.9 407.3 %reduce-scatter.13.cloned.1.call-start = ((), (), s32[]{:S(2)}) async-start(), calls=%async_computation.12 | async-start | bytes 10027008 | tf_op jit(solution)/shard_map/reduce_scatter | solution.py:135
  187.2 574.2 %reduce-scatter.15.cloned.1.call-start = ((), (), s32[]{:S(2)}) async-start(), calls=%async_computation.13 | async-start | bytes 10027008 | tf_op jit(solution)/shard_map/reduce_scatter | solution.py:136
  197.3 741.0 %reduce-scatter.17.cloned.1.call-start = ((), (), s32[]{:S(2)}) async-start(), calls=%async_computation.14 | async-start | bytes 10027008 | tf_op jit(solution)/shard_map/reduce_scatter | solution.py:137
  295.2 643.2 %copy-start.1 = (bf16[512,1024]{1,0:T(8,128)(2,1)S(1)}, bf16[512,1024]{1,0:T(8,128)(2,1)}, u32[]{:S(2)}) copy-start(bf16[512,1024]{1,0:T(8,128)(2,1)} %param.14) | copy-start | bytes 3145732
Sparse Core Ops, SparseCore 0:
  29.4 30.0 all-reduce.4
  61.1 11.7 all-gather.2
  117.8 22.4 all-reduce.6
  142.4 10.7 reduce-scatter.6
  162.3 22.4 all-reduce.8
  187.5 82.3 reduce-scatter.10
  272.8 133.3 reduce-scatter.8
  412.4 171.7 reduce-scatter.12
  590.5 170.7 reduce-scatter.14
  767.4 170.8 reduce-scatter.16
where the time goes:
time: 950 us; the launch traced here: 945 us
  waiting for transfers between devices  685 us (72%)
  matrix products  125 us (13%)
  blocking collectives  77.6 us (8%)
  other arithmetic  32.3 us (3%)
  between operations  14.7 us (2%)
    reduce_scatter x1, waiting for transfers between devices, local(): lax.psum_scatter(gate_term, ('dp', 'seq'), scatter_dimension=0, tiled=True)  178 us
    reduce_scatter x1, waiting for transfers between devices, local(): lax.psum_scatter(up_term, ('dp', 'seq'), scatter_dimension=0, tiled=True)  177 us
    reduce_scatter x1, waiting for transfers between devices, local(): lax.psum_scatter(down_term, ('dp', 'seq'), scatter_dimension=1, tiled=True)  177 us
    dot_general x21, matrix products, product(): return jnp.dot(left, right, preferred_element_type=jnp.float32)  125 us
    reduce_scatter x1, waiting for transfers between devices, local(): lax.psum_scatter(in_term, ('dp', 'seq'), scatter_dimension=1, tiled=True)  106 us
    psum x1, blocking collectives, local(): lax.psum((kernel_term, gain_one_term, gain_two_term), ('dp', 'seq'))  77.6 us
    psum x1, waiting for transfers between devices, local(): resid = token_float + lax.psum(product(mixed_in, out_weight), 'tensor')  29.3 us
  transfers between devices with their start and end apart: 12, of which 8 were waited for; matrix products, arithmetic and copies ran while one was open for 11% of the time, Pallas kernels for 0%

commit v1 on v0

v1 whole, which is shorter than its diff:
```python
import functools

import jax
import jax.numpy as jnp
from jax import lax
from jax.experimental import pallas as pl
from jax.experimental.pallas import tpu as pltpu
from jax.sharding import PartitionSpec as P

EPSILON = 1e-05
MESH = pl.DeviceIdType.MESH
UNIT = 256
VMEM_BYTES = 63 * 1024 * 1024
F32 = jnp.float32
BF16 = jnp.bfloat16


def shifted(value, axis, steps):
    count = lax.axis_size(axis)
    first, last = (max(0, -steps), min(count, count - steps))
    return lax.ppermute(value, axis, [(source, source + steps) for source in range(first, last)])


def inverse_rms(values):
    return lax.rsqrt(jnp.mean(values * values, axis=-1, keepdims=True) + EPSILON)


def product(left, right):
    return jnp.dot(left, right, preferred_element_type=F32)


def product_t(left, right):
    return lax.dot_general(left, right, (((1,), (1,)), ((), ())), preferred_element_type=F32)


def own_columns(values, start, count):
    return lax.dynamic_slice_in_dim(values, start, count, 1)


class Halving:
    def __init__(self, seq_size, shards, rows):
        self.seq_size = seq_size
        self.bits = shards.bit_length() - 1
        self.shards = shards
        self.rows = rows

    def stage_rows(self, stage):
        return self.rows << (self.bits - 1 - stage)

    def enter(self):
        self.me = lax.axis_index("dp") * self.seq_size + lax.axis_index("seq")
        self.core = lax.axis_index("tensor")

    def place(self, flat):
        return (flat // self.seq_size, flat % self.seq_size, self.core)

    def flipped(self, weight):
        return self.me + (1 - 2 * ((self.me // weight) % 2)) * weight

    def other_core(self):
        return (self.me // self.seq_size, self.me % self.seq_size, 1 - self.core)

    def greet(self):
        barrier = pltpu.get_barrier_semaphore()
        partners = [self.place(self.flipped(1 << bit)) for bit in range(self.bits)]
        partners.append(self.other_core())
        for partner in partners:
            pl.semaphore_signal(barrier, inc=1, device_id=partner, device_id_type=MESH)
        pl.semaphore_wait(barrier, len(partners))

    def order(self, parity):
        top = self.shards // 2
        high = (self.me // top) % 2
        low = self.me % 2
        first = (top + parity * (1 - top), high + parity * (low - high))
        third = (1 + parity * (top - 1), low + parity * (high - low))
        middle = [(2, (self.me // 2) % 2)]
        rest = [(1 << bit, (self.me // (1 << bit)) % 2) for bit in range(2, self.bits - 1)]
        return [first] + middle + [third] + rest

    def chunks(self, order, keep):
        weight, bit = order[0]
        base = (bit if keep else 1 - bit) * weight
        found = []
        for code in range(self.shards // 2):
            chunk = base
            for place in range(1, self.bits):
                if (code >> (self.bits - 1 - place)) & 1:
                    chunk = chunk + order[place][0]
            found.append(chunk)
        return found

    def offset(self, order, source, stage):
        total = 0
        for place in range(source + 1, min(stage, self.bits - 1) + 1):
            bit = order[place][1]
            if place == stage:
                bit = 1 - bit
            total = total + bit * (1 << (self.bits - 1 - place))
        return total * self.rows

    def scratch(self, units):
        half = self.stage_rows(0)
        return (
            [pltpu.VMEM((units, half, UNIT), BF16), pltpu.VMEM((units, half, UNIT), BF16)]
            + [pltpu.VMEM((units, self.stage_rows(s), UNIT), BF16) for s in range(self.bits)]
            + [
                pltpu.SemaphoreType.DMA((self.bits, units)),
                pltpu.SemaphoreType.DMA((self.bits, units)),
            ]
        )

    def bind(self, refs):
        self.first, self.keep = refs[0], refs[1]
        self.recv = refs[2 : 2 + self.bits]
        self.send_sem, self.recv_sem = refs[2 + self.bits :]

    def copy(self, order, unit, stage):
        weight, bit = order[stage]
        if stage == 0:
            source = self.first.at[unit]
        else:
            start = pl.multiple_of(self.offset(order, 0, stage), self.rows)
            source = self.keep.at[unit, pl.ds(start, self.stage_rows(stage))]
        return pltpu.make_async_remote_copy(
            src_ref=source,
            dst_ref=self.recv[stage].at[unit],
            send_sem=self.send_sem.at[stage, unit],
            recv_sem=self.recv_sem.at[stage, unit],
            device_id=self.place(self.me + (1 - 2 * bit) * weight),
            device_id_type=MESH,
        )

    def gather(self, left, order, keep):
        return jnp.concatenate([left[chunk] for chunk in self.chunks(order, keep)], axis=0)

    def begin(self, unit, parity, left, right):
        order = self.order(parity)
        self.first[unit] = product(self.gather(left, order, False), right[...]).astype(BF16)
        self.copy(order, unit, 0).start()

    def hold(self, unit, parity, left, right):
        order = self.order(parity)
        self.keep[unit] = product(self.gather(left, order, True), right[...]).astype(BF16)

    def collect(self, order, unit, stage, rows):
        start = pl.multiple_of(self.offset(order, 0, stage), self.rows)
        total = self.keep[unit, pl.ds(start, rows)].astype(F32)
        for source in range(min(stage, self.bits)):
            start = pl.multiple_of(self.offset(order, source, stage), self.rows)
            total = total + self.recv[source][unit, pl.ds(start, rows)].astype(F32)
        return total

    def advance(self, unit, parity, stage):
        order = self.order(parity)
        self.copy(order, unit, stage - 1).wait_recv()
        rows = self.stage_rows(stage)
        total = self.collect(order, unit, stage, rows)
        start = pl.multiple_of(self.offset(order, 0, stage), self.rows)
        self.keep[unit, pl.ds(start, rows)] = total.astype(BF16)
        self.copy(order, unit, stage).start()

    def finish(self, unit, parity):
        order = self.order(parity)
        self.copy(order, unit, self.bits - 1).wait_recv()
        total = self.collect(order, unit, self.bits, self.rows)
        for stage in range(self.bits):
            self.copy(order, unit, stage).wait_send()
        return total


def ffn_kernel(
    plan,
    normed_ref,
    cot_ref,
    left_ref,
    gate_hbm,
    up_hbm,
    down_hbm,
    grads_ref,
    pn_ref,
    pn_recv,
    out_ref,
    out_recv,
    gate_buf,
    up_buf,
    down_buf,
    right_ref,
    pn_acc,
    out_acc,
    out_send,
    weight_sem,
    swap_send,
    swap_recv,
    *refs,
):
    total_rows, width = normed_ref.shape
    blocks = gate_hbm.shape[1] // UNIT
    step_rows = min(256, total_rows)
    half = width // 2
    plan.bind(refs)
    plan.enter()

    def weights(index):
        slot = index % 2
        span = pl.ds(pl.multiple_of(index * UNIT, UNIT), UNIT)
        return [
            pltpu.make_async_copy(gate_hbm.at[:, span], gate_buf.at[slot], weight_sem.at[0, slot]),
            pltpu.make_async_copy(up_hbm.at[:, span], up_buf.at[slot], weight_sem.at[1, slot]),
            pltpu.make_async_copy(down_hbm.at[span], down_buf.at[slot], weight_sem.at[2, slot]),
        ]

    for item in weights(0):
        item.start()
    plan.greet()
    pn_acc[...] = jnp.zeros_like(pn_acc)
    out_acc[...] = jnp.zeros_like(out_acc)

    def swaps():
        return [
            pltpu.make_async_remote_copy(
                src_ref=source,
                dst_ref=target,
                send_sem=swap_send.at[index],
                recv_sem=swap_recv.at[index],
                device_id=plan.other_core(),
                device_id_type=MESH,
            )
            for index, (source, target) in enumerate(((pn_ref, pn_recv), (out_send, out_recv)))
        ]

    def step(index, carry):
        @pl.when(index < blocks)
        def _():
            slot = index % 2

            @pl.when(index + 1 < blocks)
            def _():
                for item in weights(index + 1):
                    item.start()

            for item in weights(index):
                item.wait()
            for first in range(0, total_rows, step_rows):
                rows = pl.ds(first, step_rows)
                normed = normed_ref[rows]
                gate_pre = product(normed, gate_buf[slot])
                up_pre = product(normed, up_buf[slot])
                grad_hidden = product_t(cot_ref[rows], down_buf[slot])
                sigma = jax.nn.sigmoid(gate_pre)
                active = gate_pre * sigma
                right_ref[0, rows] = (
                    grad_hidden * up_pre * (sigma * (1.0 + gate_pre * (1.0 - sigma)))
                ).astype(BF16)
                right_ref[1, rows] = (grad_hidden * active).astype(BF16)
                right_ref[2, rows] = (active * up_pre).astype(BF16)
            for place in range(3):
                unit = index * 3 + place
                plan.begin(unit, unit % 2, left_ref.at[place // 2], right_ref.at[place])
            for first in range(0, total_rows, step_rows):
                rows = pl.ds(first, step_rows)
                pn_acc[rows] += product_t(right_ref[0, rows], gate_buf[slot]) + product_t(
                    right_ref[1, rows], up_buf[slot]
                )
                out_acc[rows] += product(right_ref[2, rows], down_buf[slot])
            for place in range(3):
                unit = index * 3 + place
                plan.hold(unit, unit % 2, left_ref.at[place // 2], right_ref.at[place])

        @pl.when(index == blocks)
        def _():
            own = pl.ds(pl.multiple_of(plan.core * half, half), half)
            other = pl.ds(pl.multiple_of((1 - plan.core) * half, half), half)
            pn_ref[...] = pn_acc[...].astype(BF16)
            out_send[...] = out_acc[:, other].astype(BF16)
            for item in swaps():
                item.start()
            out_ref[...] = out_acc[:, own]

        for stage in range(plan.bits, 0, -1):
            block = index - stage

            @pl.when((block >= 0) & (block < blocks))
            def _(stage=stage, block=block):
                for place in range(3):
                    unit = block * 3 + place
                    if stage < plan.bits:
                        plan.advance(unit, unit % 2, stage)
                    else:
                        span = pl.ds(pl.multiple_of(block * UNIT, UNIT), UNIT)
                        grads_ref[place, :, span] = plan.finish(unit, unit % 2)

        return carry

    lax.fori_loop(0, blocks + plan.bits, step, 0)
    for item in swaps():
        item.wait()


def whole():
    return pl.BlockSpec(memory_space=pltpu.VMEM)


def anywhere():
    return pl.BlockSpec(memory_space=pl.ANY)


def ffn(plan, normed, cotangent, left, gate_weight, up_weight, down_weight):
    total_rows, width = normed.shape
    hidden = gate_weight.shape[1]
    blocks = hidden // UNIT
    half = width // 2
    shape = jax.ShapeDtypeStruct
    return pl.pallas_call(
        functools.partial(ffn_kernel, plan),
        name="ffn",
        out_shape=(
            shape((3, plan.rows, hidden), F32),
            shape((total_rows, width), BF16),
            shape((total_rows, width), BF16),
            shape((total_rows, half), F32),
            shape((total_rows, half), BF16),
        ),
        in_specs=[whole()] * 3 + [anywhere()] * 3,
        out_specs=[whole()] * 5,
        scratch_shapes=[
            pltpu.VMEM((2, width, UNIT), BF16),
            pltpu.VMEM((2, width, UNIT), BF16),
            pltpu.VMEM((2, UNIT, width), BF16),
            pltpu.VMEM((3, total_rows, UNIT), BF16),
            pltpu.VMEM((total_rows, width), F32),
            pltpu.VMEM((total_rows, width), F32),
            pltpu.VMEM((total_rows, half), BF16),
            pltpu.SemaphoreType.DMA((3, 2)),
            pltpu.SemaphoreType.DMA((2,)),
            pltpu.SemaphoreType.DMA((2,)),
        ]
        + plan.scratch(3 * blocks),
        compiler_params=pltpu.CompilerParams(
            collective_id=0, has_side_effects=True, vmem_limit_bytes=VMEM_BYTES
        ),
    )(normed, cotangent, left, gate_weight, up_weight, down_weight)


def mix_kernel(
    plan,
    left_ref,
    mixed_ref,
    b_ref,
    c_ref,
    x_ref,
    weight_ref,
    grads_ref,
    part_ref,
    part_recv,
    swap_send,
    swap_recv,
    *refs,
):
    total_rows, width = part_ref.shape
    step_rows = min(256, total_rows)
    plan.bind(refs)
    plan.enter()
    plan.greet()
    rights = [mixed_ref, b_ref, c_ref, x_ref]
    pieces = mixed_ref.shape[1] // UNIT
    units = [(place, piece) for place in range(4) for piece in range(pieces)]
    for unit, (place, piece) in enumerate(units):
        right = rights[place].at[:, pl.ds(piece * UNIT, UNIT)]
        plan.begin(unit, unit % 2, left_ref.at[0 if place else 1], right)
    swaps = []
    for index, first in enumerate(range(0, total_rows, step_rows)):
        rows = pl.ds(first, step_rows)
        total = product_t(b_ref[rows], weight_ref[0])
        total = total + product_t(c_ref[rows], weight_ref[1])
        total = total + product_t(x_ref[rows], weight_ref[2])
        part_ref[rows] = total.astype(BF16)
        swaps.append(
            pltpu.make_async_remote_copy(
                src_ref=part_ref.at[rows],
                dst_ref=part_recv.at[rows],
                send_sem=swap_send.at[index],
                recv_sem=swap_recv.at[index],
                device_id=plan.other_core(),
                device_id_type=MESH,
            )
        )
        swaps[-1].start()
    for unit, (place, piece) in enumerate(units):
        right = rights[place].at[:, pl.ds(piece * UNIT, UNIT)]
        plan.hold(unit, unit % 2, left_ref.at[0 if place else 1], right)
    for stage in range(1, plan.bits):
        for unit in range(len(units)):
            plan.advance(unit, unit % 2, stage)
    for unit, (place, piece) in enumerate(units):
        grads_ref[place, :, piece * UNIT : (piece + 1) * UNIT] = plan.finish(unit, unit % 2)
    for item in swaps:
        item.wait()


def mix(plan, left, mixed_in, grad_b, grad_c, grad_x, in_weight):
    total_rows, half = mixed_in.shape
    width = in_weight.shape[1]
    swaps = total_rows // min(256, total_rows)
    shape = jax.ShapeDtypeStruct
    return pl.pallas_call(
        functools.partial(mix_kernel, plan),
        name="mix",
        out_shape=(
            shape((4, plan.rows, half), F32),
            shape((total_rows, width), BF16),
            shape((total_rows, width), BF16),
        ),
        in_specs=[whole()] * 6,
        out_specs=[whole()] * 3,
        scratch_shapes=[pltpu.SemaphoreType.DMA((swaps,)), pltpu.SemaphoreType.DMA((swaps,))]
        + plan.scratch(4 * half // UNIT),
        compiler_params=pltpu.CompilerParams(
            collective_id=1, has_side_effects=True, vmem_limit_bytes=VMEM_BYTES
        ),
    )(left, mixed_in, grad_b, grad_c, grad_x, in_weight)


def local(
    seq_size,
    shards,
    tokens,
    norm1_gain,
    in_weight,
    conv_weight,
    out_weight,
    norm2_gain,
    gate_weight,
    up_weight,
    down_weight,
    out_cotangent,
):
    seqs, length, width = tokens.shape
    half = in_weight.shape[2]
    total_rows = seqs * length
    chunk_rows = width // shards
    plan = Halving(seq_size, shards, chunk_rows)
    start = lax.axis_index("tensor") * half
    token_float = tokens.reshape(total_rows, width).astype(F32)
    scale_one = inverse_rms(token_float)
    unit_one = token_float * scale_one
    normed = (unit_one * norm1_gain).astype(BF16)
    b_signal = product(normed, in_weight[0])
    c_signal = product(normed, in_weight[1])
    x_signal = product(normed, in_weight[2])
    gated = (b_signal * x_signal).reshape(seqs, length, half)
    prior = shifted(gated[:, length - 2 :], "seq", 1)
    extended = jnp.concatenate([prior, gated], axis=1)
    conv_out = (
        conv_weight[0] * extended[:, 0:length]
        + conv_weight[1] * extended[:, 1 : length + 1]
        + conv_weight[2] * extended[:, 2 : length + 2]
    ).reshape(total_rows, half)
    mixed_in = (c_signal * conv_out).astype(BF16)
    resid = token_float + lax.psum(product(mixed_in, out_weight), "tensor")
    scale_two = inverse_rms(resid)
    unit_two = resid * scale_two
    normed_two = (unit_two * norm2_gain).astype(BF16)
    cotangent = lax.all_gather(
        out_cotangent.reshape(total_rows, half), "tensor", axis=1, tiled=True
    )
    left = jnp.stack([normed_two.T, cotangent.T]).reshape(2, shards, chunk_rows, total_rows)
    ffn_grads, pn_own, pn_other, out_own, out_other = ffn(
        plan, normed_two, cotangent, left, gate_weight, up_weight, down_weight
    )
    gate_grad, up_grad, down_grad = ffn_grads[0], ffn_grads[1], ffn_grads[2].T
    block_out = (
        (own_columns(resid, start, half) + out_own + out_other.astype(F32))
        .astype(BF16)
        .reshape(seqs, length, half)
    )
    grad_norm_two = pn_own.astype(F32) + pn_other.astype(F32)
    gain_two_term = lax.dynamic_slice_in_dim(
        jnp.sum(grad_norm_two * unit_two, axis=0), start, half, 0
    )
    grad_unit = grad_norm_two * norm2_gain
    grad_resid = cotangent.astype(F32) + scale_two * (
        grad_unit - unit_two * jnp.mean(grad_unit * unit_two, axis=-1, keepdims=True)
    )
    resid_bf = grad_resid.astype(BF16)
    grad_mixed = product(resid_bf, out_weight.T)
    grad_c = (grad_mixed * conv_out).astype(BF16)
    grad_conv = (grad_mixed * c_signal).reshape(seqs, length, half)
    following = shifted(grad_conv[:, 0:2], "seq", -1)
    grad_ext = jnp.concatenate([grad_conv, following], axis=1)
    grad_gated = (
        conv_weight[0] * grad_ext[:, 2 : length + 2]
        + conv_weight[1] * grad_ext[:, 1 : length + 1]
        + conv_weight[2] * grad_ext[:, 0:length]
    ).reshape(total_rows, half)
    kernel_term = jnp.stack(
        [
            jnp.sum(grad_conv * extended[:, index : index + length], axis=(0, 1))
            for index in range(3)
        ]
    )
    grad_b = (grad_gated * x_signal).astype(BF16)
    grad_x = (grad_gated * b_signal).astype(BF16)
    left = jnp.stack([normed.T, resid_bf.T]).reshape(2, shards, chunk_rows, total_rows)
    mix_grads, part_own, part_other = mix(
        plan, left, mixed_in, grad_b, grad_c, grad_x, in_weight
    )
    out_grad, in_grad = mix_grads[0].T, mix_grads[1:]
    grad_normed = part_own.astype(F32) + part_other.astype(F32)
    grad_unit_one = grad_normed * norm1_gain
    row_mean = jnp.mean(grad_unit_one * unit_one, axis=-1, keepdims=True)
    tokens_full = grad_resid + scale_one * (grad_unit_one - unit_one * row_mean)
    tokens_grad = own_columns(tokens_full, start, half)
    gain_one_term = lax.dynamic_slice_in_dim(
        jnp.sum(grad_normed * unit_one, axis=0), start, half, 0
    )
    conv_grad, norm1_grad, norm2_grad = lax.psum(
        (kernel_term, gain_one_term, gain_two_term), ("dp", "seq")
    )
    tokens_grad = tokens_grad.reshape(seqs, length, half)
    return (
        block_out,
        tokens_grad,
        norm1_grad,
        in_grad,
        conv_grad,
        out_grad,
        norm2_grad,
        gate_grad,
        up_grad,
        down_grad,
    )


def solution(mesh):
    seq_size = mesh.shape["seq"]
    shards = mesh.shape["dp"] * seq_size
    return jax.shard_map(
        functools.partial(local, seq_size, shards),
        mesh=mesh,
        in_specs=(
            P("dp", "seq", None),
            P(),
            P(None, None, "tensor"),
            P(None, "tensor"),
            P("tensor", None),
            P(),
            P(None, "tensor"),
            P(None, "tensor"),
            P("tensor", None),
            P("dp", "seq", "tensor"),
        ),
        out_specs=(
            P("dp", "seq", "tensor"),
            P("dp", "seq", "tensor"),
            P("tensor"),
            P(None, ("dp", "seq"), "tensor"),
            P(None, "tensor"),
            P("tensor", ("dp", "seq")),
            P("tensor"),
            P(("dp", "seq"), "tensor"),
            P(("dp", "seq"), "tensor"),
            P("tensor", ("dp", "seq")),
        ),
        check_vma=False,
    )
```

time: 950 us -> 395 us (0.42)
  waiting for transfers between devices: 685 us -> 28.2 us
  Pallas kernels: 0 us -> 189 us
  matrix products: 125 us -> 16.5 us
  local copies, waits for them, and re-layouts: 2.74 us -> 23.2 us
  other arithmetic: 32.3 us -> 44.9 us
    reduce_scatter x6 -> x0, waiting for transfers between devices: 639 us -> none  [the longest x1 178 us: local(): lax.psum_scatter(gate_term, ('dp', 'seq'), scatter_dimension=0, tiled=True)]
    pallas_call x0 -> x2, Pallas kernels: none -> 189 us  [the longest x1 129 us: ffn(): pl.pallas_call(functools.partial(ffn_kernel, plan), name='ffn', out_shape...]
    dot_general x21 -> x5, matrix products: 125 us -> 16.5 us  [product(): return jnp.dot(left, right, preferred_element_type=F32)]
    transpose x0 -> x6, local copies, waits for them, and re-layouts: none -> 17.6 us  [the longest x2 8.08 us: local(): left = jnp.stack([normed_two.T, cotangent.T]).reshape(2, shards, chunk_ro...]
    psum x2 -> x0, waiting for transfers between devices: 13 us -> none  [the longest x1 13 us: local(): lax.psum(partial_norm.astype(jnp.bfloat16), 'tensor').astype(jnp.float32)]
  transfers between devices with their start and end apart: 12 -> 4, of which waited for: 8 -> 2; matrix products, arithmetic and copies ran while one was open for 11% -> 5% of each run, Pallas kernels for 0% -> 0%
where the time goes in v1:
time: 395 us
  Pallas kernels  189 us (48%)
  blocking collectives  71.8 us (18%)
  other arithmetic  44.9 us (11%)
  waiting for transfers between devices  28.2 us (7%)
  local copies, waits for them, and re-layouts  23.2 us (6%)
  matrix products  16.5 us (4%)
  between operations  14.3 us (4%)
  starting transfers between devices  6.48 us (2%)
    pallas_call x1, Pallas kernels, ffn(): pl.pallas_call(functools.partial(ffn_kernel, plan), name='ffn', out_shape...  129 us
    psum x1, blocking collectives, local(): lax.psum((kernel_term, gain_one_term, gain_two_term), ('dp', 'seq'))  71.8 us
    pallas_call x1, Pallas kernels, mix(): pl.pallas_call(functools.partial(mix_kernel, plan), name='mix', out_shape...  59.9 us
    psum x1, waiting for transfers between devices, local(): resid = token_float + lax.psum(product(mixed_in, out_weight), 'tensor')  26.2 us
    dot_general x5, matrix products, product(): return jnp.dot(left, right, preferred_element_type=F32)  16.5 us
    transpose x2, local copies, waits for them, and re-layouts, local(): left = jnp.stack([normed_two.T, cotangent.T]).reshape(2, shards, chunk_ro...  8.08 us
  transfers between devices with their start and end apart: 4, of which 2 were waited for; matrix products, arithmetic and copies ran while one was open for 5% of the time, Pallas kernels for 0%

profile of v1, /device:TPU:0, one launch (start us, length us, event | category | flops | bytes accessed | tf_op | source)
XLA Modules:
  0.0 394.7 jit_solution(16451563507701004347)
XLA Ops:
  7.2 0.0 copy-start.2
  7.2 0.0 all-gather.3.cloned.1.call-start
  7.2 0.7 all-gather.3.cloned.1.call-update
  7.9 0.0 all-reduce.3.cloned.1.call-start
  8.0 2.1 fusion.3
  10.1 0.0 copy-start.13
  10.1 2.7 fusion.22
  12.8 0.0 copy-start.22
  12.8 2.6 fusion.40
  15.4 4.9 %collective-permute-start = (f32[1,2,512]{2,1,0:T(2,128)S(1)}, f32[1,2,512]{2,1,0:T(2,128)S(1)}, u32[]{:S(2)}, u32[]{:S(2)}) collective-permute-start(f32[1,2,512]{2,1,0:T(2,128)S(1)} %slice.73), channel_id=1, source_target_pairs={{0,2},{2,4},{4,6},{6,8},{8,10},{10,12},{12,14},{1,3},{3,5},{5,7},{... | collective-permute-start | bytes 12296 | tf_op jit(solution)/shard_map/ppermute | solution.py:21
  20.4 1.3 collective-permute-done
  21.6 3.3 fusion.19
  24.9 1.0 copy-done.18
  25.9 3.2 fusion.41
  29.1 0.0 all-reduce.3.cloned.1.call-update
  29.1 0.0 all-gather.3.cloned.1.call-done
  29.2 4.0 %copy.25 = bf16[1024,1024]{1,0:T(8,128)(2,1)} copy(bf16[1024,1024]{0,1:T(8,128)(2,1)} %bitcast.106) | data formatting | bytes 4194304 | tf_op jit(solution)/shard_map/transpose | solution.py:467
  33.2 26.2 %all-reduce.3.cloned.1.call-done = f32[1024,1024]{1,0:T(8,128)} async-done(((f32[1024,1024]{1,0:T(8,128)}), f32[1024,1024]{1,0:T(8,128)}) %all-reduce.3.cloned.1.call-update) | async-done | bytes 4194320 | tf_op jit(solution)/shard_map/psum | solution.py:460
  59.4 6.1 %fusion = (f32[1024,1024]{1,0:T(8,128)}, bf16[1024,1024]{0,1:T(8,128)(2,1)}, f32[1024]{0:T(1024)S(1)}, f32[1024,1024]{1,0:T(8,128)S(1)}) fusion(bf16[1,1024,1024]{2,1,0:T(8,128)(2,1)S(1)} %copy-done.2, f32[1024]{0:T(1024)S(1)} %add_rsqrt_fusion.1, f32[1024]{0:T(1024)S(1)} %copy-done.21, f32[1024,1024]{1,0:T(8,128)} %all-reduce.3.cloned.1.call-done), kind=kLoop, calls=%fused_computation.2 | loop fusion | flops 7339008 | bytes 16789504 | tf_op jit(solution)/shard_map/mul | solution.py:446
  65.5 2.1 fusion.45
  67.6 0.5 copy-done
  68.1 1.7 multiply_convert_fusion.1.normed_ref
  69.8 4.1 %copy.24 = bf16[1024,1024]{1,0:T(8,128)(2,1)} copy(bf16[1024,1024]{0,1:T(8,128)(2,1)} %fusion.45) | data formatting | bytes 4194304 | tf_op jit(solution)/shard_map/transpose | solution.py:467
  73.9 2.6 copy.26
  76.5 4.6 %pad_maximum_fusion.left_ref = bf16[2,16,64,1024]{3,2,1,0:T(8,128)(2,1)} fusion(bf16[1,16,64,1024]{3,2,1,0:T(8,128)(2,1)} %bitcast.110, bf16[1,16,64,1024]{3,2,1,0:T(8,128)(2,1)} %bitcast.111), kind=kLoop, calls=%fused_computation.8 | loop fusion | flops 2097152 | bytes 8388608 | tf_op jit(solution)/shard_map/stack | solution.py:467
  81.1 129.4 %ffn.1 = (f32[3,64,2304]{2,1,0:T(8,128)}, bf16[1024,1024]{1,0:T(8,128)(2,1)}, bf16[1024,1024]{1,0:T(8,128)(2,1)}, f32[1024,512]{1,0:T(8,128)}, bf16[1024,512]{1,0:T(8,128)(2,1)}) custom-call(bf16[1024,1024]{1,0:T(8,128)(2,1)} %multiply_convert_fusion.1.normed_ref, bf16[1024,1024]{1,0:T(8,128)(2,1)} %bitcast.107, ...), custom_call_target="tpu_custom_call" | custom-call | tf_op jit(solution)/shard_map/ffn/pallas_call | solution.py:314
  210.5 5.0 %multiply_reduce_fusion = (f32[1024]{0:T(1024)S(1)}, f32[1024]{0:T(1024)S(1)}) fusion(bf16[1024,1024]{1,0:T(8,128)(2,1)} %get-tuple-element.21, bf16[1024,1024]{1,0:T(8,128)(2,1)} %get-tuple-element.20, f32[1024,1024]{1,0:T(8,128)} %copy-done, f32[1024]{0:T(1024)S(1)} %add_rsqrt_fusion, f32[1024]{0:T(1024)S(1)} %copy-done.20), kind=kLoop, calls=%fused_computation.10 | loop fusion | flops 9435136 | bytes 8404992 | tf_op jit(solution)/shard_map/reduce_sum | solution.py:479
  215.5 0.3 copy-done.5
  215.8 0.6 copy-done.7
  216.4 4.3 %convert_bitcast_fusion.1 = (bf16[1024,1024]{0,1:T(8,128)(2,1)S(1)}, f32[1024,1024]{1,0:T(8,128)}) fusion(f32[1024]{0:T(1024)S(1)} %broadcast_multiply_fusion.1, f32[1024,1024]{1,0:T(8,128)S(1)} %copy-done.1, f32[1024]{0:T(1024)S(1)} %copy-done.20, bf16[1024,1024]{1,0:T(8,128)(2,1)} %get-tuple-element.21, bf16[1024,1024]{1,0:T(8,128)(2,1)S(1)} %copy-done.7, ...), kind=kLoop, calls=%fused_computation.62 | loop fusion | flops 11534336 | bytes 16789504 | tf_op jit(solution)/shard_map/transpose | solution.py:504
  220.7 2.5 copy.27
  223.2 2.8 slice_bitcast_fusion
  226.1 4.7 %multiply_reduce_fusion.7 = (f32[512]{0:T(512)S(1)}, f32[512]{0:T(512)S(1)}, f32[1024,512]{1,0:T(8,128)S(1)}, f32[1024,512]{1,0:T(8,128)S(1)}) fusion(f32[1,1024,512]{2,1,0:T(8,128)S(1)} %bitcast.103, f32[1,2,512]{2,1,0:T(2,128)S(1)} %collective-permute-done, f32[1024,512]{1,0:T(8,128)} %get-tuple-element.58, bf16[512,1024]{1,0:T(8,128)(2,1)S(1)} %copy-done.17, ...), kind=kOutput, calls=%fused_computation.49 | convolution fusion | flops 1078459392 | bytes 13639680 | tf_op jit(solution)/shard_map/dot_general | solution.py:29
  230.8 1.5 collective-permute-start.1
  232.3 1.4 fusion.20.c_ref
  233.7 0.6 copy-done.10
  234.3 0.6 copy-done.11
  234.9 2.3 pad_maximum_fusion.1.left_ref
  237.2 0.1 dynamic_slice.15
  237.3 2.1 multiply_convert_fusion.2
  239.4 1.3 multiply_convert_fusion.3.b_ref
  240.7 59.9 %mix.1 = (f32[4,64,512]{2,1,0:T(8,128)}, bf16[1024,1024]{1,0:T(8,128)(2,1)}, bf16[1024,1024]{1,0:T(8,128)(2,1)}) custom-call(bf16[2,16,64,1024]{3,2,1,0:T(8,128)(2,1)} %pad_maximum_fusion.1.left_ref, bf16[1024,512]{1,0:T(8,128)(2,1)} %copy-done.18, bf16[1024,512]{1,0:T(8,128)(2,1)} %multiply_convert_fusion.3.b_ref, bf16[1024,512]{1,0:T(8,128)(2,1)} %fusion.20.c_ref, ...), custom_call_target="tpu_custom_call" | custom-call | tf_op jit(solution)/shard_map/mix/pallas_call | solution.py:406
  300.7 1.6 slice_bitcast_fusion.3
  302.2 1.8 slice.68
  304.0 6.5 %multiply_reduce_fusion.1 = (f32[1024]{0:T(1024)S(1)}, f32[1024]{0:T(1024)S(1)}, f32[1024,1024]{1,0:T(8,128)}) fusion(bf16[1024,1024]{1,0:T(8,128)(2,1)} %get-tuple-element.23, bf16[1024,1024]{1,0:T(8,128)(2,1)} %get-tuple-element.22, bf16[1,1024,1024]{2,1,0:T(8,128)(2,1)} %param.10, f32[1024]{0:T(1024)S(1)} %add_rsqrt_fusion.1, f32[1024]{0:T(1024)S(1)} %copy-done.21), kind=kLoop, calls=%fused_computation.11 | loop fusion | flops 10483712 | bytes 10502144 | tf_op jit(solution)/shard_map/reduce_sum | solution.py:515
  310.5 0.1 dynamic_slice.14
  310.6 71.8 %all-reduce = (f32[512]{0:T(512)}, f32[3,512]{1,0:T(4,128)}, f32[512]{0:T(512)}) all-reduce(f32[512]{0:T(512)S(1)} %dynamic_slice.14, f32[3,512]{1,0:T(4,128)S(1)} %pad_maximum_fusion.4, f32[512]{0:T(512)S(1)} %dynamic_slice.15), channel_id=1, replica_groups=mesh['dp'=2,'seq'=8,'tensor'=2] {'dp','seq'}, use_global_device_ids=true, to_apply=%region_6.0 | all-reduce | flops 2560 | bytes 20480 | tf_op jit(solution)/shard_map/psum | solution.py:517
  382.3 5.5 %fusion.16 = (f32[1,1024,512]{2,1,0:T(8,128)}, bf16[1,1024,512]{2,1,0:T(8,128)(2,1)}) fusion(f32[1024,1024]{1,0:T(8,128)} %get-tuple-element.40, s32[]{:T(128)S(6)} %select_n.2, f32[1024,1024]{1,0:T(8,128)} %get-tuple-element.36, f32[1024,1024]{1,0:T(8,128)} %get-tuple-element.45, f32[1024]{0:T(1024)S(1)} %add_rsqrt_fusion.1, ...), kind=kLoop, calls=%fused_computation.35 | loop fusion | flops 4194304 | bytes 14688260 | tf_op jit(solution)/shard_map/reshape | solution.py:520
  (46 shorter events, 0.1 us)
Async XLA Ops:
  7.2 2.9 copy-start.2
  7.2 2.9 copy-start.21
  7.2 22.0 %all-gather.3.cloned.1.call-start = ((), (), s32[]{:S(2)}) async-start(), calls=%async_computation.1 | async-start | bytes 3145728 | tf_op jit(solution)/shard_map/all_gather | solution.py:464
  7.9 51.5 %all-reduce.3.cloned.1.call-start = ((), (), s32[]{:S(2)}) async-start(), calls=%async_computation | async-start | bytes 8388608 | tf_op jit(solution)/shard_map/psum | solution.py:460
  10.1 2.7 copy-start.13
  12.8 2.6 copy-start.8
  12.8 7.6 %copy-start.22 = (f32[3,512]{1,0:T(4,128)S(1)}, f32[3,512]{1,0:T(4,128)}, u32[]{:S(2)}) copy-start(f32[3,512]{1,0:T(4,128)} %param.13) | copy-start | bytes 18436
  15.4 9.5 %copy-start.3 = (f32[1024,512]{1,0:T(8,128)}, f32[1024,512]{1,0:T(8,128)S(1)}, u32[]{:S(2)}) copy-start(f32[1024,512]{1,0:T(8,128)S(1)} %get-tuple-element.56) | copy-start | bytes 6291460
  15.4 6.2 %collective-permute-start = (f32[1,2,512]{2,1,0:T(2,128)S(1)}, f32[1,2,512]{2,1,0:T(2,128)S(1)}, u32[]{:S(2)}, u32[]{:S(2)}) collective-permute-start(f32[1,2,512]{2,1,0:T(2,128)S(1)} %slice.73), channel_id=1, source_target_pairs={{0,2},{2,4},{4,6},{6,8},{8,10},{10,12},{12,14},{1,3},{3,5},{5,7},{... | collective-permute-start | bytes 12296 | tf_op jit(solution)/shard_map/ppermute | solution.py:21
  21.6 4.3 %copy-start.16 = (bf16[512,1024]{1,0:T(8,128)(2,1)S(1)}, bf16[512,1024]{1,0:T(8,128)(2,1)}, u32[]{:S(2)}) copy-start(bf16[512,1024]{1,0:T(8,128)(2,1)} %param.14) | copy-start | bytes 3145732
  24.9 1.0 copy-start.18
  33.2 32.3 %copy-start.20 = (f32[1024]{0:T(1024)S(1)}, f32[1024]{0:T(1024)}, u32[]{:S(2)}) copy-start(f32[1024]{0:T(1024)} %param.15) | copy-start | bytes 12292
  65.4 2.6 copy-start
  69.8 4.1 %copy-start.6 = (bf16[1024,1024]{0,1:T(8,128)(2,1)S(1)}, bf16[1024,1024]{0,1:T(8,128)(2,1)}, u32[]{:S(2)}) copy-start(bf16[1024,1024]{0,1:T(8,128)(2,1)} %get-tuple-element.46) | copy-start | bytes 6291460
  210.5 5.0 %copy-start.1 = (f32[1024,1024]{1,0:T(8,128)S(1)}, f32[1024,1024]{1,0:T(8,128)}, u32[]{:S(2)}) copy-start(f32[1024,1024]{1,0:T(8,128)} %copy-done) | copy-start | bytes 12582916
  210.5 5.3 %copy-start.5 = (bf16[1,1024,1024]{2,1,0:T(8,128)(2,1)S(1)}, bf16[1,1024,1024]{2,1,0:T(8,128)(2,1)}, u32[]{:S(2)}) copy-start(bf16[1,1024,1024]{2,1,0:T(8,128)(2,1)} %all-gather.3.cloned.1.call-done) | copy-start | bytes 6291460
  210.5 5.9 %copy-start.7 = (bf16[1024,1024]{1,0:T(8,128)(2,1)S(1)}, bf16[1024,1024]{1,0:T(8,128)(2,1)}, u32[]{:S(2)}) copy-start(bf16[1024,1024]{1,0:T(8,128)(2,1)} %get-tuple-element.20) | copy-start | bytes 6291460
  223.2 2.8 copy-start.4
  223.2 2.8 copy-start.17
  226.1 6.3 %copy-start.14 = (f32[1,1024,512]{2,1,0:T(8,128)S(1)}, f32[1,1024,512]{2,1,0:T(8,128)}, u32[]{:S(2)}) copy-start(f32[1,1024,512]{2,1,0:T(8,128)} %get-tuple-element.44) | copy-start | bytes 6291460
  230.8 6.5 %collective-permute-start.1 = (f32[1,2,512]{2,1,0:T(2,128)S(1)}, f32[1,2,512]{2,1,0:T(2,128)S(1)}, u32[]{:S(2)}, u32[]{:S(2)}) collective-permute-start(f32[1,2,512]{2,1,0:T(2,128)S(1)} %slice.76), channel_id=1, source_target_pairs={{2,0},{4,2},{6,4},{8,6},{10,8},{12,10},{14,12},{3,1},{5,3},{7,5},{... | collective-permute-start | bytes 12296 | tf_op jit(solution)/shard_map/ppermute | solution.py:21
  232.3 2.0 copy-start.10
  232.3 2.6 copy-start.11
  234.9 2.4 copy-start.12
  237.3 2.1 copy-start.9
  304.0 78.3 %copy-start.15 = (f32[1024,512]{1,0:T(8,128)S(1)}, f32[1024,512]{1,0:T(8,128)}, u32[]{:S(2)}) copy-start(f32[1024,512]{1,0:T(8,128)} %get-tuple-element.18) | copy-start | bytes 6291460
  304.0 78.3 %copy-start.19 = (bf16[1024,512]{1,0:T(8,128)(2,1)S(1)}, bf16[1024,512]{1,0:T(8,128)(2,1)}, u32[]{:S(2)}) copy-start(bf16[1024,512]{1,0:T(8,128)(2,1)} %get-tuple-element.19) | copy-start | bytes 3145732
Sparse Core Ops, SparseCore 0:
  9.5 13.2 all-gather.2
  29.3 30.0 all-reduce.2

commit v2 on v1

--- a/solution.py
+++ b/solution.py
@@ -60,10 +60,15 @@
     def other_core(self):
         return (self.me // self.seq_size, self.me % self.seq_size, 1 - self.core)
 
-    def greet(self):
+    def along_seq(self, steps):
+        seq = (self.me + steps) % self.seq_size
+        return (self.me // self.seq_size, seq, self.core)
+
+    def greet(self, steps=()):
         barrier = pltpu.get_barrier_semaphore()
         partners = [self.place(self.flipped(1 << bit)) for bit in range(self.bits)]
         partners.append(self.other_core())
+        partners.extend(self.along_seq(count) for count in steps)
         for partner in partners:
             pl.semaphore_signal(barrier, inc=1, device_id=partner, device_id_type=MESH)
         pl.semaphore_wait(barrier, len(partners))
@@ -342,83 +347,301 @@
     )(normed, cotangent, left, gate_weight, up_weight, down_weight)
 
 
-def mix_kernel(
+def back_kernel(
     plan,
+    gain_ref,
+    tap_ref,
+    pn_ref,
+    pn_recv,
+    cot_ref,
+    mixed_ref,
+    prior_ref,
+    out_weight_ref,
+    in_weight_ref,
+    left_hbm,
+    resid_hbm,
+    token_hbm,
+    b_hbm,
+    c_hbm,
+    x_hbm,
+    grads_ref,
+    tokens_ref,
+    small_ref,
     left_ref,
-    mixed_ref,
+    resid_ref,
+    token_ref,
     b_ref,
     c_ref,
     x_ref,
-    weight_ref,
-    grads_ref,
+    full_ref,
+    gated_ref,
+    conv_ref,
+    grad_own,
+    right_ref,
     part_ref,
     part_recv,
+    sums_ref,
+    small_send,
+    small_recv,
+    load_sem,
+    left_sem,
     swap_send,
     swap_recv,
+    halo_send,
+    halo_recv,
+    small_send_sem,
+    small_recv_sem,
     *refs,
 ):
-    total_rows, width = part_ref.shape
-    step_rows = min(256, total_rows)
+    total_rows, width = cot_ref.shape
+    half = width // 2
+    step = min(256, total_rows)
+    steps = total_rows // step
     plan.bind(refs)
     plan.enter()
-    plan.greet()
-    rights = [mixed_ref, b_ref, c_ref, x_ref]
-    pieces = mixed_ref.shape[1] // UNIT
-    units = [(place, piece) for place in range(4) for piece in range(pieces)]
+    seq = lax.axis_index("seq")
+    last = plan.seq_size - 1
+
+    def loads(index):
+        rows = pl.ds(pl.multiple_of(index * step, step), step)
+        pairs = (
+            (resid_hbm, resid_ref),
+            (b_hbm, b_ref),
+            (x_hbm, x_ref),
+            (c_hbm, c_ref),
+            (token_hbm, token_ref),
+        )
+        return [
+            pltpu.make_async_copy(source.at[rows], target.at[rows], load_sem.at[index, place])
+            for place, (source, target) in enumerate(pairs)
+        ]
+
+    left_load = pltpu.make_async_copy(left_hbm, left_ref.at[0], left_sem.at[0])
+    for index in range(steps):
+        for item in loads(index):
+            item.start()
+    left_load.start()
+    plan.greet((-1, 1))
+    own = pl.ds(pl.multiple_of(plan.core * half, half), half)
+    gain_one, gain_two = gain_ref[0:1], gain_ref[1:2]
+    taps = [tap_ref[k : k + 1] for k in range(3)]
+    sums_ref[...] = jnp.zeros_like(sums_ref)
+    gated_ref[0:8] = prior_ref[...]
+
+    def halo():
+        return pltpu.make_async_remote_copy(
+            src_ref=conv_ref.at[pl.ds(0, 8)],
+            dst_ref=conv_ref.at[pl.ds(total_rows, 8)],
+            send_sem=halo_send.at[0],
+            recv_sem=halo_recv.at[0],
+            device_id=plan.along_seq(-1),
+            device_id_type=MESH,
+        )
+
+    def first_pass(index, carry):
+        start = pl.multiple_of(index * step, step)
+        rows = pl.ds(start, step)
+        for item in loads(index):
+            item.wait()
+        resid = resid_ref[rows]
+        scale = inverse_rms(resid)
+        unit = resid * scale
+        grad = pn_ref[rows].astype(F32) + pn_recv[rows].astype(F32)
+        sums_ref[0:1] += jnp.sum(grad * unit, axis=0, keepdims=True)
+        grad = grad * gain_two
+        mean = jnp.mean(grad * unit, axis=-1, keepdims=True)
+        grad = cot_ref[rows].astype(F32) + scale * (grad - unit * mean)
+        full_ref[...] = grad
+        grad_own[rows] = full_ref[:, own]
+        rounded = grad.astype(BF16)
+        left_ref[1, :, :, rows] = rounded.T.reshape(plan.shards, plan.rows, step)
+        grad_mixed = product_t(rounded, out_weight_ref[...])
+        gated_ref[pl.ds(start + 8, step)] = b_ref[rows] * x_ref[rows]
+        window = gated_ref[pl.ds(start, step + 8)]
+        views = [window[6 + k : 6 + k + step] for k in range(3)]
+        conv_out = taps[0] * views[0] + taps[1] * views[1] + taps[2] * views[2]
+        right_ref[1, rows] = (grad_mixed * conv_out).astype(BF16)
+        grad_conv = grad_mixed * c_ref[rows]
+        conv_ref[rows] = grad_conv
+        for k in range(3):
+            sums_ref[1 + k : 2 + k, 0:half] += jnp.sum(grad_conv * views[k], axis=0, keepdims=True)
+
+        @pl.when((index == 0) & (seq > 0))
+        def _():
+            halo().start()
+
+        return carry
+
+    lax.fori_loop(0, steps, first_pass, 0)
+    pieces = half // UNIT
+    places = (3, 1, 0, 2)
+    units = [(place, piece) for place in places for piece in range(pieces)]
+
+    def right_of(place, piece):
+        span = pl.ds(piece * UNIT, UNIT)
+        return mixed_ref.at[:, span] if place == 3 else right_ref.at[place, :, span]
+
+    def left_of(place):
+        return left_ref.at[1 if place == 3 else 0]
+
+    early = 2 * pieces
+    left_load.wait()
+    for unit, (place, piece) in enumerate(units[:early]):
+        plan.begin(unit, unit % 2, left_of(place), right_of(place, piece))
+
+    @pl.when(seq < last)
+    def _():
+        halo().wait_recv()
+
+    @pl.when(seq == last)
+    def _():
+        conv_ref[pl.ds(total_rows, 8)] = jnp.zeros((8, half), F32)
+
+    def second_pass(index, carry):
+        start = pl.multiple_of(index * step, step)
+        rows = pl.ds(start, step)
+        window = conv_ref[pl.ds(start, step + 8)]
+        grad_gated = (
+            taps[0] * window[2 : 2 + step]
+            + taps[1] * window[1 : 1 + step]
+            + taps[2] * window[0:step]
+        )
+        right_ref[0, rows] = (grad_gated * x_ref[rows]).astype(BF16)
+        right_ref[2, rows] = (grad_gated * b_ref[rows]).astype(BF16)
+        return carry
+
+    lax.fori_loop(0, steps, second_pass, 0)
+    for unit, (place, piece) in list(enumerate(units))[early:]:
+        plan.begin(unit, unit % 2, left_of(place), right_of(place, piece))
+
+    def swap(index):
+        rows = pl.ds(pl.multiple_of(index * step, step), step)
+        return pltpu.make_async_remote_copy(
+            src_ref=part_ref.at[rows],
+            dst_ref=part_recv.at[rows],
+            send_sem=swap_send.at[index],
+            recv_sem=swap_recv.at[index],
+            device_id=plan.other_core(),
+            device_id_type=MESH,
+        )
+
+    def third_pass(index, carry):
+        rows = pl.ds(pl.multiple_of(index * step, step), step)
+        total = product_t(right_ref[0, rows], in_weight_ref[0])
+        total = total + product_t(right_ref[1, rows], in_weight_ref[1])
+        total = total + product_t(right_ref[2, rows], in_weight_ref[2])
+        part_ref[rows] = total.astype(BF16)
+        swap(index).start()
+        return carry
+
+    lax.fori_loop(0, steps, third_pass, 0)
     for unit, (place, piece) in enumerate(units):
-        right = rights[place].at[:, pl.ds(piece * UNIT, UNIT)]
-        plan.begin(unit, unit % 2, left_ref.at[0 if place else 1], right)
-    swaps = []
-    for index, first in enumerate(range(0, total_rows, step_rows)):
-        rows = pl.ds(first, step_rows)
-        total = product_t(b_ref[rows], weight_ref[0])
-        total = total + product_t(c_ref[rows], weight_ref[1])
-        total = total + product_t(x_ref[rows], weight_ref[2])
-        part_ref[rows] = total.astype(BF16)
-        swaps.append(
-            pltpu.make_async_remote_copy(
-                src_ref=part_ref.at[rows],
-                dst_ref=part_recv.at[rows],
-                send_sem=swap_send.at[index],
-                recv_sem=swap_recv.at[index],
-                device_id=plan.other_core(),
-                device_id_type=MESH,
-            )
+        plan.hold(unit, unit % 2, left_of(place), right_of(place, piece))
+    for unit in range(len(units)):
+        plan.advance(unit, unit % 2, 1)
+
+    def fourth_pass(index, carry):
+        rows = pl.ds(pl.multiple_of(index * step, step), step)
+        swap(index).wait_recv()
+        value = token_ref[rows].astype(F32)
+        scale = inverse_rms(value)
+        unit = value * scale
+        grad = part_ref[rows].astype(F32) + part_recv[rows].astype(F32)
+        sums_ref[4:5] += jnp.sum(grad * unit, axis=0, keepdims=True)
+        grad = grad * gain_one
+        mean = jnp.mean(grad * unit, axis=-1, keepdims=True)
+        full_ref[...] = scale * (grad - unit * mean)
+        tokens_ref[rows] = grad_own[rows] + full_ref[:, own]
+        return carry
+
+    lax.fori_loop(0, steps, fourth_pass, 0)
+    small_send[0] = jnp.zeros_like(small_ref)
+    small_send[0, 0:3] = sums_ref[1:4, 0:half]
+    small_send[0, 3:4] = sums_ref[4:5, own]
+    small_send[0, 4:5] = sums_ref[0:1, own]
+
+    def small(bit):
+        return pltpu.make_async_remote_copy(
+            src_ref=small_send.at[bit],
+            dst_ref=small_recv.at[bit],
+            send_sem=small_send_sem.at[bit],
+            recv_sem=small_recv_sem.at[bit],
+            device_id=plan.place(plan.flipped(1 << bit)),
+            device_id_type=MESH,
         )
-        swaps[-1].start()
-    for unit, (place, piece) in enumerate(units):
-        right = rights[place].at[:, pl.ds(piece * UNIT, UNIT)]
-        plan.hold(unit, unit % 2, left_ref.at[0 if place else 1], right)
-    for stage in range(1, plan.bits):
-        for unit in range(len(units)):
-            plan.advance(unit, unit % 2, stage)
-    for unit, (place, piece) in enumerate(units):
-        grads_ref[place, :, piece * UNIT : (piece + 1) * UNIT] = plan.finish(unit, unit % 2)
-    for item in swaps:
-        item.wait()
-
-
-def mix(plan, left, mixed_in, grad_b, grad_c, grad_x, in_weight):
-    total_rows, half = mixed_in.shape
-    width = in_weight.shape[1]
-    swaps = total_rows // min(256, total_rows)
+
+    for bit in range(plan.bits):
+        small(bit).start()
+        if bit + 2 < plan.bits + 0:
+            for unit in range(len(units)):
+                plan.advance(unit, unit % 2, bit + 2)
+        elif bit == plan.bits - 1:
+            for unit, (place, piece) in enumerate(units):
+                grads_ref[place, :, piece * UNIT : (piece + 1) * UNIT] = plan.finish(unit, unit % 2)
+        small(bit).wait_recv()
+        total = small_send[bit] + small_recv[bit]
+        if bit + 1 < plan.bits:
+            small_send[bit + 1] = total
+        else:
+            small_ref[...] = total
+    for bit in range(plan.bits):
+        small(bit).wait_send()
+
+    @pl.when(seq > 0)
+    def _():
+        halo().wait_send()
+
+    for index in range(steps):
+        swap(index).wait_send()
+
+
+def back(plan, gains, taps, pn, pn_other, cot, mixed, prior, out_weight, in_weight, left, streams):
+    total_rows, width = cot.shape
+    half = width // 2
+    steps = total_rows // min(256, total_rows)
     shape = jax.ShapeDtypeStruct
+    dma = pltpu.SemaphoreType.DMA
     return pl.pallas_call(
-        functools.partial(mix_kernel, plan),
-        name="mix",
+        functools.partial(back_kernel, plan),
+        name="back",
         out_shape=(
             shape((4, plan.rows, half), F32),
-            shape((total_rows, width), BF16),
-            shape((total_rows, width), BF16),
+            shape((total_rows, half), F32),
+            shape((8, half), F32),
         ),
-        in_specs=[whole()] * 6,
+        in_specs=[whole()] * 9 + [anywhere()] * 6,
         out_specs=[whole()] * 3,
-        scratch_shapes=[pltpu.SemaphoreType.DMA((swaps,)), pltpu.SemaphoreType.DMA((swaps,))]
+        scratch_shapes=[
+            pltpu.VMEM((2, plan.shards, plan.rows, total_rows), BF16),
+            pltpu.VMEM((total_rows, width), F32),
+            pltpu.VMEM((total_rows, width), BF16),
+            pltpu.VMEM((total_rows, half), F32),
+            pltpu.VMEM((total_rows, half), F32),
+            pltpu.VMEM((total_rows, half), F32),
+            pltpu.VMEM((total_rows // steps, width), F32),
+            pltpu.VMEM((total_rows + 8, half), F32),
+            pltpu.VMEM((total_rows + 8, half), F32),
+            pltpu.VMEM((total_rows, half), F32),
+            pltpu.VMEM((3, total_rows, half), BF16),
+            pltpu.VMEM((total_rows, width), BF16),
+            pltpu.VMEM((total_rows, width), BF16),
+            pltpu.VMEM((8, width), F32),
+            pltpu.VMEM((plan.bits, 8, half), F32),
+            pltpu.VMEM((plan.bits, 8, half), F32),
+            dma((steps, 5)),
+            dma((1,)),
+            dma((steps,)),
+            dma((steps,)),
+            dma((1,)),
+            dma((1,)),
+            dma((plan.bits,)),
+            dma((plan.bits,)),
+        ]
         + plan.scratch(4 * half // UNIT),
         compiler_params=pltpu.CompilerParams(
             collective_id=1, has_side_effects=True, vmem_limit_bytes=VMEM_BYTES
         ),
-    )(left, mixed_in, grad_b, grad_c, grad_x, in_weight)
+    )(gains, taps, pn, pn_other, cot, mixed, prior, out_weight, in_weight, left, *streams)
 
 
 def local(
@@ -442,9 +665,7 @@
     plan = Halving(seq_size, shards, chunk_rows)
     start = lax.axis_index("tensor") * half
     token_float = tokens.reshape(total_rows, width).astype(F32)
-    scale_one = inverse_rms(token_float)
-    unit_one = token_float * scale_one
-    normed = (unit_one * norm1_gain).astype(BF16)
+    normed = (token_float * inverse_rms(token_float) * norm1_gain).astype(BF16)
     b_signal = product(normed, in_weight[0])
     c_signal = product(normed, in_weight[1])
     x_signal = product(normed, in_weight[2])
@@ -458,9 +679,7 @@
     ).reshape(total_rows, half)
     mixed_in = (c_signal * conv_out).astype(BF16)
     resid = token_float + lax.psum(product(mixed_in, out_weight), "tensor")
-    scale_two = inverse_rms(resid)
-    unit_two = resid * scale_two
-    normed_two = (unit_two * norm2_gain).astype(BF16)
+    normed_two = (resid * inverse_rms(resid) * norm2_gain).astype(BF16)
     cotangent = lax.all_gather(
         out_cotangent.reshape(total_rows, half), "tensor", axis=1, tiled=True
     )
@@ -474,49 +693,22 @@
         .astype(BF16)
         .reshape(seqs, length, half)
     )
-    grad_norm_two = pn_own.astype(F32) + pn_other.astype(F32)
-    gain_two_term = lax.dynamic_slice_in_dim(
-        jnp.sum(grad_norm_two * unit_two, axis=0), start, half, 0
+    mix_grads, tokens_grad, small = back(
+        plan,
+        jnp.stack([norm1_gain, norm2_gain]),
+        conv_weight,
+        pn_own,
+        pn_other,
+        cotangent,
+        mixed_in,
+        jnp.pad(prior[0], ((6, 0), (0, 0))),
+        out_weight,
+        in_weight,
+        normed.T.reshape(shards, chunk_rows, total_rows),
+        (resid, tokens.reshape(total_rows, width), b_signal, c_signal, x_signal),
     )
-    grad_unit = grad_norm_two * norm2_gain
-    grad_resid = cotangent.astype(F32) + scale_two * (
-        grad_unit - unit_two * jnp.mean(grad_unit * unit_two, axis=-1, keepdims=True)
-    )
-    resid_bf = grad_resid.astype(BF16)
-    grad_mixed = product(resid_bf, out_weight.T)
-    grad_c = (grad_mixed * conv_out).astype(BF16)
-    grad_conv = (grad_mixed * c_signal).reshape(seqs, length, half)
-    following = shifted(grad_conv[:, 0:2], "seq", -1)
-    grad_ext = jnp.concatenate([grad_conv, following], axis=1)
-    grad_gated = (
-        conv_weight[0] * grad_ext[:, 2 : length + 2]
-        + conv_weight[1] * grad_ext[:, 1 : length + 1]
-        + conv_weight[2] * grad_ext[:, 0:length]
-    ).reshape(total_rows, half)
-    kernel_term = jnp.stack(
-        [
-            jnp.sum(grad_conv * extended[:, index : index + length], axis=(0, 1))
-            for index in range(3)
-        ]
-    )
-    grad_b = (grad_gated * x_signal).astype(BF16)
-    grad_x = (grad_gated * b_signal).astype(BF16)
-    left = jnp.stack([normed.T, resid_bf.T]).reshape(2, shards, chunk_rows, total_rows)
-    mix_grads, part_own, part_other = mix(
-        plan, left, mixed_in, grad_b, grad_c, grad_x, in_weight
-    )
-    out_grad, in_grad = mix_grads[0].T, mix_grads[1:]
-    grad_normed = part_own.astype(F32) + part_other.astype(F32)
-    grad_unit_one = grad_normed * norm1_gain
-    row_mean = jnp.mean(grad_unit_one * unit_one, axis=-1, keepdims=True)
-    tokens_full = grad_resid + scale_one * (grad_unit_one - unit_one * row_mean)
-    tokens_grad = own_columns(tokens_full, start, half)
-    gain_one_term = lax.dynamic_slice_in_dim(
-        jnp.sum(grad_normed * unit_one, axis=0), start, half, 0
-    )
-    conv_grad, norm1_grad, norm2_grad = lax.psum(
-        (kernel_term, gain_one_term, gain_two_term), ("dp", "seq")
-    )
+    in_grad, out_grad = mix_grads[0:3], mix_grads[3].T
+    conv_grad, norm1_grad, norm2_grad = small[0:3], small[3], small[4]
     tokens_grad = tokens_grad.reshape(seqs, length, half)
     return (
         block_out,

time: 395 us -> 296 us (0.75)
  blocking collectives: 71.8 us -> 0 us
  other arithmetic: 44.9 us -> 20 us
  Pallas kernels: 189 us -> 197 us
  matrix products: 16.5 us -> 10.2 us
    psum x1 -> x0, blocking collectives: 71.8 us -> none  [local(): lax.psum((kernel_term, gain_one_term, gain_two_term), ('dp', 'seq'))]
    reduce_sum x2 -> x0, other arithmetic: 11.4 us -> none  [the longest x1 6.46 us: local(): jnp.sum(grad_normed * unit_one, axis=0)]
    pallas_call x1, Pallas kernels: 59.9 us -> 67 us  [back(): pl.pallas_call(functools.partial(back_kernel, plan), name='back', out_sha...]
    dot_general x5 -> x4, matrix products: 16.5 us -> 10.2 us  [product(): return jnp.dot(left, right, preferred_element_type=F32)]
    mul x1 -> x0, other arithmetic: 6.06 us -> none  [local(): unit_one = token_float * scale_one]
    convert_element_type x4 -> x1, other arithmetic: 6.55 us -> 1.78 us  [local(): normed_two = (resid * inverse_rms(resid) * norm2_gain).astype(BF16)]
    reduce_sum x1 -> x2, other arithmetic: 2.07 us -> 6.76 us  [inverse_rms(): jnp.mean(values * values, axis=-1, keepdims=True) + EPSILON]
    transpose x1 -> x0, other arithmetic: 4.29 us -> none  [local(): left = jnp.stack([normed.T, resid_bf.T]).reshape(2, shards, chunk_rows, t...]
  transfers between devices with their start and end apart: 4 -> 3, of which waited for: 2 -> 2; matrix products, arithmetic and copies ran while one was open for 5% -> 6% of each run, Pallas kernels for 0% -> 0%
where the time goes in v2:
time: 296 us
  Pallas kernels  197 us (67%)
  waiting for transfers between devices  26.4 us (9%)
  local copies, waits for them, and re-layouts  23.7 us (8%)
  other arithmetic  20 us (7%)
  between operations  14.2 us (5%)
  matrix products  10.2 us (3%)
  starting transfers between devices  4.98 us (2%)
    pallas_call x1, Pallas kernels, ffn(): pl.pallas_call(functools.partial(ffn_kernel, plan), name='ffn', out_shape...  129 us
    pallas_call x1, Pallas kernels, back(): pl.pallas_call(functools.partial(back_kernel, plan), name='back', out_sha...  67 us
    psum x1, waiting for transfers between devices, local(): resid = token_float + lax.psum(product(mixed_in, out_weight), 'tensor')  24.4 us
    dot_general x4, matrix products, product(): return jnp.dot(left, right, preferred_element_type=F32)  10.2 us
    transpose x2, local copies, waits for them, and re-layouts, local(): left = jnp.stack([normed_two.T, cotangent.T]).reshape(2, shards, chunk_ro...  8.04 us
    reduce_sum x2, other arithmetic, inverse_rms(): jnp.mean(values * values, axis=-1, keepdims=True) + EPSILON  6.76 us
  transfers between devices with their start and end apart: 3, of which 2 were waited for; matrix products, arithmetic and copies ran while one was open for 6% of the time, Pallas kernels for 0%

profile of v2, /device:TPU:0, one launch (start us, length us, event | category | flops | bytes accessed | tf_op | source)
XLA Modules:
  0.0 296.0 jit_solution(11275700047866597086)
XLA Ops:
  7.2 0.0 copy-start.2
  7.2 0.0 copy-start.12
  7.2 0.0 all-gather.3.cloned.1.call-start
  7.2 0.7 all-gather.3.cloned.1.call-update
  7.9 0.0 all-reduce.3.cloned.1.call-start
  8.0 2.1 fusion
  10.1 0.0 copy-done.2
  10.1 0.0 copy-done.12
  10.1 0.0 copy-start.6
  10.1 2.7 fusion.14.x_hbm
  12.8 0.0 copy-done.6
  12.8 0.0 copy-start.3
  12.8 1.3 fusion.16.b_hbm
  14.1 0.0 copy-start.11
  14.1 0.5 multiply_bitcast_fusion
  14.6 4.9 %collective-permute-start = (f32[1,2,512]{2,1,0:T(2,128)S(1)}, f32[1,2,512]{2,1,0:T(2,128)S(1)}, u32[]{:S(2)}, u32[]{:S(2)}) collective-permute-start(f32[1,2,512]{2,1,0:T(2,128)S(1)} %slice.68), channel_id=1, source_target_pairs={{0,2},{2,4},{4,6},{6,8},{8,10},{10,12},{12,14},{1,3},{3,5},{5,7},{... | collective-permute-start | bytes 12296 | tf_op jit(solution)/shard_map/ppermute | solution.py:21
  19.5 0.0 copy-done.11
  19.6 1.3 collective-permute-done
  20.8 0.0 copy-done.3
  20.8 0.0 copy-done.4
  20.9 3.0 %fusion.9 = (bf16[1024,512]{1,0:T(8,128)(2,1)S(1)}, f32[1024,512]{1,0:T(8,128)}) fusion(f32[1,2,512]{2,1,0:T(2,128)S(1)} %collective-permute-done, f32[1,1024,512]{2,1,0:T(8,128)S(1)} %multiply_bitcast_fusion, f32[512]{0:T(512)S(1)} %bitcast.83, f32[512]{0:T(512)S(1)} %bitcast.82, f32[512]{0:T(512)S(1)} %bitcast.81, f32[1024,512]{1,0:T(8,128)S(1)} %fusion.16.b_hbm, ...), kind=kOutput, calls=%fused_computation.18 | convolution fusion | flops 1083179008 | bytes 12601344 | tf_op jit(solution)/shard_map/dot_general | solution.py:29
  23.9 1.0 copy-done.9
  24.8 0.0 copy-done.8
  24.8 3.2 %fusion.28 = f32[1024,1024]{1,0:T(8,128)} fusion(bf16[1024,512]{1,0:T(8,128)(2,1)S(1)} %get-tuple-element.37.mixed_ref, bf16[512,1024]{1,0:T(8,128)(2,1)S(1)} %copy-done.8), kind=kOutput, calls=%fused_computation.44 | convolution fusion | flops 1073741824 | bytes 6291456 | tf_op jit(solution)/shard_map/dot_general | solution.py:29
  28.1 0.0 all-reduce.3.cloned.1.call-update
  28.1 0.7 copy-done.10
  28.8 0.6 pad_maximum_fusion.2.gain_ref
  29.4 0.6 pad.4.prior_ref
  30.0 4.0 %copy.24 = bf16[1024,1024]{1,0:T(8,128)(2,1)} copy(bf16[1024,1024]{0,1:T(8,128)(2,1)} %bitcast.69) | data formatting | bytes 4194304 | tf_op jit(solution)/shard_map/transpose | solution.py:686
  33.9 24.4 %all-reduce.3.cloned.1.call-done = f32[1024,1024]{1,0:T(8,128)} async-done(((f32[1024,1024]{1,0:T(8,128)}), f32[1024,1024]{1,0:T(8,128)}) %all-reduce.3.cloned.1.call-update) | async-done | bytes 4194320 | tf_op jit(solution)/shard_map/psum | solution.py:681
  58.3 4.7 %multiply_reduce_fusion = (f32[1024]{0:T(1024)S(1)}, f32[1024,1024]{1,0:T(8,128)S(1)}, bf16[1024,1024]{0,1:T(8,128)(2,1)}) fusion(f32[1024,1024]{1,0:T(8,128)} %all-reduce.3.cloned.1.call-done, bf16[1,1024,1024]{2,1,0:T(8,128)(2,1)S(1)} %copy-done.2, f32[1024]{0:T(1024)S(1)} %copy-done.12, f32[1024]{0:T(1024)S(1)} %add_rsqrt_fusion.1), kind=kLoop, calls=%fused_computation.8 | loop fusion | flops 7339008 | bytes 12595200 | tf_op jit(solution)/shard_map/reduce_sum | solution.py:25
  63.0 2.0 fusion.31
  65.1 0.6 copy-done
  65.7 1.8 multiply_convert_fusion.normed_ref
  67.5 4.1 %copy.23 = bf16[1024,1024]{1,0:T(8,128)(2,1)} copy(bf16[1024,1024]{0,1:T(8,128)(2,1)} %fusion.31) | data formatting | bytes 4194304 | tf_op jit(solution)/shard_map/transpose | solution.py:686
  71.6 0.0 copy-done.5
  71.6 2.6 copy.25
  74.1 4.6 %pad_maximum_fusion.left_ref = bf16[2,16,64,1024]{3,2,1,0:T(8,128)(2,1)} fusion(bf16[1,16,64,1024]{3,2,1,0:T(8,128)(2,1)} %bitcast.73, bf16[1,16,64,1024]{3,2,1,0:T(8,128)(2,1)} %bitcast.74), kind=kLoop, calls=%fused_computation.6 | loop fusion | flops 2097152 | bytes 8388608 | tf_op jit(solution)/shard_map/stack | solution.py:686
  78.7 129.5 %ffn.1 = (f32[3,64,2304]{2,1,0:T(8,128)}, bf16[1024,1024]{1,0:T(8,128)(2,1)}, bf16[1024,1024]{1,0:T(8,128)(2,1)}, f32[1024,512]{1,0:T(8,128)}, bf16[1024,512]{1,0:T(8,128)(2,1)}) custom-call(bf16[1024,1024]{1,0:T(8,128)(2,1)} %multiply_convert_fusion.normed_ref, bf16[1024,1024]{1,0:T(8,128)(2,1)} %bitcast.70, ...), custom_call_target="tpu_custom_call" | custom-call | tf_op jit(solution)/shard_map/ffn/pallas_call | solution.py:319
  208.2 67.0 %back.1 = (f32[4,64,512]{2,1,0:T(8,128)}, f32[1024,512]{1,0:T(8,128)}, f32[8,512]{1,0:T(8,128)}) custom-call(f32[2,1024]{1,0:T(2,128)} %pad_maximum_fusion.2.gain_ref, f32[3,512]{1,0:T(4,128)} %tap_ref.1, bf16[1024,1024]{1,0:T(8,128)(2,1)} %get-tuple-element.20.pn_ref, bf16[1024,1024]{1,0:T(8,128)(2,1)} %get-tuple-element.21.pn_recv, ...), custom_call_target="tpu_custom_call" | custom-call | tf_op jit(solution)/shard_map/back/pallas_call | solution.py:604
  275.2 0.0 copy-start.1
  275.3 1.9 slice.61
  277.2 1.6 slice_bitcast_fusion.3
  278.7 1.3 slice.62
  280.1 1.4 fusion.26
  281.4 2.7 slice_bitcast_fusion
  284.1 3.7 %fusion.13 = bf16[1,1024,512]{2,1,0:T(8,128)(2,1)} fusion(bf16[1024,512]{1,0:T(8,128)(2,1)} %get-tuple-element.19, f32[1024,512]{1,0:T(8,128)} %get-tuple-element.18, f32[1024,1024]{1,0:T(8,128)S(1)} %copy-done.1, s32[]{:T(128)S(6)} %select_n.3), kind=kLoop, calls=%fused_computation.24 | loop fusion | flops 2097152 | bytes 6291460 | tf_op jit(solution)/shard_map/reshape | solution.py:694
  287.8 1.3 copy.28
  (14 shorter events, 0.0 us)
Async XLA Ops:
  7.2 2.9 copy-start.2
  7.2 2.9 copy-start.12
  7.2 22.8 %all-gather.3.cloned.1.call-start = ((), (), s32[]{:S(2)}) async-start(), calls=%async_computation.1 | async-start | bytes 3145728 | tf_op jit(solution)/shard_map/all_gather | solution.py:683
  7.9 50.4 %all-reduce.3.cloned.1.call-start = ((), (), s32[]{:S(2)}) async-start(), calls=%async_computation | async-start | bytes 8388608 | tf_op jit(solution)/shard_map/psum | solution.py:681
  10.1 2.7 copy-start.6
  12.8 8.1 %copy-start.3 = (f32[1024,512]{1,0:T(8,128)}, f32[1024,512]{1,0:T(8,128)S(1)}, u32[]{:S(2)}) copy-start(f32[1024,512]{1,0:T(8,128)S(1)} %fusion.14.x_hbm) | copy-start | bytes 6291460
  14.1 6.8 %copy-start.4 = (f32[1024,512]{1,0:T(8,128)}, f32[1024,512]{1,0:T(8,128)S(1)}, u32[]{:S(2)}) copy-start(f32[1024,512]{1,0:T(8,128)S(1)} %fusion.16.b_hbm) | copy-start | bytes 6291460
  14.1 5.4 %copy-start.11 = (f32[3,512]{1,0:T(4,128)S(1)}, f32[3,512]{1,0:T(4,128)}, u32[]{:S(2)}) copy-start(f32[3,512]{1,0:T(4,128)} %tap_ref.1) | copy-start | bytes 18436
  14.6 6.2 %collective-permute-start = (f32[1,2,512]{2,1,0:T(2,128)S(1)}, f32[1,2,512]{2,1,0:T(2,128)S(1)}, u32[]{:S(2)}, u32[]{:S(2)}) collective-permute-start(f32[1,2,512]{2,1,0:T(2,128)S(1)} %slice.68), channel_id=1, source_target_pairs={{0,2},{2,4},{4,6},{6,8},{8,10},{10,12},{12,14},{1,3},{3,5},{5,7},{... | collective-permute-start | bytes 12296 | tf_op jit(solution)/shard_map/ppermute | solution.py:21
  20.9 4.0 %copy-start.8 = (bf16[512,1024]{1,0:T(8,128)(2,1)S(1)}, bf16[512,1024]{1,0:T(8,128)(2,1)}, u32[]{:S(2)}) copy-start(bf16[512,1024]{1,0:T(8,128)(2,1)} %out_weight_ref.1) | copy-start | bytes 3145732
  23.9 1.0 copy-start.9
  28.1 0.7 copy-start.10
  63.0 2.7 copy-start
  67.5 4.1 %copy-start.5 = (bf16[1024,1024]{0,1:T(8,128)(2,1)S(1)}, bf16[1024,1024]{0,1:T(8,128)(2,1)}, u32[]{:S(2)}) copy-start(bf16[1024,1024]{0,1:T(8,128)(2,1)} %get-tuple-element.28) | copy-start | bytes 6291460
  275.2 8.9 %copy-start.1 = (f32[1024,1024]{1,0:T(8,128)S(1)}, f32[1024,1024]{1,0:T(8,128)}, u32[]{:S(2)}) copy-start(f32[1024,1024]{1,0:T(8,128)} %copy-done) | copy-start | bytes 12582916
  284.1 3.7 %copy-start.7 = (f32[1024,512]{1,0:T(8,128)S(1)}, f32[1024,512]{1,0:T(8,128)}, u32[]{:S(2)}) copy-start(f32[1024,512]{1,0:T(8,128)} %get-tuple-element.22) | copy-start | bytes 6291460
Sparse Core Ops, SparseCore 0:
  9.5 13.2 all-gather.2
  28.2 30.0 all-reduce.2

commit v3 on v2

--- a/solution.py
+++ b/solution.py
@@ -15,12 +15,6 @@
 BF16 = jnp.bfloat16
 
 
-def shifted(value, axis, steps):
-    count = lax.axis_size(axis)
-    first, last = (max(0, -steps), min(count, count - steps))
-    return lax.ppermute(value, axis, [(source, source + steps) for source in range(first, last)])
-
-
 def inverse_rms(values):
     return lax.rsqrt(jnp.mean(values * values, axis=-1, keepdims=True) + EPSILON)
 
@@ -64,10 +58,11 @@
         seq = (self.me + steps) % self.seq_size
         return (self.me // self.seq_size, seq, self.core)
 
-    def greet(self, steps=()):
+    def greet(self, steps=(), shards=True):
         barrier = pltpu.get_barrier_semaphore()
-        partners = [self.place(self.flipped(1 << bit)) for bit in range(self.bits)]
-        partners.append(self.other_core())
+        partners = [self.other_core()]
+        if shards:
+            partners += [self.place(self.flipped(1 << bit)) for bit in range(self.bits)]
         partners.extend(self.along_seq(count) for count in steps)
         for partner in partners:
             pl.semaphore_signal(barrier, inc=1, device_id=partner, device_id_type=MESH)
@@ -172,6 +167,279 @@
         for stage in range(self.bits):
             self.copy(order, unit, stage).wait_send()
         return total
+
+
+def front_kernel(
+    plan,
+    gain_ref,
+    tap_ref,
+    token_hbm,
+    cot_hbm,
+    in_weight_hbm,
+    out_weight_hbm,
+    normed_ref,
+    cot_ref,
+    left_ref,
+    resid_hbm,
+    b_hbm,
+    c_hbm,
+    x_hbm,
+    mixed_hbm,
+    first_hbm,
+    prior_ref,
+    token_ref,
+    edge_ref,
+    in_weight_ref,
+    out_weight_ref,
+    b_ref,
+    c_ref,
+    x_ref,
+    gated_ref,
+    mixed_ref,
+    first_ref,
+    resid_ref,
+    part_ref,
+    part_recv,
+    token_sem,
+    weight_sem,
+    cot_sem,
+    cot_send,
+    cot_recv,
+    edge_send,
+    edge_recv,
+    swap_send,
+    swap_recv,
+    store_sem,
+):
+    total_rows, width = token_ref.shape
+    half = width // 2
+    step = min(256, total_rows)
+    steps = total_rows // step
+    edge = edge_ref.shape[0]
+    plan.enter()
+    seq = lax.axis_index("seq")
+    last = plan.seq_size - 1
+
+    def span(index):
+        return pl.ds(pl.multiple_of(index * step, step), step)
+
+    def load(index):
+        rows = span(index)
+        return pltpu.make_async_copy(token_hbm.at[rows], token_ref.at[rows], token_sem.at[index])
+
+    own = pl.ds(pl.multiple_of(plan.core * half, half), half)
+    for index in range(steps):
+        load(index).start()
+    weights = [
+        pltpu.make_async_copy(in_weight_hbm, in_weight_ref, weight_sem.at[0]),
+        pltpu.make_async_copy(out_weight_hbm, out_weight_ref, weight_sem.at[1]),
+    ]
+    for item in weights:
+        item.start()
+    cot_own = pltpu.make_async_copy(cot_hbm, cot_ref.at[:, own], cot_sem.at[0])
+    cot_own.start()
+    plan.greet((-1, 1), shards=False)
+    cot_swap = pltpu.make_async_remote_copy(
+        src_ref=cot_hbm,
+        dst_ref=cot_ref.at[:, own],
+        send_sem=cot_send.at[0],
+        recv_sem=cot_recv.at[0],
+        device_id=plan.other_core(),
+        device_id_type=MESH,
+    )
+
+    def edge_copy():
+        return pltpu.make_async_remote_copy(
+            src_ref=token_hbm.at[pl.ds(total_rows - edge, edge)],
+            dst_ref=edge_ref,
+            send_sem=edge_send.at[0],
+            recv_sem=edge_recv.at[0],
+            device_id=plan.along_seq(1),
+            device_id_type=MESH,
+        )
+
+    @pl.when(seq < last)
+    def _():
+        edge_copy().start()
+
+    cot_swap.start()
+    gain_one, gain_two = gain_ref[0:1], gain_ref[1:2]
+    taps = [tap_ref[k : k + 1] for k in range(3)]
+
+    def stores(index, pairs, first):
+        return [
+            pltpu.make_async_copy(source, target, store_sem.at[first + place, index])
+            for place, (source, target) in enumerate(pairs)
+        ]
+
+    def early_stores(index):
+        rows = span(index)
+        return stores(
+            index,
+            (
+                (b_ref.at[rows], b_hbm.at[rows]),
+                (c_ref.at[rows], c_hbm.at[rows]),
+                (x_ref.at[rows], x_hbm.at[rows]),
+                (first_ref.at[:, :, rows], first_hbm.at[:, :, rows]),
+            ),
+            0,
+        )
+
+    def late_stores(index):
+        rows = span(index)
+        return stores(
+            index,
+            (
+                (mixed_ref.at[rows], mixed_hbm.at[rows]),
+                (resid_ref.at[rows], resid_hbm.at[rows]),
+            ),
+            4,
+        )
+
+    def normalise(value, gain):
+        return (value * inverse_rms(value) * gain).astype(BF16)
+
+    weights[0].wait()
+
+    def first_pass(index, carry):
+        start = pl.multiple_of(index * step, step)
+        rows = pl.ds(start, step)
+        load(index).wait()
+        normed = normalise(token_ref[rows].astype(F32), gain_one)
+        b_signal = product(normed, in_weight_ref[0])
+        x_signal = product(normed, in_weight_ref[2])
+        b_ref[rows] = b_signal
+        x_ref[rows] = x_signal
+        gated_ref[pl.ds(start + 8, step)] = b_signal * x_signal
+        c_ref[rows] = product(normed, in_weight_ref[1])
+        first_ref[:, :, rows] = normed.T.reshape(plan.shards, plan.rows, step)
+        for item in early_stores(index):
+            item.start()
+        return carry
+
+    lax.fori_loop(0, steps, first_pass, 0)
+
+    @pl.when(seq > 0)
+    def _():
+        edge_copy().wait_recv()
+
+    @pl.when(seq == 0)
+    def _():
+        edge_ref[...] = jnp.zeros_like(edge_ref)
+
+    normed = normalise(edge_ref[...].astype(F32), gain_one)
+    gated = product(normed, in_weight_ref[0]) * product(normed, in_weight_ref[2])
+    gated_ref[0:8] = gated[edge - 8 : edge]
+    prior_ref[...] = gated[edge - 8 : edge]
+    weights[1].wait()
+
+    def swap(index):
+        rows = span(index)
+        return pltpu.make_async_remote_copy(
+            src_ref=part_ref.at[rows],
+            dst_ref=part_recv.at[rows],
+            send_sem=swap_send.at[index],
+            recv_sem=swap_recv.at[index],
+            device_id=plan.other_core(),
+            device_id_type=MESH,
+        )
+
+    def second_pass(index, carry):
+        start = pl.multiple_of(index * step, step)
+        rows = pl.ds(start, step)
+        window = gated_ref[pl.ds(start, step + 8)]
+        views = [window[6 + k : 6 + k + step] for k in range(3)]
+        conv_out = taps[0] * views[0] + taps[1] * views[1] + taps[2] * views[2]
+        mixed = (c_ref[rows] * conv_out).astype(BF16)
+        mixed_ref[rows] = mixed
+        part = product(mixed, out_weight_ref[...])
+        part_ref[rows] = part.astype(BF16)
+        swap(index).start()
+        resid_ref[rows] = token_ref[rows].astype(F32) + part
+        return carry
+
+    lax.fori_loop(0, steps, second_pass, 0)
+    cot_own.wait()
+    cot_swap.wait_recv()
+
+    def third_pass(index, carry):
+        rows = span(index)
+        swap(index).wait_recv()
+        resid = resid_ref[rows] + part_recv[rows].astype(F32)
+        resid_ref[rows] = resid
+        for item in late_stores(index):
+            item.start()
+        normed = normalise(resid, gain_two)
+        normed_ref[rows] = normed
+        left_ref[0, :, :, rows] = normed.T.reshape(plan.shards, plan.rows, step)
+        left_ref[1, :, :, rows] = cot_ref[rows].T.reshape(plan.shards, plan.rows, step)
+        return carry
+
+    lax.fori_loop(0, steps, third_pass, 0)
+    for index in range(steps):
+        for item in early_stores(index) + late_stores(index):
+            item.wait()
+        swap(index).wait_send()
+    cot_swap.wait_send()
+
+    @pl.when(seq < last)
+    def _():
+        edge_copy().wait_send()
+
+
+def front(plan, gains, taps, tokens, cotangent, in_weight, out_weight):
+    total_rows, width = tokens.shape
+    half = in_weight.shape[2]
+    steps = total_rows // min(256, total_rows)
+    shape = jax.ShapeDtypeStruct
+    dma = pltpu.SemaphoreType.DMA
+    chunked = (plan.shards, plan.rows, total_rows)
+    return pl.pallas_call(
+        functools.partial(front_kernel, plan),
+        name="front",
+        out_shape=(
+            shape((total_rows, width), BF16),
+            shape((total_rows, width), BF16),
+            shape((2,) + chunked, BF16),
+            shape((total_rows, width), F32),
+            shape((total_rows, half), F32),
+            shape((total_rows, half), F32),
+            shape((total_rows, half), F32),
+            shape((total_rows, half), BF16),
+            shape(chunked, BF16),
+            shape((8, half), F32),
+        ),
+        in_specs=[whole()] * 2 + [anywhere()] * 4,
+        out_specs=[whole()] * 3 + [anywhere()] * 6 + [whole()],
+        scratch_shapes=[
+            pltpu.VMEM((total_rows, width), BF16),
+            pltpu.VMEM((16, width), BF16),
+            pltpu.VMEM((3, width, half), BF16),
+            pltpu.VMEM((half, width), BF16),
+            pltpu.VMEM((total_rows, half), F32),
+            pltpu.VMEM((total_rows, half), F32),
+            pltpu.VMEM((total_rows, half), F32),
+            pltpu.VMEM((total_rows + 8, half), F32),
+            pltpu.VMEM((total_rows, half), BF16),
+            pltpu.VMEM(chunked, BF16),
+            pltpu.VMEM((total_rows, width), F32),
+            pltpu.VMEM((total_rows, width), BF16),
+            pltpu.VMEM((total_rows, width), BF16),
+            dma((steps,)),
+            dma((2,)),
+            dma((1,)),
+            dma((1,)),
+            dma((1,)),
+            dma((1,)),
+            dma((1,)),
+            dma((steps,)),
+            dma((steps,)),
+            dma((6, steps)),
+        ],
+        compiler_params=pltpu.CompilerParams(
+            collective_id=2, has_side_effects=True, vmem_limit_bytes=VMEM_BYTES
+        ),
+    )(gains, taps, tokens, cotangent, in_weight, out_weight)
 
 
 def ffn_kernel(
@@ -659,31 +927,23 @@
     out_cotangent,
 ):
     seqs, length, width = tokens.shape
+    assert seqs == 1
     half = in_weight.shape[2]
     total_rows = seqs * length
     chunk_rows = width // shards
     plan = Halving(seq_size, shards, chunk_rows)
     start = lax.axis_index("tensor") * half
-    token_float = tokens.reshape(total_rows, width).astype(F32)
-    normed = (token_float * inverse_rms(token_float) * norm1_gain).astype(BF16)
-    b_signal = product(normed, in_weight[0])
-    c_signal = product(normed, in_weight[1])
-    x_signal = product(normed, in_weight[2])
-    gated = (b_signal * x_signal).reshape(seqs, length, half)
-    prior = shifted(gated[:, length - 2 :], "seq", 1)
-    extended = jnp.concatenate([prior, gated], axis=1)
-    conv_out = (
-        conv_weight[0] * extended[:, 0:length]
-        + conv_weight[1] * extended[:, 1 : length + 1]
-        + conv_weight[2] * extended[:, 2 : length + 2]
-    ).reshape(total_rows, half)
-    mixed_in = (c_signal * conv_out).astype(BF16)
-    resid = token_float + lax.psum(product(mixed_in, out_weight), "tensor")
-    normed_two = (resid * inverse_rms(resid) * norm2_gain).astype(BF16)
-    cotangent = lax.all_gather(
-        out_cotangent.reshape(total_rows, half), "tensor", axis=1, tiled=True
+    gains = jnp.stack([norm1_gain, norm2_gain])
+    tokens = tokens.reshape(total_rows, width)
+    normed_two, cotangent, left, resid, b_signal, c_signal, x_signal, mixed_in, first, prior = front(
+        plan,
+        gains,
+        conv_weight,
+        tokens,
+        out_cotangent.reshape(total_rows, half),
+        in_weight,
+        out_weight,
     )
-    left = jnp.stack([normed_two.T, cotangent.T]).reshape(2, shards, chunk_rows, total_rows)
     ffn_grads, pn_own, pn_other, out_own, out_other = ffn(
         plan, normed_two, cotangent, left, gate_weight, up_weight, down_weight
     )
@@ -695,17 +955,17 @@
     )
     mix_grads, tokens_grad, small = back(
         plan,
-        jnp.stack([norm1_gain, norm2_gain]),
+        gains,
         conv_weight,
         pn_own,
         pn_other,
         cotangent,
         mixed_in,
-        jnp.pad(prior[0], ((6, 0), (0, 0))),
+        prior,
         out_weight,
         in_weight,
-        normed.T.reshape(shards, chunk_rows, total_rows),
-        (resid, tokens.reshape(total_rows, width), b_signal, c_signal, x_signal),
+        first,
+        (resid, tokens, b_signal, c_signal, x_signal),
     )
     in_grad, out_grad = mix_grads[0:3], mix_grads[3].T
     conv_grad, norm1_grad, norm2_grad = small[0:3], small[3], small[4]

time: 296 us -> 231 us (0.78)
  waiting for transfers between devices: 26.4 us -> 0 us
  Pallas kernels: 197 us -> 214 us
  other arithmetic: 20 us -> 5.56 us
  local copies, waits for them, and re-layouts: 23.7 us -> 9.58 us
  between operations: 14.2 us -> 0.67 us
  matrix products: 10.2 us -> 0 us
  starting transfers between devices: 4.98 us -> 0 us
    psum x1 -> x0, waiting for transfers between devices: 24.4 us -> none  [local(): resid = token_float + lax.psum(product(mixed_in, out_weight), 'tensor')]
    pallas_call x0 -> x1, Pallas kernels: none -> 20.8 us  [front(): pl.pallas_call(functools.partial(front_kernel, plan), name='front', out_s...]
    transpose x3 -> x0, local copies, waits for them, and re-layouts: 10.6 us -> none  [the longest x2 8.04 us: local(): left = jnp.stack([normed_two.T, cotangent.T]).reshape(2, shards, chunk_ro...]
    dot_general x4 -> x0, matrix products: 10.2 us -> none  [product(): return jnp.dot(left, right, preferred_element_type=F32)]
    reduce_sum x2 -> x0, other arithmetic: 6.76 us -> none  [inverse_rms(): jnp.mean(values * values, axis=-1, keepdims=True) + EPSILON]
    ppermute x1 -> x0, starting transfers between devices: 4.9 us -> none  [shifted(): lax.ppermute(value, axis, [(source, source + steps) for source in range(f...]
    another operation x2 -> x1, other arithmetic: 5.2 us -> 1.31 us  [local(): gains = jnp.stack([norm1_gain, norm2_gain])]
  transfers between devices with their start and end apart: 3 -> 0, of which waited for: 2 -> 0; matrix products, arithmetic and copies ran while one was open for 6% -> 0% of each run, Pallas kernels for 0% -> 0%
where the time goes in v3:
time: 231 us; the launch traced here: 230 us
  Pallas kernels  214 us (93%)
  local copies, waits for them, and re-layouts  9.58 us (4%)
  other arithmetic  5.56 us (2%)
    pallas_call x1, Pallas kernels, ffn(): pl.pallas_call(functools.partial(ffn_kernel, plan), name='ffn', out_shape...  127 us
    pallas_call x1, Pallas kernels, back(): pl.pallas_call(functools.partial(back_kernel, plan), name='back', out_sha...  65.8 us
    pallas_call x1, Pallas kernels, front(): pl.pallas_call(functools.partial(front_kernel, plan), name='front', out_s...  20.8 us

profile of v3, /device:TPU:0, one launch (start us, length us, event | category | flops | bytes accessed | tf_op | source)
XLA Modules:
  0.0 229.9 jit_solution(12334054455751555536)
XLA Ops:
  0.6 1.3 pad_maximum_fusion.gain_ref
  2.0 20.8 %front.1 = (bf16[1024,1024]{1,0:T(8,128)(2,1)}, bf16[1024,1024]{1,0:T(8,128)(2,1)}, bf16[2,16,64,1024]{3,2,1,0:T(8,128)(2,1)}, f32[1024,1024]{1,0:T(8,128)}, f32...) custom-call(f32[2,1024]{1,0:T(2,128)} %pad_maximum_fusion.gain_ref, ...), custom_call_target="tpu_custom_call" | custom-call | tf_op jit(solution)/shard_map/front/pallas_call | solution.py:397
  22.8 127.5 %ffn.1 = (f32[3,64,2304]{2,1,0:T(8,128)}, bf16[1024,1024]{1,0:T(8,128)(2,1)}, bf16[1024,1024]{1,0:T(8,128)(2,1)}, f32[1024,512]{1,0:T(8,128)}, bf16[1024,512]{1,0:T(8,128)(2,1)}) custom-call(bf16[1024,1024]{1,0:T(8,128)(2,1)} %get-tuple-element.29.normed_ref, bf16[1024,1024]{1,0:T(8,128)(2,1)} %get-tuple-element.30.cot_ref, ...), custom_call_target="tpu_custom_call" | custom-call | tf_op jit(solution)/shard_map/ffn/pallas_call | solution.py:587
  150.3 65.8 %back.1 = (f32[4,64,512]{2,1,0:T(8,128)}, f32[1024,512]{1,0:T(8,128)}, f32[8,512]{1,0:T(8,128)}) custom-call(f32[2,1024]{1,0:T(2,128)} %pad_maximum_fusion.gain_ref, f32[3,512]{1,0:T(4,128)} %tap_ref.3, bf16[1024,1024]{1,0:T(8,128)(2,1)} %get-tuple-element.34.pn_ref, bf16[1024,1024]{1,0:T(8,128)(2,1)} %get-tuple-element.35.pn_recv, ...), custom_call_target="tpu_custom_call" | custom-call | tf_op jit(solution)/shard_map/back/pallas_call | solution.py:872
  216.1 1.8 slice.25
  217.8 1.6 slice_bitcast_fusion.3
  219.4 1.3 slice.26
  220.7 1.4 fusion.1
  222.1 0.0 copy-start.1
  222.1 4.2 %fusion = bf16[1,1024,512]{2,1,0:T(8,128)(2,1)} fusion(bf16[1024,512]{1,0:T(8,128)(2,1)} %get-tuple-element.33, f32[1024,512]{1,0:T(8,128)} %get-tuple-element.32, f32[1024,1024]{1,0:T(8,128)} %get-tuple-element.28.resid_hbm, s32[]{:T(128)S(6)} %select_n.3), kind=kLoop, calls=%fused_computation.1 | loop fusion | flops 2097152 | bytes 6291460 | tf_op jit(solution)/shard_map/reshape | solution.py:954
  226.4 0.0 copy-start
  226.4 0.0 copy-done.1
  226.4 1.2 slice_bitcast_fusion
  227.6 1.0 copy-done
  228.6 1.3 copy.21
Async XLA Ops:
  222.1 4.3 %copy-start.1 = (f32[3,64,2304]{2,1,0:T(8,128)S(1)}, f32[3,64,2304]{2,1,0:T(8,128)}, u32[]{:S(2)}) copy-start(f32[3,64,2304]{2,1,0:T(8,128)} %get-tuple-element.45) | copy-start | bytes 5308420
  226.4 2.2 copy-start

commit v4 on v3

v4 whole, which is shorter than its diff:
```python
import functools

import jax
import jax.numpy as jnp
from jax import lax
from jax.experimental import pallas as pl
from jax.experimental.pallas import tpu as pltpu
from jax.sharding import PartitionSpec as P

EPSILON = 1e-05
MESH = pl.DeviceIdType.MESH
UNIT = 256
RING = 8
PACE = (5, 28)
LAGS = (-30, 9, 35, 65, 90)
STEPS = (5, 7, 2, 3, 2, 4, 4)
VMEM_BYTES = 67043328
F32 = jnp.float32
BF16 = jnp.bfloat16


def inverse_rms(values):
    return lax.rsqrt(jnp.mean(values * values, axis=-1, keepdims=True) + EPSILON)


def product(left, right):
    return jnp.dot(left, right, preferred_element_type=F32)


def product_t(left, right):
    return lax.dot_general(left, right, (((1,), (1,)), ((), ())), preferred_element_type=F32)


class Halving:
    def __init__(self, seq_size, shards, rows):
        self.seq_size = seq_size
        self.bits = shards.bit_length() - 1
        self.shards = shards
        self.rows = rows

    def stage_rows(self, stage):
        return self.rows << (self.bits - 1 - stage)

    def enter(self):
        self.me = lax.axis_index("dp") * self.seq_size + lax.axis_index("seq")
        self.core = lax.axis_index("tensor")

    def place(self, flat):
        return (flat // self.seq_size, flat % self.seq_size, self.core)

    def flipped(self, weight):
        return self.me + (1 - 2 * ((self.me // weight) % 2)) * weight

    def other_core(self):
        return (self.me // self.seq_size, self.me % self.seq_size, 1 - self.core)

    def along_seq(self, steps):
        seq = (self.me + steps) % self.seq_size
        return (self.me // self.seq_size, seq, self.core)

    def greet(self, steps=(), shards=True):
        barrier = pltpu.get_barrier_semaphore()
        partners = [self.other_core()]
        if shards:
            partners += [self.place(self.flipped(1 << bit)) for bit in range(self.bits)]
        partners.extend(self.along_seq(count) for count in steps)
        for partner in partners:
            pl.semaphore_signal(barrier, inc=1, device_id=partner, device_id_type=MESH)
        pl.semaphore_wait(barrier, len(partners))

    def order(self, parity):
        top = self.shards // 2
        high = (self.me // top) % 2
        low = self.me % 2
        first = (top + parity * (1 - top), high + parity * (low - high))
        third = (1 + parity * (top - 1), low + parity * (high - low))
        middle = [(2, (self.me // 2) % 2)]
        rest = [(1 << bit, (self.me // (1 << bit)) % 2) for bit in range(2, self.bits - 1)]
        return [first] + middle + [third] + rest

    def chunks(self, order, keep):
        weight, bit = order[0]
        base = (bit if keep else 1 - bit) * weight
        found = []
        for code in range(self.shards // 2):
            chunk = base
            for place in range(1, self.bits):
                if (code >> (self.bits - 1 - place)) & 1:
                    chunk = chunk + order[place][0]
            found.append(chunk)
        return found

    def offset(self, order, source, stage):
        total = 0
        for place in range(source + 1, min(stage, self.bits - 1) + 1):
            bit = order[place][1]
            if place == stage:
                bit = 1 - bit
            total = total + bit * (1 << (self.bits - 1 - place))
        return total * self.rows

    def scratch(self, units):
        half = self.stage_rows(0)
        ring = min(RING, units)
        return (
            [pltpu.VMEM((ring, half, UNIT), BF16), pltpu.VMEM((units, half, UNIT), BF16)]
            + [pltpu.VMEM((units, self.stage_rows(s), UNIT), BF16) for s in range(self.bits)]
            + [
                pltpu.SemaphoreType.DMA((self.bits, units)),
                pltpu.SemaphoreType.DMA((self.bits, units)),
            ]
        )

    def bind(self, refs):
        self.first, self.keep = refs[0], refs[1]
        self.recv = refs[2 : 2 + self.bits]
        self.send_sem, self.recv_sem = refs[2 + self.bits :]

    def copy(self, order, unit, stage):
        weight, bit = order[stage]
        if stage == 0:
            source = self.first.at[unit % RING]
        else:
            start = pl.multiple_of(self.offset(order, 0, stage), self.rows)
            source = self.keep.at[unit, pl.ds(start, self.stage_rows(stage))]
        return pltpu.make_async_remote_copy(
            src_ref=source,
            dst_ref=self.recv[stage].at[unit],
            send_sem=self.send_sem.at[stage, unit],
            recv_sem=self.recv_sem.at[stage, unit],
            device_id=self.place(self.me + (1 - 2 * bit) * weight),
            device_id_type=MESH,
        )

    def gather(self, left, order, keep):
        return jnp.concatenate([left[chunk] for chunk in self.chunks(order, keep)], axis=0)

    def begin(self, unit, parity, left, right):
        order = self.order(parity)

        @pl.when(unit >= RING)
        def _():
            self.copy(order, unit - RING, 0).wait_send()

        value = product(self.gather(left, order, False), right[...]).astype(BF16)
        self.first[unit % RING] = value

    def launch(self, unit, parity):
        self.copy(self.order(parity), unit, 0).start()

    def hold(self, unit, parity, left, right):
        order = self.order(parity)
        self.keep[unit] = product(self.gather(left, order, True), right[...]).astype(BF16)

    def collect(self, order, unit, stage, rows):
        start = pl.multiple_of(self.offset(order, 0, stage), self.rows)
        total = self.keep[unit, pl.ds(start, rows)].astype(F32)
        for source in range(min(stage, self.bits)):
            start = pl.multiple_of(self.offset(order, source, stage), self.rows)
            total = total + self.recv[source][unit, pl.ds(start, rows)].astype(F32)
        return total

    def advance(self, unit, parity, stage):
        order = self.order(parity)
        self.copy(order, unit, stage - 1).wait_recv()
        rows = self.stage_rows(stage)
        total = self.collect(order, unit, stage, rows)
        start = pl.multiple_of(self.offset(order, 0, stage), self.rows)
        self.keep[unit, pl.ds(start, rows)] = total.astype(BF16)
        self.copy(order, unit, stage).start()

    def finish(self, unit, parity):
        order = self.order(parity)
        self.copy(order, unit, self.bits - 1).wait_recv()
        total = self.collect(order, unit, self.bits, self.rows)
        for stage in range(1, self.bits):
            self.copy(order, unit, stage).wait_send()
        return total


def front_kernel(
    plan,
    gain_ref,
    tap_ref,
    token_hbm,
    cot_hbm,
    in_weight_hbm,
    out_weight_hbm,
    normed_hbm,
    cot_full_hbm,
    left_hbm,
    resid_hbm,
    b_hbm,
    c_hbm,
    x_hbm,
    mixed_hbm,
    first_hbm,
    prior_ref,
    normed_ref,
    cot_ref,
    left_ref,
    token_ref,
    edge_ref,
    in_weight_ref,
    out_weight_ref,
    b_ref,
    c_ref,
    x_ref,
    gated_ref,
    mixed_ref,
    first_ref,
    resid_ref,
    part_ref,
    part_recv,
    token_sem,
    weight_sem,
    cot_sem,
    cot_send,
    cot_recv,
    edge_send,
    edge_recv,
    swap_send,
    swap_recv,
    store_sem,
):
    total_rows, width = token_ref.shape
    half = width // 2
    step = min(256, total_rows)
    steps = total_rows // step
    edge = edge_ref.shape[0]
    plan.enter()
    seq = lax.axis_index("seq")
    last = plan.seq_size - 1

    def span(index):
        return pl.ds(pl.multiple_of(index * step, step), step)

    def load(index):
        rows = span(index)
        return pltpu.make_async_copy(token_hbm.at[rows], token_ref.at[rows], token_sem.at[index])

    own = pl.ds(pl.multiple_of(plan.core * half, half), half)
    for index in range(steps):
        load(index).start()
    weights = [
        pltpu.make_async_copy(in_weight_hbm, in_weight_ref, weight_sem.at[0]),
        pltpu.make_async_copy(out_weight_hbm, out_weight_ref, weight_sem.at[1]),
    ]
    for item in weights:
        item.start()
    cot_own = pltpu.make_async_copy(cot_hbm, cot_ref.at[:, own], cot_sem.at[0])
    cot_own.start()
    plan.greet((-1, 1), shards=False)
    cot_swap = pltpu.make_async_remote_copy(
        src_ref=cot_hbm,
        dst_ref=cot_ref.at[:, own],
        send_sem=cot_send.at[0],
        recv_sem=cot_recv.at[0],
        device_id=plan.other_core(),
        device_id_type=MESH,
    )

    def edge_copy():
        return pltpu.make_async_remote_copy(
            src_ref=token_hbm.at[pl.ds(total_rows - edge, edge)],
            dst_ref=edge_ref,
            send_sem=edge_send.at[0],
            recv_sem=edge_recv.at[0],
            device_id=plan.along_seq(1),
            device_id_type=MESH,
        )

    @pl.when(seq < last)
    def _():
        edge_copy().start()

    cot_swap.start()
    gain_one, gain_two = gain_ref[0:1], gain_ref[1:2]
    taps = [tap_ref[k : k + 1] for k in range(3)]

    def stores(index, pairs, first):
        return [
            pltpu.make_async_copy(source, target, store_sem.at[first + place, index])
            for place, (source, target) in enumerate(pairs)
        ]

    def early_stores(index):
        rows = span(index)
        return stores(
            index,
            (
                (b_ref.at[rows], b_hbm.at[rows]),
                (c_ref.at[rows], c_hbm.at[rows]),
                (x_ref.at[rows], x_hbm.at[rows]),
                (first_ref.at[:, :, rows], first_hbm.at[:, :, rows]),
            ),
            0,
        )

    def late_stores(index):
        rows = span(index)
        return stores(
            index,
            (
                (mixed_ref.at[rows], mixed_hbm.at[rows]),
                (resid_ref.at[rows], resid_hbm.at[rows]),
                (normed_ref.at[rows], normed_hbm.at[rows]),
                (cot_ref.at[rows], cot_full_hbm.at[rows]),
                (left_ref.at[:, :, :, rows], left_hbm.at[:, :, :, rows]),
            ),
            4,
        )

    def normalise(value, gain):
        return (value * inverse_rms(value) * gain).astype(BF16)

    weights[0].wait()

    def first_pass(index, carry):
        start = pl.multiple_of(index * step, step)
        rows = pl.ds(start, step)
        load(index).wait()
        normed = normalise(token_ref[rows].astype(F32), gain_one)
        b_signal = product(normed, in_weight_ref[0])
        x_signal = product(normed, in_weight_ref[2])
        b_ref[rows] = b_signal
        x_ref[rows] = x_signal
        gated_ref[pl.ds(start + 8, step)] = b_signal * x_signal
        c_ref[rows] = product(normed, in_weight_ref[1])
        first_ref[:, :, rows] = normed.T.reshape(plan.shards, plan.rows, step)
        for item in early_stores(index):
            item.start()
        return carry

    lax.fori_loop(0, steps, first_pass, 0)

    @pl.when(seq > 0)
    def _():
        edge_copy().wait_recv()

    @pl.when(seq == 0)
    def _():
        edge_ref[...] = jnp.zeros_like(edge_ref)

    normed = normalise(edge_ref[...].astype(F32), gain_one)
    gated = product(normed, in_weight_ref[0]) * product(normed, in_weight_ref[2])
    gated_ref[0:8] = gated[edge - 8 : edge]
    prior_ref[...] = gated[edge - 8 : edge]
    weights[1].wait()

    def swap(index):
        rows = span(index)
        return pltpu.make_async_remote_copy(
            src_ref=part_ref.at[rows],
            dst_ref=part_recv.at[rows],
            send_sem=swap_send.at[index],
            recv_sem=swap_recv.at[index],
            device_id=plan.other_core(),
            device_id_type=MESH,
        )

    def second_pass(index, carry):
        start = pl.multiple_of(index * step, step)
        rows = pl.ds(start, step)
        window = gated_ref[pl.ds(start, step + 8)]
        views = [window[6 + k : 6 + k + step] for k in range(3)]
        conv_out = taps[0] * views[0] + taps[1] * views[1] + taps[2] * views[2]
        mixed = (c_ref[rows] * conv_out).astype(BF16)
        mixed_ref[rows] = mixed
        part = product(mixed, out_weight_ref[...])
        part_ref[rows] = part.astype(BF16)
        swap(index).start()
        resid_ref[rows] = token_ref[rows].astype(F32) + part
        return carry

    lax.fori_loop(0, steps, second_pass, 0)
    cot_own.wait()
    cot_swap.wait_recv()

    def third_pass(index, carry):
        rows = span(index)
        swap(index).wait_recv()
        resid = resid_ref[rows] + part_recv[rows].astype(F32)
        resid_ref[rows] = resid
        normed = normalise(resid, gain_two)
        normed_ref[rows] = normed
        left_ref[0, :, :, rows] = normed.T.reshape(plan.shards, plan.rows, step)
        left_ref[1, :, :, rows] = cot_ref[rows].T.reshape(plan.shards, plan.rows, step)
        for item in late_stores(index):
            item.start()
        return carry

    lax.fori_loop(0, steps, third_pass, 0)
    for index in range(steps):
        for item in early_stores(index) + late_stores(index):
            item.wait()
        swap(index).wait_send()
    cot_swap.wait_send()

    @pl.when(seq < last)
    def _():
        edge_copy().wait_send()


def front(plan, gains, taps, tokens, cotangent, in_weight, out_weight):
    total_rows, width = tokens.shape
    half = in_weight.shape[2]
    steps = total_rows // min(256, total_rows)
    shape = jax.ShapeDtypeStruct
    dma = pltpu.SemaphoreType.DMA
    chunked = (plan.shards, plan.rows, total_rows)
    return pl.pallas_call(
        functools.partial(front_kernel, plan),
        name="front",
        out_shape=(
            shape((total_rows, width), BF16),
            shape((total_rows, width), BF16),
            shape((2,) + chunked, BF16),
            shape((total_rows, width), F32),
            shape((total_rows, half), F32),
            shape((total_rows, half), F32),
            shape((total_rows, half), F32),
            shape((total_rows, half), BF16),
            shape(chunked, BF16),
            shape((8, half), F32),
        ),
        in_specs=[whole()] * 2 + [anywhere()] * 4,
        out_specs=[anywhere()] * 9 + [whole()],
        scratch_shapes=[
            pltpu.VMEM((total_rows, width), BF16),
            pltpu.VMEM((total_rows, width), BF16),
            pltpu.VMEM((2,) + chunked, BF16),
            pltpu.VMEM((total_rows, width), BF16),
            pltpu.VMEM((16, width), BF16),
            pltpu.VMEM((3, width, half), BF16),
            pltpu.VMEM((half, width), BF16),
            pltpu.VMEM((total_rows, half), F32),
            pltpu.VMEM((total_rows, half), F32),
            pltpu.VMEM((total_rows, half), F32),
            pltpu.VMEM((total_rows + 8, half), F32),
            pltpu.VMEM((total_rows, half), BF16),
            pltpu.VMEM(chunked, BF16),
            pltpu.VMEM((total_rows, width), F32),
            pltpu.VMEM((total_rows, width), BF16),
            pltpu.VMEM((total_rows, width), BF16),
            dma((steps,)),
            dma((2,)),
            dma((1,)),
            dma((1,)),
            dma((1,)),
            dma((1,)),
            dma((1,)),
            dma((steps,)),
            dma((steps,)),
            dma((9, steps)),
        ],
        compiler_params=pltpu.CompilerParams(
            collective_id=2, has_side_effects=True, vmem_limit_bytes=VMEM_BYTES
        ),
    )(gains, taps, tokens, cotangent, in_weight, out_weight)


def whole():
    return pl.BlockSpec(memory_space=pltpu.VMEM)


def anywhere():
    return pl.BlockSpec(memory_space=pl.ANY)


def main_kernel(
    plan,
    gain_ref,
    tap_ref,
    prior_ref,
    normed_hbm,
    cot_hbm,
    left_hbm,
    gate_hbm,
    up_hbm,
    down_hbm,
    out_weight_hbm,
    in_weight_hbm,
    first_hbm,
    mixed_hbm,
    resid_hbm,
    token_hbm,
    b_hbm,
    c_hbm,
    x_hbm,
    grads_ref,
    small_ref,
    block_hbm,
    tokens_hbm,
    normed_ref,
    cot_ref,
    left_ref,
    gate_buf,
    up_buf,
    down_buf,
    right_ref,
    pn_acc,
    out_acc,
    mixed_ref,
    pn_recv,
    out_recv,
    out_weight_ref,
    x_weight_ref,
    resid_buf,
    token_buf,
    full_ref,
    block_buf,
    sums_ref,
    small_send,
    small_recv,
    weight_sem,
    load_sem,
    late_sem,
    resid_sem,
    token_sem,
    block_sem,
    store_sem,
    pn_send_sem,
    pn_recv_sem,
    out_send_sem,
    out_recv_sem,
    part_send_sem,
    part_recv_sem,
    halo_send,
    halo_recv,
    small_send_sem,
    small_recv_sem,
    free_sem,
    *refs,
):
    total_rows, width = normed_ref.shape
    blocks = gate_hbm.shape[1] // UNIT
    half = width // 2
    step = min(256, total_rows)
    steps = total_rows // step
    pieces = half // UNIT
    early = 3 * blocks
    units = early + 4 * pieces
    plan.bind(refs)
    plan.enter()
    seq = lax.axis_index("seq")
    last = plan.seq_size - 1
    own = pl.ds(pl.multiple_of(plan.core * half, half), half)
    other = pl.ds(pl.multiple_of((1 - plan.core) * half, half), half)

    def span(index):
        return pl.ds(pl.multiple_of(index * step, step), step)

    def later(index):
        return pl.ds(pl.multiple_of(index * step + 8, 8), step)

    def local_copy(source, target, sem):
        return pltpu.make_async_copy(source, target, sem)

    def core_copy(source, target, send, recv):
        return pltpu.make_async_remote_copy(
            src_ref=source,
            dst_ref=target,
            send_sem=send,
            recv_sem=recv,
            device_id=plan.other_core(),
            device_id_type=MESH,
        )

    def weights(index):
        slot = index % 2
        columns = pl.ds(pl.multiple_of(index * UNIT, UNIT), UNIT)
        tall = pl.ds(0, width)
        return [
            local_copy(gate_hbm.at[:, columns], gate_buf.at[slot, tall], weight_sem.at[0, slot]),
            local_copy(up_hbm.at[:, columns], up_buf.at[slot, tall], weight_sem.at[1, slot]),
            local_copy(down_hbm.at[columns], down_buf.at[slot], weight_sem.at[2, slot]),
        ]

    def rows_loads(index):
        rows = span(index)
        return [
            local_copy(normed_hbm.at[rows], normed_ref.at[rows], load_sem.at[0, index]),
            local_copy(cot_hbm.at[rows], cot_ref.at[rows], load_sem.at[1, index]),
        ]

    def side_loads():
        return [
            local_copy(left_hbm, left_ref, late_sem.at[0]),
            local_copy(out_weight_hbm, out_weight_ref, late_sem.at[1]),
            local_copy(in_weight_hbm.at[2], x_weight_ref, late_sem.at[2]),
        ]

    def back_loads(index):
        rows = span(index)
        low, high = pl.ds(0, half), pl.ds(half, half)
        return [
            local_copy(b_hbm.at[rows], pn_acc.at[later(index), low], load_sem.at[2, index]),
            local_copy(x_hbm.at[rows], pn_acc.at[later(index), high], load_sem.at[3, index]),
            local_copy(c_hbm.at[rows], out_acc.at[rows, other], load_sem.at[4, index]),
        ]

    def resid_load(index):
        slot = index % 2
        return local_copy(resid_hbm.at[span(index)], resid_buf.at[slot], resid_sem.at[slot])

    def token_load(index):
        slot = index % 2
        return local_copy(token_hbm.at[span(index)], token_buf.at[slot], token_sem.at[slot])

    def block_store(index):
        slot = index % 2
        return local_copy(block_buf.at[slot], block_hbm.at[span(index)], block_sem.at[slot])

    def token_store(index):
        rows = span(index)
        return local_copy(out_acc.at[rows, own], tokens_hbm.at[rows], store_sem.at[index])

    def in_weight_loads():
        tall = pl.ds(0, width)
        return [
            local_copy(
                in_weight_hbm.at[place],
                cot_ref.at[tall, pl.ds(place * half, half)],
                late_sem.at[3 + place],
            )
            for place in range(2)
        ]

    def first_load():
        return local_copy(first_hbm, left_ref.at[0], late_sem.at[5])

    def mixed_load():
        return local_copy(mixed_hbm, mixed_ref, late_sem.at[6])

    def pn_swap(index):
        rows = span(index)
        return core_copy(
            normed_ref.at[rows], pn_recv.at[rows], pn_send_sem.at[index], pn_recv_sem.at[index]
        )

    def out_swap(index):
        rows = span(index)
        return core_copy(
            mixed_ref.at[rows], out_recv.at[rows], out_send_sem.at[index], out_recv_sem.at[index]
        )

    def part_swap(index):
        rows = span(index)
        return core_copy(
            normed_ref.at[rows],
            pn_recv.at[rows],
            part_send_sem.at[index],
            part_recv_sem.at[index],
        )

    def halo():
        return pltpu.make_async_remote_copy(
            src_ref=out_acc.at[pl.ds(0, 8), other],
            dst_ref=out_acc.at[pl.ds(total_rows, 8), other],
            send_sem=halo_send.at[0],
            recv_sem=halo_recv.at[0],
            device_id=plan.along_seq(-1),
            device_id_type=MESH,
        )

    def small(bit):
        return pltpu.make_async_remote_copy(
            src_ref=small_send.at[bit],
            dst_ref=small_recv.at[bit],
            send_sem=small_send_sem.at[bit],
            recv_sem=small_recv_sem.at[bit],
            device_id=plan.place(plan.flipped(1 << bit)),
            device_id_type=MESH,
        )

    def limit(stage, clock, floor, cap):
        lag = LAGS[min(stage, len(LAGS) - 1)] + 12 * max(0, stage - len(LAGS) + 1)
        if stage:
            floor = 0
        count = (clock - lag) * PACE[0] // PACE[1]
        if all(isinstance(value, int) for value in (clock, floor, cap)):
            return max(floor, min(count, cap), 0)
        return jnp.maximum(jnp.maximum(jnp.minimum(count, cap), floor), 0)

    def tick(before, after):
        for stage in range(plan.bits + 1):
            low = limit(stage, before[0], before[1], before[2 + (stage > 0)])
            high = limit(stage, after[0], after[1], after[2 + (stage > 0)])
            if isinstance(low, int) and isinstance(high, int) and low >= high:
                continue

            def advance(unit, carry, stage=stage):
                if stage == 0:
                    plan.launch(unit, unit % 2)
                elif stage < plan.bits:
                    plan.advance(unit, unit % 2, stage)
                else:
                    grads_ref[unit] = plan.finish(unit, unit % 2)
                return carry

            lax.fori_loop(low, high, advance, 0)

    for item in weights(0):
        item.start()
    for index in range(steps):
        for item in rows_loads(index):
            item.start()
    for item in side_loads():
        item.start()
    for index in range(min(2, steps)):
        resid_load(index).start()
        token_load(index).start()
    plan.greet((-1, 1))
    pn_acc[...] = jnp.zeros_like(pn_acc)
    out_acc[...] = jnp.zeros_like(out_acc)
    sums_ref[...] = jnp.zeros_like(sums_ref)

    def block_step(index, carry):
        slot = index % 2

        @pl.when(index + 1 < blocks)
        def _():
            for item in weights(index + 1):
                item.start()

        for item in weights(index):
            item.wait()
        for place in range(steps):
            rows = pl.ds(place * step, step)

            @pl.when(index == 0)
            def _(place=place):
                for item in rows_loads(place):
                    item.wait()

            normed = normed_ref[rows]
            gate_pre = product(normed, gate_buf[slot, 0:width])
            up_pre = product(normed, up_buf[slot, 0:width])
            grad_hidden = product_t(cot_ref[rows], down_buf[slot])
            sigma = jax.nn.sigmoid(gate_pre)
            active = gate_pre * sigma
            right_ref[0, rows] = (
                grad_hidden * up_pre * (sigma * (1.0 + gate_pre * (1.0 - sigma)))
            ).astype(BF16)
            right_ref[1, rows] = (grad_hidden * active).astype(BF16)
            right_ref[2, rows] = (active * up_pre).astype(BF16)

        @pl.when(index == 0)
        def _():
            for item in side_loads():
                item.wait()

        start, stop = index * 3, index * 3 + 3
        marks = [
            (12 * index, start - RING, start, start),
            (12 * index + 4, stop - RING, start, start),
            (12 * index + 6, stop - RING, stop, start),
            (12 * index + 10, stop - RING, stop, start),
            (12 * index + 12, stop - RING, stop, stop),
        ]
        tick(marks[0], marks[1])
        for place in range(3):
            unit = index * 3 + place
            plan.begin(unit, unit % 2, left_ref.at[place // 2], right_ref.at[place])
        tick(marks[1], marks[2])
        for place in range(steps):
            rows = pl.ds(place * step, step)
            pn_acc[pl.ds(place * step + 8, step)] += product_t(
                right_ref[0, rows], gate_buf[slot, 0:width]
            ) + product_t(right_ref[1, rows], up_buf[slot, 0:width])
            out_acc[rows] += product(right_ref[2, rows], down_buf[slot])
        tick(marks[2], marks[3])
        for place in range(3):
            unit = index * 3 + place
            plan.hold(unit, unit % 2, left_ref.at[place // 2], right_ref.at[place])
        tick(marks[3], marks[4])
        return carry

    lax.fori_loop(0, blocks, block_step, 0)
    mark = (12 * blocks, early - RING, early, early)

    def paced(mark, clock, body):
        def run(index, carry):
            body(index)
            before = mark[0] + clock * index
            tick((before,) + mark[1:], (before + clock,) + mark[1:])
            return carry

        lax.fori_loop(0, steps, run, 0)
        return (mark[0] + clock * steps,) + mark[1:]

    def move(mark, clock, begun=None, held=None):
        begun = mark[2] if begun is None else begun
        held = mark[3] if held is None else held
        new = (mark[0] + clock, max(mark[1], begun - RING), begun, held)
        tick(mark, new)
        return new

    pn_acc[0:8, 0:half] = prior_ref[...]
    pn_acc[0:8, half:width] = jnp.ones((8, half), F32)

    def hand_over(index, carry):
        rows = span(index)
        normed_ref[rows] = pn_acc[later(index)].astype(BF16)
        pn_swap(index).start()
        mixed_ref[rows] = out_acc[rows, other].astype(BF16)
        out_swap(index).start()
        for item in back_loads(index):
            item.start()
        return carry

    lax.fori_loop(0, steps, hand_over, 0)
    mark = move(mark, STEPS[0])
    first_load().start()
    gain_one, gain_two = gain_ref[0:1], gain_ref[1:2]
    taps = [tap_ref[k : k + 1] for k in range(3)]

    def right_of(place, piece):
        tall = pl.ds(0, total_rows)
        if place == 0:
            return gate_buf.at[piece, tall]
        if place == 1:
            return up_buf.at[piece, tall]
        if place == 2:
            return right_ref.at[piece]
        return mixed_ref.at[:, pl.ds(piece * UNIT, UNIT)]

    def first_pass(index):
        start = pl.multiple_of(index * step, step)
        rows = span(index)
        slot = index % 2
        resid_load(index).wait()
        for item in back_loads(index):
            item.wait()
        pn_swap(index).wait_recv()
        out_swap(index).wait_recv()

        @pl.when(index >= 2)
        def _():
            block_store(index - 2).wait()

        block_buf[slot] = (
            resid_buf[slot, :, own] + out_acc[rows, own] + out_recv[rows].astype(F32)
        ).astype(BF16)
        block_store(index).start()
        resid = resid_buf[slot]
        scale = inverse_rms(resid)
        unit = resid * scale
        grad = normed_ref[rows].astype(F32) + pn_recv[rows].astype(F32)
        sums_ref[0:1] += jnp.sum(grad * unit, axis=0, keepdims=True)
        grad = grad * gain_two
        mean = jnp.mean(grad * unit, axis=-1, keepdims=True)
        grad = cot_ref[rows].astype(F32) + scale * (grad - unit * mean)
        full_ref[...] = grad
        out_acc[rows, own] = full_ref[:, own]

        @pl.when(index + 2 < steps)
        def _():
            resid_load(index + 2).start()

        rounded = grad.astype(BF16)
        left_ref[1, :, :, rows] = rounded.T.reshape(plan.shards, plan.rows, step)
        grad_mixed = product_t(rounded, out_weight_ref[...])
        window = pn_acc[pl.ds(start, step + 8), 0:half] * pn_acc[pl.ds(start, step + 8), half:width]
        views = [window[6 + k : 6 + k + step] for k in range(3)]
        conv_out = taps[0] * views[0] + taps[1] * views[1] + taps[2] * views[2]
        grad_c = (grad_mixed * conv_out).astype(BF16)
        for piece in range(pieces):
            up_buf[piece, rows] = grad_c[:, piece * UNIT : (piece + 1) * UNIT]
        grad_conv = grad_mixed * out_acc[rows, other]
        out_acc[rows, other] = grad_conv
        for k in range(3):
            sums_ref[1 + k : 2 + k, 0:half] += jnp.sum(grad_conv * views[k], axis=0, keepdims=True)

        @pl.when((index == 0) & (seq > 0))
        def _():
            halo().start()

    mark = paced(mark, STEPS[1], first_pass)
    pl.semaphore_signal(
        free_sem.at[0], inc=1, device_id=plan.other_core(), device_id_type=MESH
    )
    for index in range(steps):
        out_swap(index).wait_send()
        pn_swap(index).wait_send()
    mixed_load().start()
    for item in in_weight_loads():
        item.start()
    first_load().wait()
    places = (1, 3, 0, 2)
    work = [(place, piece) for place in places for piece in range(pieces)]

    def produce(mark, count, stop):
        room = (mark[0], max(mark[1], early + stop - RING)) + mark[2:]
        tick(mark, room)
        for hold in (False, True):
            for index in range(count, stop):
                place, piece = work[index]
                unit = early + index
                call = plan.hold if hold else plan.begin
                call(unit, unit % 2, left_ref.at[int(place == 3)], right_of(place, piece))
            if not hold:
                room = move(room, STEPS[2], early + stop)
        return move(room, STEPS[2], None, early + stop)

    mark = produce(mark, 0, pieces)
    mixed_load().wait()
    mark = produce(mark, pieces, 2 * pieces)

    @pl.when(seq < last)
    def _():
        halo().wait_recv()

    @pl.when(seq == last)
    def _():
        out_acc[pl.ds(total_rows, 8), other] = jnp.zeros((8, half), F32)

    def second_pass(index):
        start = pl.multiple_of(index * step, step)
        rows = span(index)
        window = out_acc[pl.ds(start, step + 8), other]
        grad_gated = (
            taps[0] * window[2 : 2 + step]
            + taps[1] * window[1 : 1 + step]
            + taps[2] * window[0:step]
        )
        grad_b = (grad_gated * pn_acc[later(index), half:width]).astype(BF16)
        grad_x = (grad_gated * pn_acc[later(index), 0:half]).astype(BF16)
        for piece in range(pieces):
            columns = slice(piece * UNIT, (piece + 1) * UNIT)
            gate_buf[piece, rows] = grad_b[:, columns]
            right_ref[piece, rows] = grad_x[:, columns]

    mark = paced(mark, STEPS[3], second_pass)
    mark = produce(mark, 2 * pieces, 3 * pieces)
    mark = produce(mark, 3 * pieces, 4 * pieces)
    pl.semaphore_wait(free_sem.at[0], 1)
    for item in in_weight_loads():
        item.wait()

    def third_pass(index):
        rows = span(index)
        total = None
        for place in range(3):
            for piece in range(pieces):
                columns = pl.ds(piece * UNIT, UNIT)
                if place < 2:
                    weight = cot_ref[pl.ds(0, width), pl.ds(place * half + piece * UNIT, UNIT)]
                else:
                    weight = x_weight_ref[:, columns]
                term = product_t(right_of(place, piece)[rows], weight)
                total = term if total is None else total + term
        normed_ref[rows] = total.astype(BF16)
        part_swap(index).start()

    mark = paced(mark, STEPS[4], third_pass)

    def fourth_pass(index):
        rows = span(index)
        slot = index % 2
        part_swap(index).wait_recv()
        token_load(index).wait()
        value = token_buf[slot].astype(F32)
        scale = inverse_rms(value)
        unit = value * scale
        grad = normed_ref[rows].astype(F32) + pn_recv[rows].astype(F32)
        sums_ref[4:5] += jnp.sum(grad * unit, axis=0, keepdims=True)
        grad = grad * gain_one
        mean = jnp.mean(grad * unit, axis=-1, keepdims=True)
        full_ref[...] = scale * (grad - unit * mean)
        out_acc[rows, own] += full_ref[:, own]
        token_store(index).start()

        @pl.when(index + 2 < steps)
        def _():
            token_load(index + 2).start()

    mark = paced(mark, STEPS[5], fourth_pass)
    small_send[0] = jnp.zeros_like(small_ref)
    small_send[0, 0:3] = sums_ref[1:4, 0:half]
    small_send[0, 3:4] = sums_ref[4:5, own]
    small_send[0, 4:5] = sums_ref[0:1, own]
    small(0).start()
    mark = move(mark, STEPS[6])
    for bit in range(plan.bits):
        small(bit).wait_recv()
        total = small_send[bit] + small_recv[bit]
        if bit + 1 < plan.bits:
            small_send[bit + 1] = total
            small(bit + 1).start()
            mark = move(mark, STEPS[6])
        else:
            small_ref[...] = total
    rest = 0
    while limit(plan.bits, mark[0] + 3 * rest, 0, units) < units:
        rest += 1

    def drain(index, carry):
        clock = mark[0] + 3 * index
        tick((clock,) + mark[1:], (clock + 3,) + mark[1:])
        return carry

    lax.fori_loop(0, rest, drain, 0)
    for unit in range(units - RING, units):
        plan.copy(plan.order(unit % 2), unit, 0).wait_send()
    for bit in range(plan.bits):
        small(bit).wait_send()

    @pl.when(seq > 0)
    def _():
        halo().wait_send()

    for index in range(steps):
        part_swap(index).wait_send()
        token_store(index).wait()
    for index in range(max(0, steps - 2), steps):
        block_store(index).wait()


def main(plan, smalls, operands, hidden):
    total_rows, width = operands[0].shape
    half = width // 2
    step = min(256, total_rows)
    steps = total_rows // step
    tall = max(total_rows, width)
    units = (3 * hidden + 4 * half) // UNIT
    shape = jax.ShapeDtypeStruct
    dma = pltpu.SemaphoreType.DMA
    vmem = pltpu.VMEM
    assert total_rows >= width
    return pl.pallas_call(
        functools.partial(main_kernel, plan),
        name="main",
        out_shape=(
            shape((units, plan.rows, UNIT), F32),
            shape((8, half), F32),
            shape((total_rows, half), BF16),
            shape((total_rows, half), F32),
        ),
        in_specs=[whole()] * 3 + [anywhere()] * 15,
        out_specs=[whole()] * 2 + [anywhere()] * 2,
        scratch_shapes=[
            vmem((total_rows, width), BF16),
            vmem((total_rows, width), BF16),
            vmem((2, plan.shards, plan.rows, total_rows), BF16),
            vmem((2, tall, UNIT), BF16),
            vmem((2, tall, UNIT), BF16),
            vmem((2, UNIT, width), BF16),
            vmem((3, total_rows, UNIT), BF16),
            vmem((total_rows + 8, width), F32),
            vmem((total_rows + 8, width), F32),
            vmem((total_rows, half), BF16),
            vmem((total_rows, width), BF16),
            vmem((total_rows, half), BF16),
            vmem((half, width), BF16),
            vmem((width, half), BF16),
            vmem((2, step, width), F32),
            vmem((2, step, width), BF16),
            vmem((step, width), F32),
            vmem((2, step, half), BF16),
            vmem((8, width), F32),
            vmem((plan.bits, 8, half), F32),
            vmem((plan.bits, 8, half), F32),
            dma((3, 2)),
            dma((5, steps)),
            dma((7,)),
            dma((2,)),
            dma((2,)),
            dma((2,)),
            dma((steps,)),
            dma((steps,)),
            dma((steps,)),
            dma((steps,)),
            dma((steps,)),
            dma((steps,)),
            dma((steps,)),
            dma((1,)),
            dma((1,)),
            dma((plan.bits,)),
            dma((plan.bits,)),
            pltpu.SemaphoreType.REGULAR((1,)),
        ]
        + plan.scratch(units),
        compiler_params=pltpu.CompilerParams(
            collective_id=0, has_side_effects=True, vmem_limit_bytes=VMEM_BYTES
        ),
    )(*smalls, *operands)


def local(
    seq_size,
    shards,
    tokens,
    norm1_gain,
    in_weight,
    conv_weight,
    out_weight,
    norm2_gain,
    gate_weight,
    up_weight,
    down_weight,
    out_cotangent,
):
    seqs, length, width = tokens.shape
    assert seqs == 1
    half = in_weight.shape[2]
    total_rows = seqs * length
    chunk_rows = width // shards
    plan = Halving(seq_size, shards, chunk_rows)
    gains = jnp.stack([norm1_gain, norm2_gain])
    tokens = tokens.reshape(total_rows, width)
    normed_two, cotangent, left, resid, b_signal, c_signal, x_signal, mixed_in, first, prior = front(
        plan,
        gains,
        conv_weight,
        tokens,
        out_cotangent.reshape(total_rows, half),
        in_weight,
        out_weight,
    )
    hidden = gate_weight.shape[1]
    grads, small, block_out, tokens_grad = main(
        plan,
        (gains, conv_weight, prior),
        (
            normed_two,
            cotangent,
            left,
            gate_weight,
            up_weight,
            down_weight,
            out_weight,
            in_weight,
            first,
            mixed_in,
            resid,
            tokens,
            b_signal,
            c_signal,
            x_signal,
        ),
        hidden,
    )
    blocks, pieces = hidden // UNIT, half // UNIT
    late = grads[3 * blocks :].reshape(4, pieces, chunk_rows, UNIT)
    grads = grads[: 3 * blocks].reshape(blocks, 3, chunk_rows, UNIT)
    gate_grad = grads[:, 0].transpose(1, 0, 2).reshape(chunk_rows, hidden)
    up_grad = grads[:, 1].transpose(1, 0, 2).reshape(chunk_rows, hidden)
    down_grad = grads[:, 2].transpose(0, 2, 1).reshape(hidden, chunk_rows)
    in_grad = jnp.stack([late[2], late[0], late[3]]).transpose(0, 2, 1, 3)
    in_grad = in_grad.reshape(3, chunk_rows, half)
    out_grad = late[1].transpose(0, 2, 1).reshape(half, chunk_rows)
    conv_grad, norm1_grad, norm2_grad = small[0:3], small[3], small[4]
    block_out = block_out.reshape(seqs, length, half)
    tokens_grad = tokens_grad.reshape(seqs, length, half)
    return (
        block_out,
        tokens_grad,
        norm1_grad,
        in_grad,
        conv_grad,
        out_grad,
        norm2_grad,
        gate_grad,
        up_grad,
        down_grad,
    )


def solution(mesh):
    seq_size = mesh.shape["seq"]
    shards = mesh.shape["dp"] * seq_size
    return jax.shard_map(
        functools.partial(local, seq_size, shards),
        mesh=mesh,
        in_specs=(
            P("dp", "seq", None),
            P(),
            P(None, None, "tensor"),
            P(None, "tensor"),
            P("tensor", None),
            P(),
            P(None, "tensor"),
            P(None, "tensor"),
            P("tensor", None),
            P("dp", "seq", "tensor"),
        ),
        out_specs=(
            P("dp", "seq", "tensor"),
            P("dp", "seq", "tensor"),
            P("tensor"),
            P(None, ("dp", "seq"), "tensor"),
            P(None, "tensor"),
            P("tensor", ("dp", "seq")),
            P("tensor"),
            P(("dp", "seq"), "tensor"),
            P(("dp", "seq"), "tensor"),
            P("tensor", ("dp", "seq")),
        ),
        check_vma=False,
    )
```

time: 231 us -> 206 us (0.89)
  Pallas kernels: 214 us -> 191 us
  other arithmetic: 5.56 us -> 1.34 us
  local copies, waits for them, and re-layouts: 9.58 us -> 11.9 us
    pallas_call x2 -> x1, Pallas kernels: 193 us -> 171 us  [main(): pl.pallas_call(functools.partial(main_kernel, plan), name='main', out_sha...]
    reshape x1 -> x0, other arithmetic: 4.25 us -> none  [local(): block_out = (own_columns(resid, start, half) + out_own + out_other.astype...]
    unnamed x5 -> x10, local copies, waits for them, and re-layouts: 2.31 us -> 5.99 us
    transpose x2 -> x0, local copies, waits for them, and re-layouts: 2.81 us -> none  [the longest x1 1.57 us: local(): in_grad, out_grad = (mix_grads[0:3], mix_grads[3].T)]
where the time goes in v4:
time: 206 us; the launch traced here: 205 us
  Pallas kernels  191 us (93%)
  local copies, waits for them, and re-layouts  11.9 us (6%)
    pallas_call x1, Pallas kernels, main(): pl.pallas_call(functools.partial(main_kernel, plan), name='main', out_sha...  171 us
    pallas_call x1, Pallas kernels, front(): pl.pallas_call(functools.partial(front_kernel, plan), name='front', out_s...  20.5 us
    unnamed x10, local copies, waits for them, and re-layouts  5.99 us

profile of v4, /device:TPU:0, one launch (start us, length us, event | category | flops | bytes accessed | tf_op | source)
XLA Modules:
  0.0 205.3 jit_solution(16478184210274989727)
XLA Ops:
  0.6 1.3 pad_maximum_fusion.gain_ref
  2.0 20.5 %front.1 = (bf16[1024,1024]{1,0:T(8,128)(2,1)}, bf16[1024,1024]{1,0:T(8,128)(2,1)}, bf16[2,16,64,1024]{3,2,1,0:T(8,128)(2,1)}, f32[1024,1024]{1,0:T(8,128)}, f32...) custom-call(f32[2,1024]{1,0:T(2,128)} %pad_maximum_fusion.gain_ref, ...), custom_call_target="tpu_custom_call" | custom-call | tf_op jit(solution)/shard_map/front/pallas_call | solution.py:412
  22.5 170.8 %main.1 = (f32[35,64,256]{2,1,0:T(8,128)}, f32[8,512]{1,0:T(8,128)}, bf16[1024,512]{1,0:T(8,128)(2,1)}, f32[1024,512]{1,0:T(8,128)}) custom-call(f32[2,1024]{1,0:T(2,128)} %pad_maximum_fusion.gain_ref, f32[3,512]{1,0:T(4,128)} %tap_ref.3, f32[8,512]{1,0:T(8,128)} %get-tuple-element.24.prior_ref, bf16[1024,1024]{1,0:T(8,128)(2,1)} %get-tuple-element.25.normed_hbm, ...), custom_call_target="tpu_custom_call" | custom-call | tf_op jit(solution)/shard_map/main/pallas_call | solution.py:1032
  193.4 1.4 fusion.1
  194.7 1.3 slice.55
  196.1 1.1 slice_bitcast_fusion
  197.2 1.6 slice.58
  198.8 0.7 copy.32
  199.4 0.2 fusion
  199.6 0.9 copy.35
  200.5 0.0 copy-start.1
  200.5 0.9 copy.34
  201.4 0.0 copy-start
  201.4 0.8 copy.31
  202.2 0.9 copy.33
  203.0 0.0 copy-done.1
  203.0 1.0 copy.41
  204.0 0.0 copy-done
  204.0 1.3 copy.42
  (1 shorter events, 0.0 us)
Async XLA Ops:
  200.5 2.5 %copy-start.1 = (bf16[1024,512]{1,0:T(8,128)(2,1)S(1)}, bf16[1024,512]{1,0:T(8,128)(2,1)}, u32[]{:S(2)}) copy-start(bf16[1024,512]{1,0:T(8,128)(2,1)} %get-tuple-element.34) | copy-start | bytes 3145732
  201.4 2.6 %copy-start = (f32[1024,512]{1,0:T(8,128)S(1)}, f32[1024,512]{1,0:T(8,128)}, u32[]{:S(2)}) copy-start(f32[1024,512]{1,0:T(8,128)} %get-tuple-element.35) | copy-start | bytes 6291460

commit v5 on v4

--- a/solution.py
+++ b/solution.py
@@ -11,9 +11,10 @@
 MESH = pl.DeviceIdType.MESH
 UNIT = 256
 RING = 8
-PACE = (5, 28)
-LAGS = (-30, 9, 35, 65, 90)
-STEPS = (5, 7, 2, 3, 2, 4, 4)
+PACE = (5, 25)
+LATE_FIRST = 1
+LAGS = (-10, 9, 29, 47, 126)
+STEPS = (7, 7, 2, 1, 4, 4, 5)
 VMEM_BYTES = 67043328
 F32 = jnp.float32
 BF16 = jnp.bfloat16
@@ -180,7 +181,8 @@
 
 def front_kernel(
     plan,
-    gain_ref,
+    gain_one_ref,
+    gain_two_ref,
     tap_ref,
     token_hbm,
     cot_hbm,
@@ -275,7 +277,7 @@
         edge_copy().start()
 
     cot_swap.start()
-    gain_one, gain_two = gain_ref[0:1], gain_ref[1:2]
+    gain_one, gain_two = gain_one_ref[...], gain_two_ref[...]
     taps = [tap_ref[k : k + 1] for k in range(3)]
 
     def stores(index, pairs, first):
@@ -424,7 +426,7 @@
             shape(chunked, BF16),
             shape((8, half), F32),
         ),
-        in_specs=[whole()] * 2 + [anywhere()] * 4,
+        in_specs=[whole()] * 3 + [anywhere()] * 4,
         out_specs=[anywhere()] * 9 + [whole()],
         scratch_shapes=[
             pltpu.VMEM((total_rows, width), BF16),
@@ -457,7 +459,7 @@
         compiler_params=pltpu.CompilerParams(
             collective_id=2, has_side_effects=True, vmem_limit_bytes=VMEM_BYTES
         ),
-    )(gains, taps, tokens, cotangent, in_weight, out_weight)
+    )(*gains, taps, tokens, cotangent, in_weight, out_weight)
 
 
 def whole():
@@ -470,7 +472,8 @@
 
 def main_kernel(
     plan,
-    gain_ref,
+    gain_one_ref,
+    gain_two_ref,
     tap_ref,
     prior_ref,
     normed_hbm,
@@ -488,10 +491,11 @@
     b_hbm,
     c_hbm,
     x_hbm,
-    grads_ref,
     small_ref,
+    grads_hbm,
     block_hbm,
     tokens_hbm,
+    grads_ref,
     normed_ref,
     cot_ref,
     left_ref,
@@ -531,6 +535,7 @@
     small_send_sem,
     small_recv_sem,
     free_sem,
+    grads_sem,
     *refs,
 ):
     total_rows, width = normed_ref.shape
@@ -616,6 +621,9 @@
         rows = span(index)
         return local_copy(out_acc.at[rows, own], tokens_hbm.at[rows], store_sem.at[index])
 
+    def grads_store(unit):
+        return local_copy(grads_ref.at[unit], grads_hbm.at[unit], grads_sem.at[unit])
+
     def in_weight_loads():
         tall = pl.ds(0, width)
         return [
@@ -684,7 +692,7 @@
         return jnp.maximum(jnp.maximum(jnp.minimum(count, cap), floor), 0)
 
     def tick(before, after):
-        for stage in range(plan.bits + 1):
+        for stage in [0] + sorted(range(1, plan.bits + 1), reverse=bool(LATE_FIRST)):
             low = limit(stage, before[0], before[1], before[2 + (stage > 0)])
             high = limit(stage, after[0], after[1], after[2 + (stage > 0)])
             if isinstance(low, int) and isinstance(high, int) and low >= high:
@@ -697,6 +705,7 @@
                     plan.advance(unit, unit % 2, stage)
                 else:
                     grads_ref[unit] = plan.finish(unit, unit % 2)
+                    grads_store(unit).start()
                 return carry
 
             lax.fori_loop(low, high, advance, 0)
@@ -711,10 +720,10 @@
     for index in range(min(2, steps)):
         resid_load(index).start()
         token_load(index).start()
-    plan.greet((-1, 1))
     pn_acc[...] = jnp.zeros_like(pn_acc)
     out_acc[...] = jnp.zeros_like(out_acc)
     sums_ref[...] = jnp.zeros_like(sums_ref)
+    plan.greet((-1, 1))
 
     def block_step(index, carry):
         slot = index % 2
@@ -813,7 +822,7 @@
     lax.fori_loop(0, steps, hand_over, 0)
     mark = move(mark, STEPS[0])
     first_load().start()
-    gain_one, gain_two = gain_ref[0:1], gain_ref[1:2]
+    gain_one, gain_two = gain_one_ref[...], gain_two_ref[...]
     taps = [tap_ref[k : k + 1] for k in range(3)]
 
     def right_of(place, piece):
@@ -1004,6 +1013,8 @@
     lax.fori_loop(0, rest, drain, 0)
     for unit in range(units - RING, units):
         plan.copy(plan.order(unit % 2), unit, 0).wait_send()
+    for unit in range(units):
+        grads_store(unit).wait()
     for bit in range(plan.bits):
         small(bit).wait_send()
 
@@ -1033,14 +1044,15 @@
         functools.partial(main_kernel, plan),
         name="main",
         out_shape=(
+            shape((8, half), F32),
             shape((units, plan.rows, UNIT), F32),
-            shape((8, half), F32),
             shape((total_rows, half), BF16),
             shape((total_rows, half), F32),
         ),
-        in_specs=[whole()] * 3 + [anywhere()] * 15,
-        out_specs=[whole()] * 2 + [anywhere()] * 2,
+        in_specs=[whole()] * 4 + [anywhere()] * 15,
+        out_specs=[whole()] + [anywhere()] * 3,
         scratch_shapes=[
+            vmem((units, plan.rows, UNIT), F32),
             vmem((total_rows, width), BF16),
             vmem((total_rows, width), BF16),
             vmem((2, plan.shards, plan.rows, total_rows), BF16),
@@ -1080,12 +1092,108 @@
             dma((plan.bits,)),
             dma((plan.bits,)),
             pltpu.SemaphoreType.REGULAR((1,)),
+            dma((units,)),
         ]
         + plan.scratch(units),
         compiler_params=pltpu.CompilerParams(
             collective_id=0, has_side_effects=True, vmem_limit_bytes=VMEM_BYTES
         ),
     )(*smalls, *operands)
+
+
+def finish_kernel(
+    grads_in,
+    block_in,
+    tokens_in,
+    small_ref,
+    gate_hbm,
+    up_hbm,
+    down_hbm,
+    in_hbm,
+    out_hbm,
+    block_hbm,
+    tokens_hbm,
+    conv_ref,
+    one_ref,
+    two_ref,
+    grads_buf,
+    block_buf,
+    tokens_buf,
+    load_sem,
+    store_sem,
+):
+    hidden, half = gate_hbm.shape[1], out_hbm.shape[1]
+    blocks, pieces = hidden // UNIT, half // UNIT
+    early = 3 * blocks
+    total_rows = block_buf.shape[0]
+    step = min(256, total_rows)
+    moves = []
+
+    def move(source, buf, target):
+        index = len(moves)
+        moves.append(
+            (
+                pltpu.make_async_copy(source, buf, load_sem.at[index]),
+                pltpu.make_async_copy(buf, target, store_sem.at[index]),
+            )
+        )
+        moves[-1][0].start()
+
+    for index in range(total_rows // step):
+        part = pl.ds(index * step, step)
+        move(tokens_in.at[part], tokens_buf.at[part], tokens_hbm.at[part])
+        move(block_in.at[part], block_buf.at[part], block_hbm.at[part])
+    for block in range(blocks):
+        columns = pl.ds(block * UNIT, UNIT)
+        for place, target in enumerate((gate_hbm, up_hbm, down_hbm)):
+            unit = 3 * block + place
+            move(grads_in.at[unit], grads_buf.at[unit], target.at[:, columns])
+    for index, place in enumerate((1, 3, 0, 2)):
+        for piece in range(pieces):
+            unit = early + index * pieces + piece
+            columns = pl.ds(piece * UNIT, UNIT)
+            target = out_hbm if place == 3 else in_hbm.at[place]
+            move(grads_in.at[unit], grads_buf.at[unit], target.at[:, columns])
+    conv_ref[...] = small_ref[0:3]
+    one_ref[...] = small_ref[3:4]
+    two_ref[...] = small_ref[4:5]
+    for load, store in moves:
+        load.wait()
+        store.start()
+    for load, store in moves:
+        store.wait()
+
+
+def finish(rows, hidden, grads, small, block_out, tokens_grad):
+    total_rows, half = block_out.shape
+    shape = jax.ShapeDtypeStruct
+    moves = 2 * (total_rows // min(256, total_rows)) + grads.shape[0]
+    return pl.pallas_call(
+        finish_kernel,
+        name="finish",
+        out_shape=(
+            shape((rows, hidden), F32),
+            shape((rows, hidden), F32),
+            shape((rows, hidden), F32),
+            shape((3, rows, half), F32),
+            shape((rows, half), F32),
+            shape((total_rows, half), BF16),
+            shape((total_rows, half), F32),
+            shape((3, half), F32),
+            shape((1, half), F32),
+            shape((1, half), F32),
+        ),
+        in_specs=[anywhere()] * 3 + [whole()],
+        out_specs=[anywhere()] * 7 + [whole()] * 3,
+        scratch_shapes=[
+            pltpu.VMEM(grads.shape, F32),
+            pltpu.VMEM((total_rows, half), BF16),
+            pltpu.VMEM((total_rows, half), F32),
+            pltpu.SemaphoreType.DMA((moves,)),
+            pltpu.SemaphoreType.DMA((moves,)),
+        ],
+        compiler_params=pltpu.CompilerParams(vmem_limit_bytes=VMEM_BYTES),
+    )(grads, block_out, tokens_grad, small)
 
 
 def local(
@@ -1108,7 +1216,7 @@
     total_rows = seqs * length
     chunk_rows = width // shards
     plan = Halving(seq_size, shards, chunk_rows)
-    gains = jnp.stack([norm1_gain, norm2_gain])
+    gains = (norm1_gain.reshape(1, width), norm2_gain.reshape(1, width))
     tokens = tokens.reshape(total_rows, width)
     normed_two, cotangent, left, resid, b_signal, c_signal, x_signal, mixed_in, first, prior = front(
         plan,
@@ -1120,9 +1228,9 @@
         out_weight,
     )
     hidden = gate_weight.shape[1]
-    grads, small, block_out, tokens_grad = main(
+    small, grads, block_out, tokens_grad = main(
         plan,
-        (gains, conv_weight, prior),
+        (*gains, conv_weight, prior),
         (
             normed_two,
             cotangent,
@@ -1142,16 +1250,20 @@
         ),
         hidden,
     )
-    blocks, pieces = hidden // UNIT, half // UNIT
-    late = grads[3 * blocks :].reshape(4, pieces, chunk_rows, UNIT)
-    grads = grads[: 3 * blocks].reshape(blocks, 3, chunk_rows, UNIT)
-    gate_grad = grads[:, 0].transpose(1, 0, 2).reshape(chunk_rows, hidden)
-    up_grad = grads[:, 1].transpose(1, 0, 2).reshape(chunk_rows, hidden)
-    down_grad = grads[:, 2].transpose(0, 2, 1).reshape(hidden, chunk_rows)
-    in_grad = jnp.stack([late[2], late[0], late[3]]).transpose(0, 2, 1, 3)
-    in_grad = in_grad.reshape(3, chunk_rows, half)
-    out_grad = late[1].transpose(0, 2, 1).reshape(half, chunk_rows)
-    conv_grad, norm1_grad, norm2_grad = small[0:3], small[3], small[4]
+    (
+        gate_grad,
+        up_grad,
+        down_grad,
+        in_grad,
+        out_grad,
+        block_out,
+        tokens_grad,
+        conv_grad,
+        norm1_grad,
+        norm2_grad,
+    ) = finish(chunk_rows, hidden, grads, small, block_out, tokens_grad)
+    norm1_grad, norm2_grad = norm1_grad[0], norm2_grad[0]
+    down_grad, out_grad = down_grad.T, out_grad.T
     block_out = block_out.reshape(seqs, length, half)
     tokens_grad = tokens_grad.reshape(seqs, length, half)
     return (

time: 206 us -> 191 us (0.927)
  local copies, waits for them, and re-layouts: 11.9 us -> 0 us
    pallas_call x1, Pallas kernels: 171 us -> 163 us  [main(): pl.pallas_call(functools.partial(main_kernel, plan), name='main', out_sha...]
    pallas_call x0 -> x1, Pallas kernels: none -> 6.59 us  [finish(): pl.pallas_call(finish_kernel, name='finish', out_shape=(shape((rows, hidd...]
    unnamed x10 -> x0, local copies, waits for them, and re-layouts: 5.99 us -> none
    slice x4 -> x0, local copies, waits for them, and re-layouts: 4.46 us -> none  [the longest x2 2.7 us: local(): conv_grad, norm1_grad, norm2_grad = (small[0:3], small[3], small[4])]
where the time goes in v5:
time: 191 us
  Pallas kernels  190 us (99%)
    pallas_call x1, Pallas kernels, main(): pl.pallas_call(functools.partial(main_kernel, plan), name='main', out_sha...  163 us
    pallas_call x1, Pallas kernels, front(): pl.pallas_call(functools.partial(front_kernel, plan), name='front', out_s...  20.5 us
    pallas_call x1, Pallas kernels, finish(): pl.pallas_call(finish_kernel, name='finish', out_shape=(shape((rows, hidd...  6.59 us

profile of v5, /device:TPU:0, one launch (start us, length us, event | category | flops | bytes accessed | tf_op | source)
XLA Modules:
  0.0 190.6 jit_solution(6360345226852240630)
XLA Ops:
  0.6 20.5 %front.1 = (bf16[1024,1024]{1,0:T(8,128)(2,1)}, bf16[1024,1024]{1,0:T(8,128)(2,1)}, bf16[2,16,64,1024]{3,2,1,0:T(8,128)(2,1)}, f32[1024,1024]{1,0:T(8,128)}, f32...) custom-call(f32[1,1024]{1,0:T(1,128)} %bitcast.13, ...), custom_call_target="tpu_custom_call" | custom-call | tf_op jit(solution)/shard_map/front/pallas_call | solution.py:414
  21.2 162.7 %main.1 = (f32[8,512]{1,0:T(8,128)}, f32[35,64,256]{2,1,0:T(8,128)}, bf16[1024,512]{1,0:T(8,128)(2,1)}, f32[1024,512]{1,0:T(8,128)}) custom-call(f32[1,1024]{1,0:T(1,128)} %bitcast.14, f32[1,1024]{1,0:T(1,128)} %bitcast.16, f32[3,512]{1,0:T(4,128)} %tap_ref.3, f32[8,512]{1,0:T(8,128)} %get-tuple-element.34.prior_ref, ...), custom_call_target="tpu_custom_call" | custom-call | tf_op jit(solution)/shard_map/main/pallas_call | solution.py:1043
  183.9 6.6 %finish.1 = (f32[64,2304]{1,0:T(8,128)}, f32[64,2304]{1,0:T(8,128)}, f32[64,2304]{1,0:T(8,128)}, f32[3,64,512]{2,1,0:T(8,128)}, f32[64,512]{1,0:T(8,128)}, /*ind...) custom-call(f32[35,64,256]{2,1,0:T(8,128)} %get-tuple-element.44.grad, ...), custom_call_target="tpu_custom_call" | custom-call | tf_op jit(solution)/shard_map/finish/pallas_call | solution.py:1171

commit v6 on v5

--- a/solution.py
+++ b/solution.py
@@ -59,11 +59,10 @@
         seq = (self.me + steps) % self.seq_size
         return (self.me // self.seq_size, seq, self.core)
 
-    def greet(self, steps=(), shards=True):
+    def greet(self, steps):
         barrier = pltpu.get_barrier_semaphore()
         partners = [self.other_core()]
-        if shards:
-            partners += [self.place(self.flipped(1 << bit)) for bit in range(self.bits)]
+        partners += [self.place(self.flipped(1 << bit)) for bit in range(self.bits)]
         partners.extend(self.along_seq(count) for count in steps)
         for partner in partners:
             pl.semaphore_signal(barrier, inc=1, device_id=partner, device_id_type=MESH)
@@ -179,322 +178,37 @@
         return total
 
 
-def front_kernel(
+def whole():
+    return pl.BlockSpec(memory_space=pltpu.VMEM)
+
+
+def anywhere():
+    return pl.BlockSpec(memory_space=pl.ANY)
+
+
+def main_kernel(
     plan,
     gain_one_ref,
     gain_two_ref,
     tap_ref,
     token_hbm,
     cot_hbm,
+    gate_hbm,
+    up_hbm,
+    down_hbm,
+    out_weight_hbm,
     in_weight_hbm,
-    out_weight_hbm,
-    normed_hbm,
-    cot_full_hbm,
-    left_hbm,
+    small_ref,
+    grads_hbm,
+    block_hbm,
+    tokens_hbm,
     resid_hbm,
     b_hbm,
     c_hbm,
     x_hbm,
     mixed_hbm,
-    first_hbm,
+    edge_ref,
     prior_ref,
-    normed_ref,
-    cot_ref,
-    left_ref,
-    token_ref,
-    edge_ref,
-    in_weight_ref,
-    out_weight_ref,
-    b_ref,
-    c_ref,
-    x_ref,
-    gated_ref,
-    mixed_ref,
-    first_ref,
-    resid_ref,
-    part_ref,
-    part_recv,
-    token_sem,
-    weight_sem,
-    cot_sem,
-    cot_send,
-    cot_recv,
-    edge_send,
-    edge_recv,
-    swap_send,
-    swap_recv,
-    store_sem,
-):
-    total_rows, width = token_ref.shape
-    half = width // 2
-    step = min(256, total_rows)
-    steps = total_rows // step
-    edge = edge_ref.shape[0]
-    plan.enter()
-    seq = lax.axis_index("seq")
-    last = plan.seq_size - 1
-
-    def span(index):
-        return pl.ds(pl.multiple_of(index * step, step), step)
-
-    def load(index):
-        rows = span(index)
-        return pltpu.make_async_copy(token_hbm.at[rows], token_ref.at[rows], token_sem.at[index])
-
-    own = pl.ds(pl.multiple_of(plan.core * half, half), half)
-    for index in range(steps):
-        load(index).start()
-    weights = [
-        pltpu.make_async_copy(in_weight_hbm, in_weight_ref, weight_sem.at[0]),
-        pltpu.make_async_copy(out_weight_hbm, out_weight_ref, weight_sem.at[1]),
-    ]
-    for item in weights:
-        item.start()
-    cot_own = pltpu.make_async_copy(cot_hbm, cot_ref.at[:, own], cot_sem.at[0])
-    cot_own.start()
-    plan.greet((-1, 1), shards=False)
-    cot_swap = pltpu.make_async_remote_copy(
-        src_ref=cot_hbm,
-        dst_ref=cot_ref.at[:, own],
-        send_sem=cot_send.at[0],
-        recv_sem=cot_recv.at[0],
-        device_id=plan.other_core(),
-        device_id_type=MESH,
-    )
-
-    def edge_copy():
-        return pltpu.make_async_remote_copy(
-            src_ref=token_hbm.at[pl.ds(total_rows - edge, edge)],
-            dst_ref=edge_ref,
-            send_sem=edge_send.at[0],
-            recv_sem=edge_recv.at[0],
-            device_id=plan.along_seq(1),
-            device_id_type=MESH,
-        )
-
-    @pl.when(seq < last)
-    def _():
-        edge_copy().start()
-
-    cot_swap.start()
-    gain_one, gain_two = gain_one_ref[...], gain_two_ref[...]
-    taps = [tap_ref[k : k + 1] for k in range(3)]
-
-    def stores(index, pairs, first):
-        return [
-            pltpu.make_async_copy(source, target, store_sem.at[first + place, index])
-            for place, (source, target) in enumerate(pairs)
-        ]
-
-    def early_stores(index):
-        rows = span(index)
-        return stores(
-            index,
-            (
-                (b_ref.at[rows], b_hbm.at[rows]),
-                (c_ref.at[rows], c_hbm.at[rows]),
-                (x_ref.at[rows], x_hbm.at[rows]),
-                (first_ref.at[:, :, rows], first_hbm.at[:, :, rows]),
-            ),
-            0,
-        )
-
-    def late_stores(index):
-        rows = span(index)
-        return stores(
-            index,
-            (
-                (mixed_ref.at[rows], mixed_hbm.at[rows]),
-                (resid_ref.at[rows], resid_hbm.at[rows]),
-                (normed_ref.at[rows], normed_hbm.at[rows]),
-                (cot_ref.at[rows], cot_full_hbm.at[rows]),
-                (left_ref.at[:, :, :, rows], left_hbm.at[:, :, :, rows]),
-            ),
-            4,
-        )
-
-    def normalise(value, gain):
-        return (value * inverse_rms(value) * gain).astype(BF16)
-
-    weights[0].wait()
-
-    def first_pass(index, carry):
-        start = pl.multiple_of(index * step, step)
-        rows = pl.ds(start, step)
-        load(index).wait()
-        normed = normalise(token_ref[rows].astype(F32), gain_one)
-        b_signal = product(normed, in_weight_ref[0])
-        x_signal = product(normed, in_weight_ref[2])
-        b_ref[rows] = b_signal
-        x_ref[rows] = x_signal
-        gated_ref[pl.ds(start + 8, step)] = b_signal * x_signal
-        c_ref[rows] = product(normed, in_weight_ref[1])
-        first_ref[:, :, rows] = normed.T.reshape(plan.shards, plan.rows, step)
-        for item in early_stores(index):
-            item.start()
-        return carry
-
-    lax.fori_loop(0, steps, first_pass, 0)
-
-    @pl.when(seq > 0)
-    def _():
-        edge_copy().wait_recv()
-
-    @pl.when(seq == 0)
-    def _():
-        edge_ref[...] = jnp.zeros_like(edge_ref)
-
-    normed = normalise(edge_ref[...].astype(F32), gain_one)
-    gated = product(normed, in_weight_ref[0]) * product(normed, in_weight_ref[2])
-    gated_ref[0:8] = gated[edge - 8 : edge]
-    prior_ref[...] = gated[edge - 8 : edge]
-    weights[1].wait()
-
-    def swap(index):
-        rows = span(index)
-        return pltpu.make_async_remote_copy(
-            src_ref=part_ref.at[rows],
-            dst_ref=part_recv.at[rows],
-            send_sem=swap_send.at[index],
-            recv_sem=swap_recv.at[index],
-            device_id=plan.other_core(),
-            device_id_type=MESH,
-        )
-
-    def second_pass(index, carry):
-        start = pl.multiple_of(index * step, step)
-        rows = pl.ds(start, step)
-        window = gated_ref[pl.ds(start, step + 8)]
-        views = [window[6 + k : 6 + k + step] for k in range(3)]
-        conv_out = taps[0] * views[0] + taps[1] * views[1] + taps[2] * views[2]
-        mixed = (c_ref[rows] * conv_out).astype(BF16)
-        mixed_ref[rows] = mixed
-        part = product(mixed, out_weight_ref[...])
-        part_ref[rows] = part.astype(BF16)
-        swap(index).start()
-        resid_ref[rows] = token_ref[rows].astype(F32) + part
-        return carry
-
-    lax.fori_loop(0, steps, second_pass, 0)
-    cot_own.wait()
-    cot_swap.wait_recv()
-
-    def third_pass(index, carry):
-        rows = span(index)
-        swap(index).wait_recv()
-        resid = resid_ref[rows] + part_recv[rows].astype(F32)
-        resid_ref[rows] = resid
-        normed = normalise(resid, gain_two)
-        normed_ref[rows] = normed
-        left_ref[0, :, :, rows] = normed.T.reshape(plan.shards, plan.rows, step)
-        left_ref[1, :, :, rows] = cot_ref[rows].T.reshape(plan.shards, plan.rows, step)
-        for item in late_stores(index):
-            item.start()
-        return carry
-
-    lax.fori_loop(0, steps, third_pass, 0)
-    for index in range(steps):
-        for item in early_stores(index) + late_stores(index):
-            item.wait()
-        swap(index).wait_send()
-    cot_swap.wait_send()
-
-    @pl.when(seq < last)
-    def _():
-        edge_copy().wait_send()
-
-
-def front(plan, gains, taps, tokens, cotangent, in_weight, out_weight):
-    total_rows, width = tokens.shape
-    half = in_weight.shape[2]
-    steps = total_rows // min(256, total_rows)
-    shape = jax.ShapeDtypeStruct
-    dma = pltpu.SemaphoreType.DMA
-    chunked = (plan.shards, plan.rows, total_rows)
-    return pl.pallas_call(
-        functools.partial(front_kernel, plan),
-        name="front",
-        out_shape=(
-            shape((total_rows, width), BF16),
-            shape((total_rows, width), BF16),
-            shape((2,) + chunked, BF16),
-            shape((total_rows, width), F32),
-            shape((total_rows, half), F32),
-            shape((total_rows, half), F32),
-            shape((total_rows, half), F32),
-            shape((total_rows, half), BF16),
-            shape(chunked, BF16),
-            shape((8, half), F32),
-        ),
-        in_specs=[whole()] * 3 + [anywhere()] * 4,
-        out_specs=[anywhere()] * 9 + [whole()],
-        scratch_shapes=[
-            pltpu.VMEM((total_rows, width), BF16),
-            pltpu.VMEM((total_rows, width), BF16),
-            pltpu.VMEM((2,) + chunked, BF16),
-            pltpu.VMEM((total_rows, width), BF16),
-            pltpu.VMEM((16, width), BF16),
-            pltpu.VMEM((3, width, half), BF16),
-            pltpu.VMEM((half, width), BF16),
-            pltpu.VMEM((total_rows, half), F32),
-            pltpu.VMEM((total_rows, half), F32),
-            pltpu.VMEM((total_rows, half), F32),
-            pltpu.VMEM((total_rows + 8, half), F32),
-            pltpu.VMEM((total_rows, half), BF16),
-            pltpu.VMEM(chunked, BF16),
-            pltpu.VMEM((total_rows, width), F32),
-            pltpu.VMEM((total_rows, width), BF16),
-            pltpu.VMEM((total_rows, width), BF16),
-            dma((steps,)),
-            dma((2,)),
-            dma((1,)),
-            dma((1,)),
-            dma((1,)),
-            dma((1,)),
-            dma((1,)),
-            dma((steps,)),
-            dma((steps,)),
-            dma((9, steps)),
-        ],
-        compiler_params=pltpu.CompilerParams(
-            collective_id=2, has_side_effects=True, vmem_limit_bytes=VMEM_BYTES
-        ),
-    )(*gains, taps, tokens, cotangent, in_weight, out_weight)
-
-
-def whole():
-    return pl.BlockSpec(memory_space=pltpu.VMEM)
-
-
-def anywhere():
-    return pl.BlockSpec(memory_space=pl.ANY)
-
-
-def main_kernel(
-    plan,
-    gain_one_ref,
-    gain_two_ref,
-    tap_ref,
-    prior_ref,
-    normed_hbm,
-    cot_hbm,
-    left_hbm,
-    gate_hbm,
-    up_hbm,
-    down_hbm,
-    out_weight_hbm,
-    in_weight_hbm,
-    first_hbm,
-    mixed_hbm,
-    resid_hbm,
-    token_hbm,
-    b_hbm,
-    c_hbm,
-    x_hbm,
-    small_ref,
-    grads_hbm,
-    block_hbm,
-    tokens_hbm,
     grads_ref,
     normed_ref,
     cot_ref,
@@ -536,6 +250,12 @@
     small_recv_sem,
     free_sem,
     grads_sem,
+    front_sem,
+    cot_sem,
+    edge_send,
+    edge_recv,
+    first_send_sem,
+    first_recv_sem,
     *refs,
 ):
     total_rows, width = normed_ref.shape
@@ -582,19 +302,61 @@
             local_copy(down_hbm.at[columns], down_buf.at[slot], weight_sem.at[2, slot]),
         ]
 
-    def rows_loads(index):
-        rows = span(index)
+    def front_loads():
+        tall = pl.ds(0, width)
+        pairs = [(in_weight_hbm.at[2], x_weight_ref), (out_weight_hbm, out_weight_ref)]
+        for piece in range(pieces):
+            columns = pl.ds(piece * UNIT, UNIT)
+            pairs.append((in_weight_hbm.at[0, :, columns], gate_buf.at[piece, tall]))
+            pairs.append((in_weight_hbm.at[1, :, columns], up_buf.at[piece, tall]))
+        pairs.append((cot_hbm, cot_ref.at[:, own]))
         return [
-            local_copy(normed_hbm.at[rows], normed_ref.at[rows], load_sem.at[0, index]),
-            local_copy(cot_hbm.at[rows], cot_ref.at[rows], load_sem.at[1, index]),
+            local_copy(source, target, front_sem.at[place])
+            for place, (source, target) in enumerate(pairs)
         ]
 
-    def side_loads():
+    def c_place(index):
+        columns = pl.ds(pl.multiple_of((index % 2) * half, half), half)
+        return resid_buf.at[index // 2, :, columns]
+
+    def early_stores(index):
+        rows = span(index)
+        low, high = pl.ds(0, half), pl.ds(half, half)
         return [
-            local_copy(left_hbm, left_ref, late_sem.at[0]),
-            local_copy(out_weight_hbm, out_weight_ref, late_sem.at[1]),
-            local_copy(in_weight_hbm.at[2], x_weight_ref, late_sem.at[2]),
+            local_copy(pn_acc.at[later(index), low], b_hbm.at[rows], load_sem.at[0, index]),
+            local_copy(pn_acc.at[later(index), high], x_hbm.at[rows], load_sem.at[1, index]),
+            local_copy(c_place(index), c_hbm.at[rows], load_sem.at[5, index]),
         ]
+
+    def mixed_store(index):
+        rows = span(index)
+        return local_copy(mixed_ref.at[rows], mixed_hbm.at[rows], load_sem.at[6, index])
+
+    def resid_store(index):
+        rows = span(index)
+        return local_copy(out_acc.at[rows], resid_hbm.at[rows], load_sem.at[7, index])
+
+    def cot_swap():
+        return core_copy(cot_hbm, cot_ref.at[:, own], cot_sem.at[0], cot_sem.at[1])
+
+    def first_swap(index):
+        rows = span(index)
+        return core_copy(
+            normed_ref.at[rows],
+            pn_recv.at[rows],
+            first_send_sem.at[index],
+            first_recv_sem.at[index],
+        )
+
+    def edge_copy():
+        return pltpu.make_async_remote_copy(
+            src_ref=token_hbm.at[pl.ds(total_rows - edge_ref.shape[0], edge_ref.shape[0])],
+            dst_ref=edge_ref,
+            send_sem=edge_send.at[0],
+            recv_sem=edge_recv.at[0],
+            device_id=plan.along_seq(1),
+            device_id_type=MESH,
+        )
 
     def back_loads(index):
         rows = span(index)
@@ -630,16 +392,13 @@
             local_copy(
                 in_weight_hbm.at[place],
                 cot_ref.at[tall, pl.ds(place * half, half)],
-                late_sem.at[3 + place],
+                late_sem.at[place],
             )
             for place in range(2)
         ]
 
-    def first_load():
-        return local_copy(first_hbm, left_ref.at[0], late_sem.at[5])
-
     def mixed_load():
-        return local_copy(mixed_hbm, mixed_ref, late_sem.at[6])
+        return local_copy(mixed_hbm, mixed_ref, late_sem.at[2])
 
     def pn_swap(index):
         rows = span(index)
@@ -710,20 +469,117 @@
 
             lax.fori_loop(low, high, advance, 0)
 
+    def normalise(value, gain):
+        return (value * inverse_rms(value) * gain).astype(BF16)
+
+    def chunked(value):
+        return value.T.reshape(plan.shards, plan.rows, step)
+
+    gain_one, gain_two = gain_one_ref[...], gain_two_ref[...]
+    taps = [tap_ref[k : k + 1] for k in range(3)]
+
+    def start_tokens():
+        for index in range(min(2, steps)):
+            token_load(index).start()
+
+    def next_tokens(index):
+        @pl.when(index + 2 < steps)
+        def _():
+            token_load(index + 2).start()
+
+    start_tokens()
+    for item in front_loads():
+        item.start()
+    sums_ref[...] = jnp.zeros_like(sums_ref)
+    plan.greet((-1, 1))
+
+    @pl.when(seq < last)
+    def _():
+        edge_copy().start()
+
+    cot_swap().start()
+    for item in front_loads():
+        item.wait()
+
+    def project(index, carry):
+        rows = span(index)
+        slot = index % 2
+        token_load(index).wait()
+        value = token_buf[slot].astype(F32)
+        out_acc[rows] = value
+        normed = normalise(value, gain_one)
+        next_tokens(index)
+        for piece in range(pieces):
+            columns = pl.ds(piece * UNIT, UNIT)
+            pn_acc[later(index), columns] = product(normed, gate_buf[piece, 0:width])
+            pn_acc[later(index), pl.ds(half + piece * UNIT, UNIT)] = product(
+                normed, x_weight_ref[:, columns]
+            )
+            place = pl.ds(pl.multiple_of((index % 2) * half + piece * UNIT, UNIT), UNIT)
+            resid_buf[index // 2, :, place] = product(normed, up_buf[piece, 0:width])
+        for item in early_stores(index):
+            item.start()
+        return carry
+
+    lax.fori_loop(0, steps, project, 0)
+    start_tokens()
+
+    @pl.when(seq > 0)
+    def _():
+        edge_copy().wait_recv()
+
+    @pl.when(seq == 0)
+    def _():
+        edge_ref[...] = jnp.zeros_like(edge_ref)
+
+    normed = normalise(edge_ref[...].astype(F32), gain_one)
+    edge = edge_ref.shape[0]
+    for piece in range(pieces):
+        columns = pl.ds(piece * UNIT, UNIT)
+        gated = product(normed, gate_buf[piece, 0:width]) * product(
+            normed, x_weight_ref[:, columns]
+        )
+        prior_ref[:, columns] = gated[edge - 8 : edge]
     for item in weights(0):
         item.start()
-    for index in range(steps):
-        for item in rows_loads(index):
-            item.start()
-    for item in side_loads():
-        item.start()
-    for index in range(min(2, steps)):
-        resid_load(index).start()
-        token_load(index).start()
-    pn_acc[...] = jnp.zeros_like(pn_acc)
-    out_acc[...] = jnp.zeros_like(out_acc)
-    sums_ref[...] = jnp.zeros_like(sums_ref)
-    plan.greet((-1, 1))
+    pn_acc[0:8, 0:half] = prior_ref[...]
+    pn_acc[0:8, half:width] = jnp.ones((8, half), F32)
+
+    def convolve(index, carry):
+        start = pl.multiple_of(index * step, step)
+        rows = span(index)
+        window = pn_acc[pl.ds(start, step + 8), 0:half] * pn_acc[pl.ds(start, step + 8), half:width]
+        views = [window[6 + k : 6 + k + step] for k in range(3)]
+        conv_out = taps[0] * views[0] + taps[1] * views[1] + taps[2] * views[2]
+        mixed = (c_place(index)[...] * conv_out).astype(BF16)
+        mixed_ref[rows] = mixed
+        part = product(mixed, out_weight_ref[...])
+        normed_ref[rows] = part.astype(BF16)
+        first_swap(index).start()
+        out_acc[rows] += part
+        mixed_store(index).start()
+        return carry
+
+    lax.fori_loop(0, steps, convolve, 0)
+    cot_swap().wait_recv()
+
+    def settle(index, carry):
+        rows = span(index)
+        first_swap(index).wait_recv()
+        first_swap(index).wait_send()
+        resid = out_acc[rows] + pn_recv[rows].astype(F32)
+        out_acc[rows] = resid
+        normed = normalise(resid, gain_two)
+        normed_ref[rows] = normed
+        resid_store(index).start()
+        left_ref[0, :, :, rows] = chunked(normed)
+        left_ref[1, :, :, rows] = chunked(cot_ref[rows])
+        return carry
+
+    lax.fori_loop(0, steps, settle, 0)
+    pl.semaphore_signal(
+        free_sem.at[0], inc=1, device_id=plan.other_core(), device_id_type=MESH
+    )
 
     def block_step(index, carry):
         slot = index % 2
@@ -737,12 +593,6 @@
             item.wait()
         for place in range(steps):
             rows = pl.ds(place * step, step)
-
-            @pl.when(index == 0)
-            def _(place=place):
-                for item in rows_loads(place):
-                    item.wait()
-
             normed = normed_ref[rows]
             gate_pre = product(normed, gate_buf[slot, 0:width])
             up_pre = product(normed, up_buf[slot, 0:width])
@@ -754,11 +604,6 @@
             ).astype(BF16)
             right_ref[1, rows] = (grad_hidden * active).astype(BF16)
             right_ref[2, rows] = (active * up_pre).astype(BF16)
-
-        @pl.when(index == 0)
-        def _():
-            for item in side_loads():
-                item.wait()
 
         start, stop = index * 3, index * 3 + 3
         marks = [
@@ -773,6 +618,17 @@
             unit = index * 3 + place
             plan.begin(unit, unit % 2, left_ref.at[place // 2], right_ref.at[place])
         tick(marks[1], marks[2])
+
+        @pl.when(index == 0)
+        def _():
+            for place in range(steps):
+                for item in early_stores(place) + [mixed_store(place), resid_store(place)]:
+                    item.wait()
+            for place in range(min(2, steps)):
+                resid_load(place).start()
+            pn_acc[...] = jnp.zeros_like(pn_acc)
+            out_acc[0:total_rows] = jnp.zeros((total_rows, width), F32)
+
         for place in range(steps):
             rows = pl.ds(place * step, step)
             pn_acc[pl.ds(place * step + 8, step)] += product_t(
@@ -809,6 +665,8 @@
     pn_acc[0:8, 0:half] = prior_ref[...]
     pn_acc[0:8, half:width] = jnp.ones((8, half), F32)
 
+    pl.semaphore_wait(free_sem.at[0], 1)
+
     def hand_over(index, carry):
         rows = span(index)
         normed_ref[rows] = pn_acc[later(index)].astype(BF16)
@@ -821,9 +679,6 @@
 
     lax.fori_loop(0, steps, hand_over, 0)
     mark = move(mark, STEPS[0])
-    first_load().start()
-    gain_one, gain_two = gain_one_ref[...], gain_two_ref[...]
-    taps = [tap_ref[k : k + 1] for k in range(3)]
 
     def right_of(place, piece):
         tall = pl.ds(0, total_rows)
@@ -869,7 +724,10 @@
             resid_load(index + 2).start()
 
         rounded = grad.astype(BF16)
-        left_ref[1, :, :, rows] = rounded.T.reshape(plan.shards, plan.rows, step)
+        left_ref[1, :, :, rows] = chunked(rounded)
+        token_load(index).wait()
+        left_ref[0, :, :, rows] = chunked(normalise(token_buf[slot].astype(F32), gain_one))
+        next_tokens(index)
         grad_mixed = product_t(rounded, out_weight_ref[...])
         window = pn_acc[pl.ds(start, step + 8), 0:half] * pn_acc[pl.ds(start, step + 8), half:width]
         views = [window[6 + k : 6 + k + step] for k in range(3)]
@@ -887,8 +745,9 @@
             halo().start()
 
     mark = paced(mark, STEPS[1], first_pass)
+    start_tokens()
     pl.semaphore_signal(
-        free_sem.at[0], inc=1, device_id=plan.other_core(), device_id_type=MESH
+        free_sem.at[1], inc=1, device_id=plan.other_core(), device_id_type=MESH
     )
     for index in range(steps):
         out_swap(index).wait_send()
@@ -896,7 +755,6 @@
     mixed_load().start()
     for item in in_weight_loads():
         item.start()
-    first_load().wait()
     places = (1, 3, 0, 2)
     work = [(place, piece) for place in places for piece in range(pieces)]
 
@@ -944,7 +802,7 @@
     mark = paced(mark, STEPS[3], second_pass)
     mark = produce(mark, 2 * pieces, 3 * pieces)
     mark = produce(mark, 3 * pieces, 4 * pieces)
-    pl.semaphore_wait(free_sem.at[0], 1)
+    pl.semaphore_wait(free_sem.at[1], 1)
     for item in in_weight_loads():
         item.wait()
 
@@ -980,10 +838,7 @@
         full_ref[...] = scale * (grad - unit * mean)
         out_acc[rows, own] += full_ref[:, own]
         token_store(index).start()
-
-        @pl.when(index + 2 < steps)
-        def _():
-            token_load(index + 2).start()
+        next_tokens(index)
 
     mark = paced(mark, STEPS[5], fourth_pass)
     small_send[0] = jnp.zeros_like(small_ref)
@@ -1018,6 +873,12 @@
     for bit in range(plan.bits):
         small(bit).wait_send()
 
+    cot_swap().wait_send()
+
+    @pl.when(seq < last)
+    def _():
+        edge_copy().wait_send()
+
     @pl.when(seq > 0)
     def _():
         halo().wait_send()
@@ -1032,6 +893,7 @@
 def main(plan, smalls, operands, hidden):
     total_rows, width = operands[0].shape
     half = width // 2
+    assert half == 2 * UNIT
     step = min(256, total_rows)
     steps = total_rows // step
     tall = max(total_rows, width)
@@ -1039,7 +901,7 @@
     shape = jax.ShapeDtypeStruct
     dma = pltpu.SemaphoreType.DMA
     vmem = pltpu.VMEM
-    assert total_rows >= width
+    assert total_rows >= width and steps <= 4
     return pl.pallas_call(
         functools.partial(main_kernel, plan),
         name="main",
@@ -1048,10 +910,17 @@
             shape((units, plan.rows, UNIT), F32),
             shape((total_rows, half), BF16),
             shape((total_rows, half), F32),
+            shape((total_rows, width), F32),
+            shape((total_rows, half), F32),
+            shape((total_rows, half), F32),
+            shape((total_rows, half), F32),
+            shape((total_rows, half), BF16),
         ),
-        in_specs=[whole()] * 4 + [anywhere()] * 15,
-        out_specs=[whole()] + [anywhere()] * 3,
+        in_specs=[whole()] * 3 + [anywhere()] * 7,
+        out_specs=[whole()] + [anywhere()] * 8,
         scratch_shapes=[
+            vmem((16, width), BF16),
+            vmem((8, half), F32),
             vmem((units, plan.rows, UNIT), F32),
             vmem((total_rows, width), BF16),
             vmem((total_rows, width), BF16),
@@ -1075,8 +944,8 @@
             vmem((plan.bits, 8, half), F32),
             vmem((plan.bits, 8, half), F32),
             dma((3, 2)),
-            dma((5, steps)),
-            dma((7,)),
+            dma((8, steps)),
+            dma((3,)),
             dma((2,)),
             dma((2,)),
             dma((2,)),
@@ -1091,8 +960,14 @@
             dma((1,)),
             dma((plan.bits,)),
             dma((plan.bits,)),
-            pltpu.SemaphoreType.REGULAR((1,)),
+            pltpu.SemaphoreType.REGULAR((2,)),
             dma((units,)),
+            dma((7,)),
+            dma((2,)),
+            dma((1,)),
+            dma((1,)),
+            dma((steps,)),
+            dma((steps,)),
         ]
         + plan.scratch(units),
         compiler_params=pltpu.CompilerParams(
@@ -1218,38 +1093,21 @@
     plan = Halving(seq_size, shards, chunk_rows)
     gains = (norm1_gain.reshape(1, width), norm2_gain.reshape(1, width))
     tokens = tokens.reshape(total_rows, width)
-    normed_two, cotangent, left, resid, b_signal, c_signal, x_signal, mixed_in, first, prior = front(
-        plan,
-        gains,
-        conv_weight,
-        tokens,
-        out_cotangent.reshape(total_rows, half),
-        in_weight,
-        out_weight,
-    )
     hidden = gate_weight.shape[1]
     small, grads, block_out, tokens_grad = main(
         plan,
-        (*gains, conv_weight, prior),
+        (*gains, conv_weight),
         (
-            normed_two,
-            cotangent,
-            left,
+            tokens,
+            out_cotangent.reshape(total_rows, half),
             gate_weight,
             up_weight,
             down_weight,
             out_weight,
             in_weight,
-            first,
-            mixed_in,
-            resid,
-            tokens,
-            b_signal,
-            c_signal,
-            x_signal,
         ),
         hidden,
-    )
+    )[:4]
     (
         gate_grad,
         up_grad,

time: 191 us -> 181 us (0.948)
  Pallas kernels: 190 us -> 180 us
    pallas_call x1 -> x0, Pallas kernels: 20.5 us -> none  [front(): pl.pallas_call(functools.partial(front_kernel, plan), name='front', out_s...]
    pallas_call x1, Pallas kernels: 163 us -> 174 us  [main(): pl.pallas_call(functools.partial(main_kernel, plan), name='main', out_sha...]
where the time goes in v6:
time: 181 us
  Pallas kernels  180 us (99%)
    pallas_call x1, Pallas kernels, main(): pl.pallas_call(functools.partial(main_kernel, plan), name='main', out_sha...  174 us
    pallas_call x1, Pallas kernels, finish(): pl.pallas_call(finish_kernel, name='finish', out_shape=(shape((rows, hidd...  6.59 us

profile of v6, /device:TPU:0, one launch (start us, length us, event | category | flops | bytes accessed | tf_op | source)
XLA Modules:
  0.0 181.0 jit_solution(6850104417699621734)
XLA Ops:
  0.6 173.6 %main.1 = (f32[8,512]{1,0:T(8,128)}, f32[35,64,256]{2,1,0:T(8,128)}, bf16[1024,512]{1,0:T(8,128)(2,1)}, f32[1024,512]{1,0:T(8,128)}, f32[1024,1024]{1,0:T(8,128)...) custom-call(f32[1,1024]{1,0:T(1,128)} %bitcast.12, ...), custom_call_target="tpu_custom_call" | custom-call | tf_op jit(solution)/shard_map/main/pallas_call | solution.py:905
  174.2 6.6 %finish.1 = (f32[64,2304]{1,0:T(8,128)}, f32[64,2304]{1,0:T(8,128)}, f32[64,2304]{1,0:T(8,128)}, f32[3,64,512]{2,1,0:T(8,128)}, f32[64,512]{1,0:T(8,128)}, /*ind...) custom-call(f32[35,64,256]{2,1,0:T(8,128)} %get-tuple-element.24.grad, ...), custom_call_target="tpu_custom_call" | custom-call | tf_op jit(solution)/shard_map/finish/pallas_call | solution.py:1046

commit v7 on v6

--- a/solution.py
+++ b/solution.py
@@ -11,10 +11,10 @@
 MESH = pl.DeviceIdType.MESH
 UNIT = 256
 RING = 8
-PACE = (5, 25)
+PACE = (5, 24)
 LATE_FIRST = 1
-LAGS = (-10, 9, 29, 47, 126)
-STEPS = (7, 7, 2, 1, 4, 4, 5)
+LAGS = (-6, 6, 26, 45, 155)
+STEPS = (7, 6, 2, 1, 1, 4, 7)
 VMEM_BYTES = 67043328
 F32 = jnp.float32
 BF16 = jnp.bfloat16
@@ -106,8 +106,8 @@
             [pltpu.VMEM((ring, half, UNIT), BF16), pltpu.VMEM((units, half, UNIT), BF16)]
             + [pltpu.VMEM((units, self.stage_rows(s), UNIT), BF16) for s in range(self.bits)]
             + [
-                pltpu.SemaphoreType.DMA((self.bits, units)),
-                pltpu.SemaphoreType.DMA((self.bits, units)),
+                pltpu.SemaphoreType.DMA((2, self.bits, units)),
+                pltpu.SemaphoreType.DMA((2, self.bits, units)),
             ]
         )
 
@@ -116,21 +116,40 @@
         self.recv = refs[2 : 2 + self.bits]
         self.send_sem, self.recv_sem = refs[2 + self.bits :]
 
-    def copy(self, order, unit, stage):
+    def copies(self, order, unit, stage):
         weight, bit = order[stage]
-        if stage == 0:
-            source = self.first.at[unit % RING]
-        else:
-            start = pl.multiple_of(self.offset(order, 0, stage), self.rows)
-            source = self.keep.at[unit, pl.ds(start, self.stage_rows(stage))]
-        return pltpu.make_async_remote_copy(
-            src_ref=source,
-            dst_ref=self.recv[stage].at[unit],
-            send_sem=self.send_sem.at[stage, unit],
-            recv_sem=self.recv_sem.at[stage, unit],
-            device_id=self.place(self.me + (1 - 2 * bit) * weight),
-            device_id_type=MESH,
-        )
+        rows = self.stage_rows(stage)
+        starts = [0]
+        if stage + 1 < self.bits:
+            rows = rows // 2
+            following = order[stage + 1][1]
+            starts = [(1 - following) * rows, following * rows]
+        base = 0 if stage == 0 else self.offset(order, 0, stage)
+        found = []
+        for part, start in enumerate(starts):
+            source = pl.ds(pl.multiple_of(base + start, self.rows), rows)
+            target = pl.ds(pl.multiple_of(start, self.rows), rows)
+            buffer = self.keep.at[unit] if stage else self.first.at[unit % RING]
+            found.append(
+                pltpu.make_async_remote_copy(
+                    src_ref=buffer.at[source],
+                    dst_ref=self.recv[stage].at[unit, target],
+                    send_sem=self.send_sem.at[part, stage, unit],
+                    recv_sem=self.recv_sem.at[part, stage, unit],
+                    device_id=self.place(self.me + (1 - 2 * bit) * weight),
+                    device_id_type=MESH,
+                )
+            )
+        return found
+
+    def arrived(self, order, unit, stage):
+        self.copies(order, unit, stage - 1)[0].wait_recv()
+        if stage >= 2:
+            self.copies(order, unit, stage - 2)[1].wait_recv()
+
+    def sent(self, order, unit, stage):
+        for item in self.copies(order, unit, stage):
+            item.wait_send()
 
     def gather(self, left, order, keep):
         return jnp.concatenate([left[chunk] for chunk in self.chunks(order, keep)], axis=0)
@@ -140,13 +159,14 @@
 
         @pl.when(unit >= RING)
         def _():
-            self.copy(order, unit - RING, 0).wait_send()
+            self.sent(order, unit - RING, 0)
 
         value = product(self.gather(left, order, False), right[...]).astype(BF16)
         self.first[unit % RING] = value
 
     def launch(self, unit, parity):
-        self.copy(self.order(parity), unit, 0).start()
+        for item in self.copies(self.order(parity), unit, 0):
+            item.start()
 
     def hold(self, unit, parity, left, right):
         order = self.order(parity)
@@ -162,19 +182,20 @@
 
     def advance(self, unit, parity, stage):
         order = self.order(parity)
-        self.copy(order, unit, stage - 1).wait_recv()
+        self.arrived(order, unit, stage)
         rows = self.stage_rows(stage)
         total = self.collect(order, unit, stage, rows)
         start = pl.multiple_of(self.offset(order, 0, stage), self.rows)
         self.keep[unit, pl.ds(start, rows)] = total.astype(BF16)
-        self.copy(order, unit, stage).start()
+        for item in self.copies(order, unit, stage):
+            item.start()
 
     def finish(self, unit, parity):
         order = self.order(parity)
-        self.copy(order, unit, self.bits - 1).wait_recv()
+        self.arrived(order, unit, self.bits)
         total = self.collect(order, unit, self.bits, self.rows)
         for stage in range(1, self.bits):
-            self.copy(order, unit, stage).wait_send()
+            self.sent(order, unit, stage)
         return total
 
 
@@ -302,16 +323,21 @@
             local_copy(down_hbm.at[columns], down_buf.at[slot], weight_sem.at[2, slot]),
         ]
 
-    def front_loads():
+    def front_loads(late):
         tall = pl.ds(0, width)
-        pairs = [(in_weight_hbm.at[2], x_weight_ref), (out_weight_hbm, out_weight_ref)]
+        if late:
+            pairs = [(out_weight_hbm, out_weight_ref), (cot_hbm, cot_ref.at[:, own])]
+            return [
+                local_copy(source, target, front_sem.at[place])
+                for place, (source, target) in enumerate(pairs)
+            ]
+        pairs = [(in_weight_hbm.at[2], x_weight_ref)]
         for piece in range(pieces):
             columns = pl.ds(piece * UNIT, UNIT)
             pairs.append((in_weight_hbm.at[0, :, columns], gate_buf.at[piece, tall]))
             pairs.append((in_weight_hbm.at[1, :, columns], up_buf.at[piece, tall]))
-        pairs.append((cot_hbm, cot_ref.at[:, own]))
         return [
-            local_copy(source, target, front_sem.at[place])
+            local_copy(source, target, front_sem.at[2 + place])
             for place, (source, target) in enumerate(pairs)
         ]
 
@@ -488,7 +514,7 @@
             token_load(index + 2).start()
 
     start_tokens()
-    for item in front_loads():
+    for item in front_loads(False) + front_loads(True):
         item.start()
     sums_ref[...] = jnp.zeros_like(sums_ref)
     plan.greet((-1, 1))
@@ -498,7 +524,7 @@
         edge_copy().start()
 
     cot_swap().start()
-    for item in front_loads():
+    for item in front_loads(False):
         item.wait()
 
     def project(index, carry):
@@ -558,10 +584,13 @@
         first_swap(index).start()
         out_acc[rows] += part
         mixed_store(index).start()
+        left_ref[1, :, :, rows] = chunked(cot_ref[rows])
         return carry
 
+    for item in front_loads(True):
+        item.wait()
+    cot_swap().wait_recv()
     lax.fori_loop(0, steps, convolve, 0)
-    cot_swap().wait_recv()
 
     def settle(index, carry):
         rows = span(index)
@@ -573,7 +602,6 @@
         normed_ref[rows] = normed
         resid_store(index).start()
         left_ref[0, :, :, rows] = chunked(normed)
-        left_ref[1, :, :, rows] = chunked(cot_ref[rows])
         return carry
 
     lax.fori_loop(0, steps, settle, 0)
@@ -867,7 +895,7 @@
 
     lax.fori_loop(0, rest, drain, 0)
     for unit in range(units - RING, units):
-        plan.copy(plan.order(unit % 2), unit, 0).wait_send()
+        plan.sent(plan.order(unit % 2), unit, 0)
     for unit in range(units):
         grads_store(unit).wait()
     for bit in range(plan.bits):

time: 181 us -> 179 us (0.989)
  Pallas kernels: 180 us -> 178 us
    pallas_call x1, Pallas kernels: 174 us -> 171 us  [main(): pl.pallas_call(functools.partial(main_kernel, plan), name='main', out_sha...]
where the time goes in v7:
time: 179 us
  Pallas kernels  178 us (99%)
    pallas_call x1, Pallas kernels, main(): pl.pallas_call(functools.partial(main_kernel, plan), name='main', out_sha...  171 us
    pallas_call x1, Pallas kernels, finish(): pl.pallas_call(finish_kernel, name='finish', out_shape=(shape((rows, hidd...  6.59 us

profile of v7, /device:TPU:0, one launch (start us, length us, event | category | flops | bytes accessed | tf_op | source)
XLA Modules:
  0.0 178.7 jit_solution(12498746552029365049)
XLA Ops:
  0.6 171.3 %main.1 = (f32[8,512]{1,0:T(8,128)}, f32[35,64,256]{2,1,0:T(8,128)}, bf16[1024,512]{1,0:T(8,128)(2,1)}, f32[1024,512]{1,0:T(8,128)}, f32[1024,1024]{1,0:T(8,128)...) custom-call(f32[1,1024]{1,0:T(1,128)} %bitcast.12, ...), custom_call_target="tpu_custom_call" | custom-call | tf_op jit(solution)/shard_map/main/pallas_call | solution.py:933
  172.0 6.6 %finish.1 = (f32[64,2304]{1,0:T(8,128)}, f32[64,2304]{1,0:T(8,128)}, f32[64,2304]{1,0:T(8,128)}, f32[3,64,512]{2,1,0:T(8,128)}, f32[64,512]{1,0:T(8,128)}, /*ind...) custom-call(f32[35,64,256]{2,1,0:T(8,128)} %get-tuple-element.24.grad, ...), custom_call_target="tpu_custom_call" | custom-call | tf_op jit(solution)/shard_map/finish/pallas_call | solution.py:1074

commit v8 on v7

--- a/solution.py
+++ b/solution.py
@@ -13,8 +13,8 @@
 RING = 8
 PACE = (5, 24)
 LATE_FIRST = 1
-LAGS = (-6, 6, 26, 45, 155)
-STEPS = (7, 6, 2, 1, 1, 4, 7)
+LAGS = (-7, 5, 25, 46, 140)
+STEPS = (6, 5, 2, 1, 5, 6, 10)
 VMEM_BYTES = 67043328
 F32 = jnp.float32
 BF16 = jnp.bfloat16

time: 179 us -> 179 us (level)
  no operation moved by 1% of the time
where the time goes in v8:
time: 179 us
  Pallas kernels  178 us (99%)
    pallas_call x1, Pallas kernels, main(): pl.pallas_call(functools.partial(main_kernel, plan), name='main', out_sha...  171 us
    pallas_call x1, Pallas kernels, finish(): pl.pallas_call(finish_kernel, name='finish', out_shape=(shape((rows, hidd...  6.59 us

profile of v8, /device:TPU:0, one launch (start us, length us, event | category | flops | bytes accessed | tf_op | source)
XLA Modules:
  0.0 178.6 jit_solution(6830344474119735301)
XLA Ops:
  0.6 171.2 %main.1 = (f32[8,512]{1,0:T(8,128)}, f32[35,64,256]{2,1,0:T(8,128)}, bf16[1024,512]{1,0:T(8,128)(2,1)}, f32[1024,512]{1,0:T(8,128)}, f32[1024,1024]{1,0:T(8,128)...) custom-call(f32[1,1024]{1,0:T(1,128)} %bitcast.12, ...), custom_call_target="tpu_custom_call" | custom-call | tf_op jit(solution)/shard_map/main/pallas_call | solution.py:933
  171.8 6.6 %finish.1 = (f32[64,2304]{1,0:T(8,128)}, f32[64,2304]{1,0:T(8,128)}, f32[64,2304]{1,0:T(8,128)}, f32[3,64,512]{2,1,0:T(8,128)}, f32[64,512]{1,0:T(8,128)}, /*ind...) custom-call(f32[35,64,256]{2,1,0:T(8,128)} %get-tuple-element.24.grad, ...), custom_call_target="tpu_custom_call" | custom-call | tf_op jit(solution)/shard_map/finish/pallas_call | solution.py:1074
